TPU v7x, 128 devices: a whole 4x4x4 slice. The times are simulated.
128 devices in a mesh: grp: 8 (over x, z_lo), mem: 16 (over z_hi, y, core).
Axes of the slice: x: 4, y: 4, z: 4 (z_hi: 2, z_lo: 2; z = z_hi * 2 + z_lo), core: 2. Of those that a mesh axis runs over, the one named last changes fastest.
Arguments:
- weight: bfloat16 [4, 8192, 16384], P(None, None, ('grp', 'mem')), may hold values from -0.046875 to 0.046875
- activation: bfloat16 [2, 16384, 512], P(None, ('grp', 'mem')), may hold values from -6 to 6
- points: int32 [8], replicated, may hold values from 0 to 7, each once
Outputs:
- share: float32 [8, 8192, 512], P('grp', 'mem')
Inputs may be any that keep to these rules, and one draw needn't show every extreme that they name: A permutation of 0 to 7; group g evaluates at points[g] + 1.
All inputs are finite; a program needn't handle non-finite values.
Results may differ from a plain program's by a relative error of at most 0.0042.
Values may be sent and summed in bfloat16 or wider, within the bound.
No kernel may reach another device: no remote copies, remote signals or barrier semaphores. Data moves between devices by JAX's collectives and lax.ppermute only.
A program may use at most 320 MiB of HBM per device.

v0:
```python
import functools

import jax
import jax.numpy as jnp
import numpy as np
from jax import lax
from jax.experimental import pallas as pl
from jax.experimental.pallas import tpu as pltpu
from jax.sharding import Mesh
from jax.sharding import PartitionSpec as P


AXES = ("x", "zl", "zh", "y", "c")
SIZES = {"x": 4, "zl": 2, "zh": 2, "y": 4, "c": 2}
TOKENS = 512
FAMILIES = "yzx"
ROWS_X, ROWS_Y, ROWS_Z = 128, 192, 192
AT_Y, AT_Z = ROWS_X, ROWS_X + ROWS_Y
VMEM = pl.BlockSpec(memory_space=pltpu.VMEM)
SMEM = pl.BlockSpec(memory_space=pltpu.SMEM)
ANY = pl.BlockSpec(memory_space=pl.ANY)
HBM = pl.BlockSpec(memory_space=pltpu.HBM)
F32, BF16 = jnp.float32, jnp.bfloat16


def flip(value, axis, d, dc=0):
    over = [n for n in AXES if (n == "c" and dc) or (d and (n == axis or (axis == "z" and n in ("zl", "zh"))))]
    sizes = [SIZES[n] for n in over]
    pairs = []
    for i in range(int(np.prod(sizes))):
        at = dict(zip(over, (int(k) for k in np.unravel_index(i, sizes))))
        to = dict(at)
        if d and axis == "z":
            to["zl"] ^= d & 1
            to["zh"] ^= d >> 1
        elif d:
            to[axis] ^= d
        if dc:
            to["c"] ^= 1
        pairs.append((i, int(np.ravel_multi_index([to[n] for n in over], sizes))))
    return lax.ppermute(value, tuple(over), pairs)


def source_slices(family, w, where, d, dc):
    x, y, zl, zh, c = (where[i] for i in range(5))
    c = c ^ dc
    if family == "x":
        return w.at[:, :, :, c, pl.ds(pl.multiple_of((x ^ d) * (ROWS_X // 4), 16), ROWS_X // 4), :]
    if family == "y":
        return w.at[:, :, y ^ d, c, pl.ds(AT_Y, ROWS_Y), :]
    start = pl.multiple_of(AT_Z + (zl ^ (d & 1)) * (ROWS_Z // 2), 16)
    return w.at[:, zh ^ (d >> 1), :, c, pl.ds(start, ROWS_Z // 2), :]


PIECE = {
    "x": (4, 2, 4, ROWS_X // 4, 128),
    "y": (4, 2, ROWS_Y, 128),
    "z": (4, 4, ROWS_Z // 2, 128),
}
SOURCES = tuple((d, dc) for dc in (0, 1) for d in range(4))
CHUNK = 32
FEATURES = 2 * 4 * 128


def rows_of(family):
    return int(np.prod(PIECE[family][1:-1]))


def planes_of(family):
    return 4 + -(-FEATURES // rows_of(family))


def plane_at(shape, row):
    index, at = [], row
    for n in shape[::-1]:
        index.append(at % n)
        at //= n
    return (4 + at, *index[:0:-1], pl.ds(index[0], CHUNK))


def pack_kernel(family, where, w, act, *refs):
    outs, token, xstage, xin, sem, x_sem = refs[:8], refs[8], *refs[9:]
    read = pltpu.make_async_copy(act, xin, x_sem.at[0])
    read.start()
    copies = [
        pltpu.make_async_copy(
            source_slices(family, w, where, d, dc), out if dc else out.at[pl.ds(0, 4)], sem.at[i]
        )
        for i, ((d, dc), out) in enumerate(zip(SOURCES, outs))
    ]
    for copy in copies:
        copy.start()
    for i in range(5):
        token[i] = where[i]
    read.wait()
    for k in range(2):
        for ct in range(4):
            for r in range(0, 128, CHUNK):
                at = plane_at(PIECE[family][1:-1], (k * 4 + ct) * 128 + r)
                xstage[(at[0] - 4, *at[1:])] = xin[k, r : r + CHUNK, ct * 128 : (ct + 1) * 128]
    writes = [
        pltpu.make_async_copy(xstage, out.at[pl.ds(4, xstage.shape[0])], x_sem.at[i]) for i, out in enumerate(outs[:4])
    ]
    for write in writes:
        write.start()
    for copy in copies + writes:
        copy.wait()


def pack(family, weight, act, where):
    shape = PIECE[family]
    wide = (planes_of(family), *shape[1:])
    size = int(np.prod(shape)) * 2
    shapes = [jax.ShapeDtypeStruct(wide, BF16)] * 4 + [jax.ShapeDtypeStruct(shape, BF16)] * 4
    out = pl.pallas_call(
        functools.partial(pack_kernel, family),
        out_shape=shapes + [jax.ShapeDtypeStruct((5,), jnp.int32)],
        in_specs=[SMEM, HBM, HBM],
        out_specs=[ANY] * 8 + [SMEM],
        scratch_shapes=[
            pltpu.VMEM((wide[0] - 4, *shape[1:]), BF16),
            pltpu.VMEM(act.shape, BF16),
            pltpu.SemaphoreType.DMA((8,)),
            pltpu.SemaphoreType.DMA((4,)),
        ],
        cost_estimate=pl.CostEstimate(flops=0, bytes_accessed=16 * size, transcendentals=0),
        compiler_params=pltpu.CompilerParams(vmem_limit_bytes=4 << 20),
    )(where, weight, act)
    return out[:8], out[8]


def relay_kernel(order, *refs):
    pieces, out, token, sem = refs[:4], refs[4], refs[5], refs[6]
    copies = [pltpu.make_async_copy(p.at[pl.ds(4, out.shape[1])], out.at[i], sem.at[i]) for i, p in enumerate(pieces)]
    for copy in copies:
        copy.start()
    token[0] = order[0]
    for copy in copies:
        copy.wait()


def relay(family, pieces, order):
    shape = (4, planes_of(family) - 4, *PIECE[family][1:])
    return pl.pallas_call(
        relay_kernel,
        out_shape=[jax.ShapeDtypeStruct(shape, BF16), jax.ShapeDtypeStruct((1,), jnp.int32)],
        in_specs=[SMEM] + [ANY] * 4,
        out_specs=[VMEM, SMEM],
        scratch_shapes=[pltpu.SemaphoreType.DMA((4,))],
        cost_estimate=pl.CostEstimate(flops=0, bytes_accessed=4 << 20, transcendentals=0),
        compiler_params=pltpu.CompilerParams(vmem_limit_bytes=4 << 20),
    )(order, *pieces)


def plan_of(family, where):
    x, y, zl, zh = (where[i] for i in range(4))
    if family == "y":
        sends = [(d, gz, ((x ^ d) * 2 + gz)) for d in range(4) for gz in range(2)]
        return [(t * 96, 96, t * 96, sends) for t in range(4)]
    if family == "z":
        return [((y ^ d) * 96, 96, 0, [(d, g, g) for g in range(8)]) for d in range(4)]
    return [
        ((zh ^ e) * ROWS_X + t * 64, 64, t * 64,
         [(2 * e + f, gx, gx * 2 + (zl ^ f)) for f in range(2) for gx in range(4)])
        for e in range(2) for t in range(2)
    ]


OUT = {"x": (4, ROWS_X, TOKENS), "y": (2, 2 * ROWS_Y, TOKENS), "z": (8, ROWS_Z // 2, TOKENS)}
TILE = {"x": 64, "y": 96, "z": 96}


def product_kernel(family, where, factors, order, *refs):
    w, xd = refs[:8], refs[8]
    outs, token, xcat, prods = refs[9:13], refs[13], refs[14], refs[15:17]
    token[0] = order[0]
    rows, tile = rows_of(family), TILE[family]
    for s in range(8):
        for k in range(2):
            for ct in range(4):
                for r in range(0, 128, CHUNK):
                    at = plane_at((rows,), (k * 4 + ct) * 128 + r)
                    piece = w[s][at] if s < 4 else xd[(s - 4, at[0] - 4, *at[1:])]
                    xcat[s * 128 + r : s * 128 + r + CHUNK, k * TOKENS + ct * 128 : k * TOKENS + (ct + 1) * 128] = piece
    plan = plan_of(family, where)

    def multiply(start, prod):
        here = pl.ds(start if isinstance(start, int) else pl.multiple_of(start, 16), tile)
        left = [jnp.concatenate([w[s][j, here, :] for s in range(8)], axis=1) for j in range(4)]
        prod[...] = jnp.dot(jnp.concatenate(left, axis=0), xcat[...], preferred_element_type=F32)

    anchors = [factors[g] for g in range(8)] if family == "z" else None

    def combine(first, sends, prod):
        at = anchors or [factors[group] for _, _, group in sends]
        for r in range(0, tile, 8):
            for col in range(0, TOKENS, 256):
                terms = [
                    prod[(p % 4) * tile + r : (p % 4) * tile + r + 8, (p // 4) * TOKENS + col : (p // 4) * TOKENS + col + 256]
                    for p in range(8)
                ]
                for (d, slot, _), anchor in zip(sends, at):
                    total = terms[7]
                    for p in range(6, -1, -1):
                        total = total * anchor + terms[p]
                    outs[d][slot, first + r : first + r + 8, col : col + 256] = total.astype(BF16)

    multiply(plan[0][0], prods[0])
    for t in range(4):
        if t < 3:
            multiply(plan[t + 1][0], prods[(t + 1) % 2])
        combine(plan[t][2], plan[t][3], prods[t % 2])


def product(family, pieces, xd, where, factors, order):
    rows = rows_of(family)
    planes = planes_of(family)
    pieces = [p.reshape(-1, rows, 128) for p in pieces]
    xd = xd.reshape(4, planes - 4, rows, 128)
    flops = 2 * 4 * rows * 1024 * 1024
    out = pl.pallas_call(
        functools.partial(product_kernel, family),
        out_shape=[jax.ShapeDtypeStruct(OUT[family], BF16)] * 4 + [jax.ShapeDtypeStruct((1,), jnp.int32)],
        in_specs=[SMEM, SMEM, SMEM] + [VMEM] * 9,
        out_specs=[VMEM] * 4 + [SMEM],
        scratch_shapes=[pltpu.VMEM((1024, 1024), BF16)] + [pltpu.VMEM((4 * TILE[family], 1024), F32)] * 2,
        cost_estimate=pl.CostEstimate(flops=2 * flops, bytes_accessed=8 << 20, transcendentals=0),
        compiler_params=pltpu.CompilerParams(vmem_limit_bytes=22 << 20),
    )(where, factors, order, *pieces, xd)
    return out[:4], out[4]


def cut_kernel(index, where, *refs):
    parts, outs = refs[:4], refs[4:]
    pos = tuple(where[i] for i in range(4))
    for d, out in enumerate(outs):
        at = index(pos, d)
        total = parts[0][at].astype(F32)
        for part in parts[1:]:
            total = total + part[at].astype(F32)
        out[...] = total.astype(out.dtype)


def sum_and_cut(parts, where, index, shape, sends):
    size = int(np.prod(parts[0].shape))
    return pl.pallas_call(
        functools.partial(cut_kernel, index),
        out_shape=[jax.ShapeDtypeStruct(shape, F32)] + [jax.ShapeDtypeStruct(shape, BF16)] * sends,
        in_specs=[SMEM] + [VMEM] * 4,
        out_specs=[VMEM] * (sends + 1),
        cost_estimate=pl.CostEstimate(flops=size * 4, bytes_accessed=size * 12, transcendentals=0),
        compiler_params=pltpu.CompilerParams(vmem_limit_bytes=8 << 20),
    )(where, *parts)


def exchange(parts, axis):
    return [parts[0]] + [flip(parts[d], axis, d) for d in range(1, len(parts))]


def final_kernel(where, *refs):
    fx, fy, fz, out = refs[:4], refs[4:8], refs[8:10], refs[10]
    x, zl = where[0], where[2]
    quarter, half = ROWS_X // 4, ROWS_Z // 2
    for d in range(4):
        out[0, pl.ds(pl.multiple_of((x ^ d) * quarter, 16), quarter), :] = fx[d][...].astype(F32)
    total = fy[0][...]
    for part in fy[1:]:
        total = total + part[...].astype(F32)
    out[0, AT_Y : AT_Y + ROWS_Y, :] = total
    for d in range(2):
        out[0, pl.ds(pl.multiple_of(AT_Z + (zl ^ d) * half, 16), half), :] = fz[d][...].astype(F32)


def per_device(weight, activation, points):
    x, y, c = lax.axis_index("x"), lax.axis_index("y"), lax.axis_index("c")
    zl, zh = lax.axis_index("zl"), lax.axis_index("zh")
    where = jnp.stack([x, y, zl, zh, c]).astype(jnp.int32)
    factors = (points + 1).astype(F32) / 8
    view = weight.reshape(4, 2, 4, 2, 512, 128)

    pieces, parts, order = {}, {}, where
    for family in FAMILIES:
        sent, order = pack(family, view, activation, order)
        same = exchange(sent[:4], family)
        pieces[family] = same + [flip(sent[4 + d], family, d, 1) for d in range(4)]
    order, shared = order[:1], {}

    def share(family, order):
        xd, order = relay(family, pieces[family][:4], order)
        shared[family] = flip(xd, "c", 0, 1)
        return order

    for family in FAMILIES:
        order = share(family, order)
    for family in FAMILIES:
        parts[family], order = product(family, pieces[family], shared[family], where, factors, order)

    px = exchange(parts["x"], "z")
    py = exchange(parts["y"], "x")
    pz = exchange(parts["z"], "y")
    px = [p.reshape(4, 4, ROWS_X // 4, TOKENS) for p in px]
    py = [p.reshape(2, 2, ROWS_Y, TOKENS) for p in py]
    pz = [p.reshape(4, 2, ROWS_Z // 2, TOKENS) for p in pz]
    px = sum_and_cut(
        px, where, lambda pos, d: (slice(None), pos[1] ^ d), (4, ROWS_X // 4, TOKENS), 3)
    py = sum_and_cut(
        py, where, lambda pos, d: (pos[2] ^ (d & 1), pos[3] ^ (d >> 1)), (ROWS_Y, TOKENS), 3)
    pz = sum_and_cut(pz, where, lambda pos, d: (pos[0] ^ d,), (2, ROWS_Z // 2, TOKENS), 3)
    px = exchange(px, "y")
    py = exchange(py, "z")
    pz = exchange(pz, "x")
    px = sum_and_cut(px, where, lambda pos, d: (pos[0] ^ d,), (ROWS_X // 4, TOKENS), 3)
    pz = sum_and_cut(pz, where, lambda pos, d: (pos[2] ^ d,), (ROWS_Z // 2, TOKENS), 1)
    px = exchange(px, "x")
    pz = exchange(pz, "z")
    return pl.pallas_call(
        final_kernel,
        out_shape=jax.ShapeDtypeStruct((1, 512, TOKENS), F32),
        in_specs=[SMEM] + [VMEM] * 10,
        out_specs=VMEM,
        cost_estimate=pl.CostEstimate(flops=1 << 20, bytes_accessed=3 << 20, transcendentals=0),
        compiler_params=pltpu.CompilerParams(vmem_limit_bytes=8 << 20),
        name="final",
    )(where, *px, *py, *pz)


def solution(mesh):
    split = Mesh(mesh.devices.reshape(4, 2, 2, 4, 2), AXES)
    grp, mem = ("x", "zl"), ("zh", "y", "c")
    placed = (P(None, None, grp + mem), P(None, grp + mem, None), P())
    return jax.shard_map(per_device, mesh=split, in_specs=placed, out_specs=P(grp, mem, None), check_vma=False)
```

profile of v0, /device:TPU:8, one launch (start us, length us, event | category | flops | bytes accessed | tf_op | source)
XLA Modules:
  0.0 221.5 jit_solution(183711004757264818)
XLA Ops:
  0.1 3.4 %copy-done = bf16[4,8192,128]{2,1,0:T(8,128)(2,1)S(1)} copy-done((bf16[4,8192,128]{2,1,0:T(8,128)(2,1)S(1)}, bf16[4,8192,128]{2,1,0:T(8,128)(2,1)}, u32[]{:S(2)}) %copy-start) | copy-done | bytes 8388632
  4.4 1.9 shard_map.37
  6.8 2.7 %collective-permute-start.1 = (bf16[7,2,192,128]{3,2,1,0:T(8,128)(2,1)S(1)}, bf16[7,2,192,128]{3,2,1,0:T(8,128)(2,1)S(1)}, u32[]{:S(2)}, u32[]{:S(2)}) collective-permute-start(bf16[7,2,192,128]{3,2,1,0:T(8,128)(2,1)S(1)} %get-tuple-element.75), channel_id=1, source_target_pairs={{0,4},{2,6},{4,0},{6,2},{1,5},{3,7},{5,1},{7,3},{8,12},{10,14},{12... | collective-permute-start | bytes 2064392 | tf_op jit(solution)/shard_map/ppermute | solution.py:41
  9.9 1.9 shard_map.38
  11.8 2.0 collective-permute-start.3
  13.8 3.6 %collective-permute-start.4 = (bf16[7,4,96,128]{3,2,1,0:T(8,128)(2,1)S(1)}, bf16[7,4,96,128]{3,2,1,0:T(8,128)(2,1)S(1)}, u32[]{:S(2)}, u32[]{:S(2)}) collective-permute-start(bf16[7,4,96,128]{3,2,1,0:T(8,128)(2,1)S(1)} %get-tuple-element.80), channel_id=1, source_target_pairs={{0,8},{8,0},{16,24},{24,16},{1,9},{9,1},{17,25},{25,17},{2,10},{10... | collective-permute-start | bytes 2064392 | tf_op jit(solution)/shard_map/ppermute | solution.py:41
  17.4 7.3 %collective-permute-done.refs_1_ = bf16[7,2,192,128]{3,2,1,0:T(8,128)(2,1)S(1)} collective-permute-done((bf16[7,2,192,128]{3,2,1,0:T(8,128)(2,1)S(1)}, bf16[7,2,192,128]{3,2,1,0:T(8,128)(2,1)S(1)}, u32[]{:S(2)}, u32[]{:S(2)}) %collective-permute-start) | collective-permute-done | bytes 688160 | tf_op jit(solution)/shard_map/ppermute | solution.py:41
  24.7 4.0 %collective-permute-start.5 = (bf16[7,4,96,128]{3,2,1,0:T(8,128)(2,1)S(1)}, bf16[7,4,96,128]{3,2,1,0:T(8,128)(2,1)S(1)}, u32[]{:S(2)}, u32[]{:S(2)}) collective-permute-start(bf16[7,4,96,128]{3,2,1,0:T(8,128)(2,1)S(1)} %get-tuple-element.81), channel_id=1, source_target_pairs={{0,24},{8,16},{16,8},{24,0},{1,25},{9,17},{17,9},{25,1},{2,26},{10... | collective-permute-start | bytes 2064392 | tf_op jit(solution)/shard_map/ppermute | solution.py:41
  28.8 10.7 %collective-permute-done.1.refs_2_ = bf16[7,2,192,128]{3,2,1,0:T(8,128)(2,1)S(1)} collective-permute-done((bf16[7,2,192,128]{3,2,1,0:T(8,128)(2,1)S(1)}, bf16[7,2,192,128]{3,2,1,0:T(8,128)(2,1)S(1)}, u32[]{:S(2)}, u32[]{:S(2)}) %collective-permute-start.1) | collective-permute-done | bytes 688160 | tf_op jit(solution)/shard_map/ppermute | solution.py:41
  39.5 1.6 shard_map.39
  42.5 2.5 %collective-permute-start.10 = (bf16[4,2,192,128]{3,2,1,0:T(8,128)(2,1)S(1)}, bf16[4,2,192,128]{3,2,1,0:T(8,128)(2,1)S(1)}, u32[]{:S(2)}, u32[]{:S(2)}) collective-permute-start(bf16[4,2,192,128]{3,2,1,0:T(8,128)(2,1)S(1)} %get-tuple-element.89), channel_id=1, source_target_pairs={{0,3},{1,2},{2,1},{3,0},{4,7},{5,6},{6,5},{7,4},{8,11},{9,10},{10,... | collective-permute-start | bytes 1179656 | tf_op jit(solution)/shard_map/ppermute | solution.py:41
  45.0 1.5 collective-permute-start.6
  46.5 3.0 %collective-permute-start.7 = (bf16[8,2,4,32,128]{4,3,2,1,0:T(8,128)(2,1)S(1)}, bf16[8,2,4,32,128]{4,3,2,1,0:T(8,128)(2,1)S(1)}, u32[]{:S(2)}, u32[]{:S(2)}) collective-permute-start(bf16[8,2,4,32,128]{4,3,2,1,0:T(8,128)(2,1)S(1)} %get-tuple-element.85), channel_id=1, source_target_pairs={{0,64},{32,96},{64,0},{96,32},{1,65},{33,97},{65,1},{97,33},{2,66}... | collective-permute-start | bytes 1572872 | tf_op jit(solution)/shard_map/ppermute | solution.py:41
  49.6 7.4 %collective-permute-done.5.refs_3_ = bf16[7,4,96,128]{3,2,1,0:T(8,128)(2,1)S(1)} collective-permute-done((bf16[7,4,96,128]{3,2,1,0:T(8,128)(2,1)S(1)}, bf16[7,4,96,128]{3,2,1,0:T(8,128)(2,1)S(1)}, u32[]{:S(2)}, u32[]{:S(2)}) %collective-permute-start.5) | collective-permute-done | bytes 688160 | tf_op jit(solution)/shard_map/ppermute | solution.py:41
  57.0 2.8 %collective-permute-start.8 = (bf16[8,2,4,32,128]{4,3,2,1,0:T(8,128)(2,1)S(1)}, bf16[8,2,4,32,128]{4,3,2,1,0:T(8,128)(2,1)S(1)}, u32[]{:S(2)}, u32[]{:S(2)}) collective-permute-start(bf16[8,2,4,32,128]{4,3,2,1,0:T(8,128)(2,1)S(1)} %get-tuple-element.86), channel_id=1, source_target_pairs={{0,96},{32,64},{64,32},{96,0},{1,97},{33,65},{65,33},{97,1},{2,98}... | collective-permute-start | bytes 1572872 | tf_op jit(solution)/shard_map/ppermute | solution.py:41
  59.7 1.5 shard_map.41
  61.3 2.4 %collective-permute-start.11 = (bf16[4,2,192,128]{3,2,1,0:T(8,128)(2,1)S(1)}, bf16[4,2,192,128]{3,2,1,0:T(8,128)(2,1)S(1)}, u32[]{:S(2)}, u32[]{:S(2)}) collective-permute-start(bf16[4,2,192,128]{3,2,1,0:T(8,128)(2,1)S(1)} %get-tuple-element.90), channel_id=1, source_target_pairs={{0,5},{1,4},{2,7},{3,6},{4,1},{5,0},{6,3},{7,2},{8,13},{9,12},{10,... | collective-permute-start | bytes 1179656 | tf_op jit(solution)/shard_map/ppermute | solution.py:41
  63.7 8.7 %collective-permute-done.7.refs_2_ = bf16[8,2,4,32,128]{4,3,2,1,0:T(8,128)(2,1)S(1)} collective-permute-done((bf16[8,2,4,32,128]{4,3,2,1,0:T(8,128)(2,1)S(1)}, bf16[8,2,4,32,128]{4,3,2,1,0:T(8,128)(2,1)S(1)}, u32[]{:S(2)}, u32[]{:S(2)}) %collective-permute-start.7) | collective-permute-done | bytes 524320 | tf_op jit(solution)/shard_map/ppermute | solution.py:41
  72.4 8.4 %collective-permute-done.8.refs_3_ = bf16[8,2,4,32,128]{4,3,2,1,0:T(8,128)(2,1)S(1)} collective-permute-done((bf16[8,2,4,32,128]{4,3,2,1,0:T(8,128)(2,1)S(1)}, bf16[8,2,4,32,128]{4,3,2,1,0:T(8,128)(2,1)S(1)}, u32[]{:S(2)}, u32[]{:S(2)}) %collective-permute-start.8) | collective-permute-done | bytes 524320 | tf_op jit(solution)/shard_map/ppermute | solution.py:41
  80.8 1.2 shard_map.42
  83.2 3.7 %collective-permute-start.16 = (bf16[4,4,96,128]{3,2,1,0:T(8,128)(2,1)S(1)}, bf16[4,4,96,128]{3,2,1,0:T(8,128)(2,1)S(1)}, u32[]{:S(2)}, u32[]{:S(2)}) collective-permute-start(bf16[4,4,96,128]{3,2,1,0:T(8,128)(2,1)S(1)} %get-tuple-element.96), channel_id=1, source_target_pairs={{0,9},{1,8},{8,1},{9,0},{16,25},{17,24},{24,17},{25,16},{2,11},{3,... | collective-permute-start | bytes 1179656 | tf_op jit(solution)/shard_map/ppermute | solution.py:41
  87.7 7.5 %shard_map.43 = (bf16[2,384,512]{2,1,0:T(8,128)(2,1)S(1)}, bf16[2,384,512]{2,1,0:T(8,128)(2,1)S(1)}, bf16[2,384,512]{2,1,0:T(8,128)(2,1)S(1)}, bf16[2,384,512]{2,1,0:T(8,128)(2,1)S(1)}, s32[1]{0:T(128)}) custom-call(s32[5]{0:T(128)S(1)} %stack.23.where, f32[8]{0:T(128)S(1)} %convert_multiply_fusion.factors, s32[1]{0:T(128)} %get-tuple-element.87.order, ...), custom_call_target="tpu_custom_call" | custom-call | flops 6442450944 | bytes 8388608 | tf_op jit(solution)/shard_map/pallas_call | solution.py:221
  95.7 8.7 %collective-permute-done.16 = bf16[4,4,96,128]{3,2,1,0:T(8,128)(2,1)S(1)} collective-permute-done((bf16[4,4,96,128]{3,2,1,0:T(8,128)(2,1)S(1)}, bf16[4,4,96,128]{3,2,1,0:T(8,128)(2,1)S(1)}, u32[]{:S(2)}, u32[]{:S(2)}) %collective-permute-start.16) | collective-permute-done | bytes 393248 | tf_op jit(solution)/shard_map/ppermute | solution.py:41
  104.8 2.5 %collective-permute-done.17 = bf16[4,4,96,128]{3,2,1,0:T(8,128)(2,1)S(1)} collective-permute-done((bf16[4,4,96,128]{3,2,1,0:T(8,128)(2,1)S(1)}, bf16[4,4,96,128]{3,2,1,0:T(8,128)(2,1)S(1)}, u32[]{:S(2)}, u32[]{:S(2)}) %collective-permute-start.17) | collective-permute-done | bytes 393248 | tf_op jit(solution)/shard_map/ppermute | solution.py:41
  107.3 1.9 collective-permute-start.21
  110.1 7.5 %shard_map.44 = (bf16[8,96,512]{2,1,0:T(8,128)(2,1)S(1)}, bf16[8,96,512]{2,1,0:T(8,128)(2,1)S(1)}, bf16[8,96,512]{2,1,0:T(8,128)(2,1)S(1)}, bf16[8,96,512]{2,1,0:T(8,128)(2,1)S(1)}, s32[1]{0:T(128)}) custom-call(s32[5]{0:T(128)S(1)} %stack.23.where, f32[8]{0:T(128)S(1)} %convert_multiply_fusion.factors, s32[1]{0:T(128)} %get-tuple-element.93.order, ...), custom_call_target="tpu_custom_call" | custom-call | flops 6442450944 | bytes 8388608 | tf_op jit(solution)/shard_map/pallas_call | solution.py:221
  118.7 1.5 collective-permute-done.21
  120.2 4.2 %collective-permute-done.22 = bf16[4,2,4,32,128]{4,3,2,1,0:T(8,128)(2,1)S(1)} collective-permute-done((bf16[4,2,4,32,128]{4,3,2,1,0:T(8,128)(2,1)S(1)}, bf16[4,2,4,32,128]{4,3,2,1,0:T(8,128)(2,1)S(1)}, u32[]{:S(2)}, u32[]{:S(2)}) %collective-permute-start.22) | collective-permute-done | bytes 262176 | tf_op jit(solution)/shard_map/ppermute | solution.py:41
  124.4 5.7 %shard_map.45 = (bf16[4,128,512]{2,1,0:T(8,128)(2,1)S(1)}, bf16[4,128,512]{2,1,0:T(8,128)(2,1)S(1)}, bf16[4,128,512]{2,1,0:T(8,128)(2,1)S(1)}, bf16[4,128,512]{2,1,0:T(8,128)(2,1)S(1)}, s32[1]{0:T(128)}) custom-call(s32[5]{0:T(128)S(1)} %stack.23.where, f32[8]{0:T(128)S(1)} %convert_multiply_fusion.factors, s32[1]{0:T(128)} %get-tuple-element.99.order, ...), custom_call_target="tpu_custom_call" | custom-call | flops 4294967296 | bytes 8388608 | tf_op jit(solution)/shard_map/pallas_call | solution.py:221
  130.2 1.8 collective-permute-start.25
  132.0 2.9 %collective-permute-start.26 = (bf16[4,128,512]{2,1,0:T(8,128)(2,1)S(1)}, bf16[4,128,512]{2,1,0:T(8,128)(2,1)S(1)}, u32[]{:S(2)}, u32[]{:S(2)}) collective-permute-start(bf16[4,128,512]{2,1,0:T(8,128)(2,1)S(1)} %get-tuple-element.108), channel_id=1, source_target_pairs={{0,24},{8,16},{16,8},{24,0},{1,25},{9,17},{17,9},{25,1},{2,26},{10... | collective-permute-start | bytes 1572872 | tf_op jit(solution)/shard_map/ppermute | solution.py:41
  134.9 1.7 collective-permute-start.40
  136.6 8.4 %collective-permute-done.24 = bf16[4,128,512]{2,1,0:T(8,128)(2,1)S(1)} collective-permute-done((bf16[4,128,512]{2,1,0:T(8,128)(2,1)S(1)}, bf16[4,128,512]{2,1,0:T(8,128)(2,1)S(1)}, u32[]{:S(2)}, u32[]{:S(2)}) %collective-permute-start.24) | collective-permute-done | bytes 524320 | tf_op jit(solution)/shard_map/ppermute | solution.py:41
  145.0 1.3 collective-permute-start.41
  146.3 9.0 %collective-permute-done.25 = bf16[4,128,512]{2,1,0:T(8,128)(2,1)S(1)} collective-permute-done((bf16[4,128,512]{2,1,0:T(8,128)(2,1)S(1)}, bf16[4,128,512]{2,1,0:T(8,128)(2,1)S(1)}, u32[]{:S(2)}, u32[]{:S(2)}) %collective-permute-start.25) | collective-permute-done | bytes 524320 | tf_op jit(solution)/shard_map/ppermute | solution.py:41
  156.1 1.8 collective-permute-done.26
  158.8 2.5 %collective-permute-start.35 = (bf16[2,384,512]{2,1,0:T(8,128)(2,1)S(1)}, bf16[2,384,512]{2,1,0:T(8,128)(2,1)S(1)}, u32[]{:S(2)}, u32[]{:S(2)}) collective-permute-start(bf16[2,384,512]{2,1,0:T(8,128)(2,1)S(1)} %get-tuple-element.120), channel_id=1, source_target_pairs={{0,96},{32,64},{64,32},{96,0},{1,97},{33,65},{65,33},{97,1},{2,98}... | collective-permute-start | bytes 2359304 | tf_op jit(solution)/shard_map/ppermute | solution.py:41
  162.9 9.3 %collective-permute-done.41 = bf16[8,96,512]{2,1,0:T(8,128)(2,1)S(1)} collective-permute-done((bf16[8,96,512]{2,1,0:T(8,128)(2,1)S(1)}, bf16[8,96,512]{2,1,0:T(8,128)(2,1)S(1)}, u32[]{:S(2)}, u32[]{:S(2)}) %collective-permute-start.41) | collective-permute-done | bytes 786464 | tf_op jit(solution)/shard_map/ppermute | solution.py:41
  173.8 1.9 collective-permute-start.28
  175.7 1.5 collective-permute-start.29
  177.2 16.1 %collective-permute-done.34 = bf16[2,384,512]{2,1,0:T(8,128)(2,1)S(1)} collective-permute-done((bf16[2,384,512]{2,1,0:T(8,128)(2,1)S(1)}, bf16[2,384,512]{2,1,0:T(8,128)(2,1)S(1)}, u32[]{:S(2)}, u32[]{:S(2)}) %collective-permute-start.34) | collective-permute-done | bytes 786464 | tf_op jit(solution)/shard_map/ppermute | solution.py:41
  193.3 1.6 collective-permute-start.43
  195.6 3.4 %collective-permute-start.44 = (bf16[2,96,512]{2,1,0:T(8,128)(2,1)S(1)}, bf16[2,96,512]{2,1,0:T(8,128)(2,1)S(1)}, u32[]{:S(2)}, u32[]{:S(2)}) collective-permute-start(bf16[2,96,512]{2,1,0:T(8,128)(2,1)S(1)} %get-tuple-element.132), channel_id=1, source_target_pairs={{0,96},{32,64},{64,32},{96,0},{1,97},{33,65},{65,33},{97,1},{2,98}... | collective-permute-start | bytes 589832 | tf_op jit(solution)/shard_map/ppermute | solution.py:41
  200.0 4.4 %collective-permute-start.37 = (bf16[192,512]{1,0:T(8,128)(2,1)S(1)}, bf16[192,512]{1,0:T(8,128)(2,1)S(1)}, u32[]{:S(2)}, u32[]{:S(2)}) collective-permute-start(bf16[192,512]{1,0:T(8,128)(2,1)S(1)} %get-tuple-element.123), channel_id=1, source_target_pairs={{0,8},{8,0},{16,24},{24,16},{1,9},{9,1},{17,25},{25,17},{2,10},{10... | collective-permute-start | bytes 589832 | tf_op jit(solution)/shard_map/ppermute | solution.py:41
  206.1 3.2 %collective-permute-done.30.refs_1_ = bf16[32,512]{1,0:T(8,128)(2,1)S(1)} collective-permute-done((bf16[32,512]{1,0:T(8,128)(2,1)S(1)}, bf16[32,512]{1,0:T(8,128)(2,1)S(1)}, u32[]{:S(2)}, u32[]{:S(2)}) %collective-permute-start.30) | collective-permute-done | bytes 32800 | tf_op jit(solution)/shard_map/ppermute | solution.py:41
  209.3 5.4 %collective-permute-done.31.refs_2_ = bf16[32,512]{1,0:T(8,128)(2,1)S(1)} collective-permute-done((bf16[32,512]{1,0:T(8,128)(2,1)S(1)}, bf16[32,512]{1,0:T(8,128)(2,1)S(1)}, u32[]{:S(2)}, u32[]{:S(2)}) %collective-permute-start.31) | collective-permute-done | bytes 32800 | tf_op jit(solution)/shard_map/ppermute | solution.py:41
  214.8 5.1 %collective-permute-done.32.refs_3_ = bf16[32,512]{1,0:T(8,128)(2,1)S(1)} collective-permute-done((bf16[32,512]{1,0:T(8,128)(2,1)S(1)}, bf16[32,512]{1,0:T(8,128)(2,1)S(1)}, u32[]{:S(2)}, u32[]{:S(2)}) %collective-permute-start.32) | collective-permute-done | bytes 32800 | tf_op jit(solution)/shard_map/ppermute | solution.py:41
  219.9 1.6 final.1
  (71 shorter events, 16.7 us)
Async XLA Ops:
  4.4 5.5 %copy-start.3 = (bf16[2,128,512]{2,1,0:T(8,128)(2,1)S(1)}, bf16[2,128,512]{2,1,0:T(8,128)(2,1)}, u32[]{:S(2)}) copy-start(bf16[2,128,512]{2,1,0:T(8,128)(2,1)} %act.5) | copy-start | bytes 786436
  6.3 18.4 %collective-permute-start = (bf16[7,2,192,128]{3,2,1,0:T(8,128)(2,1)S(1)}, bf16[7,2,192,128]{3,2,1,0:T(8,128)(2,1)S(1)}, u32[]{:S(2)}, u32[]{:S(2)}) collective-permute-start(bf16[7,2,192,128]{3,2,1,0:T(8,128)(2,1)S(1)} %get-tuple-element.74), channel_id=1, source_target_pairs={{0,2},{2,0},{4,6},{6,4},{1,3},{3,1},{5,7},{7,5},{8,10},{10,8},{12,... | collective-permute-start | bytes 2064392 | tf_op jit(solution)/shard_map/ppermute | solution.py:41
  6.8 32.7 %collective-permute-start.1 = (bf16[7,2,192,128]{3,2,1,0:T(8,128)(2,1)S(1)}, bf16[7,2,192,128]{3,2,1,0:T(8,128)(2,1)S(1)}, u32[]{:S(2)}, u32[]{:S(2)}) collective-permute-start(bf16[7,2,192,128]{3,2,1,0:T(8,128)(2,1)S(1)} %get-tuple-element.75), channel_id=1, source_target_pairs={{0,4},{2,6},{4,0},{6,2},{1,5},{3,7},{5,1},{7,3},{8,12},{10,14},{12... | collective-permute-start | bytes 2064392 | tf_op jit(solution)/shard_map/ppermute | solution.py:41
  9.5 31.6 %collective-permute-start.2 = (bf16[7,2,192,128]{3,2,1,0:T(8,128)(2,1)S(1)}, bf16[7,2,192,128]{3,2,1,0:T(8,128)(2,1)S(1)}, u32[]{:S(2)}, u32[]{:S(2)}) collective-permute-start(bf16[7,2,192,128]{3,2,1,0:T(8,128)(2,1)S(1)} %get-tuple-element.76), channel_id=1, source_target_pairs={{0,6},{2,4},{4,2},{6,0},{1,7},{3,5},{5,3},{7,1},{8,14},{10,12},{12... | collective-permute-start | bytes 2064392 | tf_op jit(solution)/shard_map/ppermute | solution.py:41
  11.8 33.2 %collective-permute-start.3 = (bf16[7,4,96,128]{3,2,1,0:T(8,128)(2,1)S(1)}, bf16[7,4,96,128]{3,2,1,0:T(8,128)(2,1)S(1)}, u32[]{:S(2)}, u32[]{:S(2)}) collective-permute-start(bf16[7,4,96,128]{3,2,1,0:T(8,128)(2,1)S(1)} %get-tuple-element.79), channel_id=1, source_target_pairs={{0,16},{8,24},{16,0},{24,8},{1,17},{9,25},{17,1},{25,9},{2,18},{10... | collective-permute-start | bytes 2064392 | tf_op jit(solution)/shard_map/ppermute | solution.py:41
  13.8 32.7 %collective-permute-start.4 = (bf16[7,4,96,128]{3,2,1,0:T(8,128)(2,1)S(1)}, bf16[7,4,96,128]{3,2,1,0:T(8,128)(2,1)S(1)}, u32[]{:S(2)}, u32[]{:S(2)}) collective-permute-start(bf16[7,4,96,128]{3,2,1,0:T(8,128)(2,1)S(1)} %get-tuple-element.80), channel_id=1, source_target_pairs={{0,8},{8,0},{16,24},{24,16},{1,9},{9,1},{17,25},{25,17},{2,10},{10... | collective-permute-start | bytes 2064392 | tf_op jit(solution)/shard_map/ppermute | solution.py:41
  24.7 32.2 %collective-permute-start.5 = (bf16[7,4,96,128]{3,2,1,0:T(8,128)(2,1)S(1)}, bf16[7,4,96,128]{3,2,1,0:T(8,128)(2,1)S(1)}, u32[]{:S(2)}, u32[]{:S(2)}) collective-permute-start(bf16[7,4,96,128]{3,2,1,0:T(8,128)(2,1)S(1)} %get-tuple-element.81), channel_id=1, source_target_pairs={{0,24},{8,16},{16,8},{24,0},{1,25},{9,17},{17,9},{25,1},{2,26},{10... | collective-permute-start | bytes 2064392 | tf_op jit(solution)/shard_map/ppermute | solution.py:41
  39.5 3.0 %collective-permute-start.9 = (bf16[4,2,192,128]{3,2,1,0:T(8,128)(2,1)S(1)}, bf16[4,2,192,128]{3,2,1,0:T(8,128)(2,1)S(1)}, u32[]{:S(2)}, u32[]{:S(2)}) collective-permute-start(bf16[4,2,192,128]{3,2,1,0:T(8,128)(2,1)S(1)} %get-tuple-element.88), channel_id=1, source_target_pairs={{0,1},{1,0},{2,3},{3,2},{4,5},{5,4},{6,7},{7,6},{8,9},{9,8},{10,11... | collective-permute-start | bytes 1179656 | tf_op jit(solution)/shard_map/ppermute | solution.py:41
  41.9 45.6 %collective-permute-start.13 = (bf16[4,3,2,192,128]{4,3,2,1,0:T(8,128)(2,1)S(1)}, bf16[4,3,2,192,128]{4,3,2,1,0:T(8,128)(2,1)S(1)}, u32[]{:S(2)}, u32[]{:S(2)}) collective-permute-start(bf16[4,3,2,192,128]{4,3,2,1,0:T(8,128)(2,1)S(1)} %get-tuple-element.92), channel_id=1, source_target_pairs={{0,1},{1,0},{2,3},{3,2},{4,5},{5,4},{6,7},{7,6},{8,9},{9,8},{10,11... | collective-permute-start | bytes 3538952 | tf_op jit(solution)/shard_map/ppermute | solution.py:41
  42.5 18.7 %collective-permute-start.10 = (bf16[4,2,192,128]{3,2,1,0:T(8,128)(2,1)S(1)}, bf16[4,2,192,128]{3,2,1,0:T(8,128)(2,1)S(1)}, u32[]{:S(2)}, u32[]{:S(2)}) collective-permute-start(bf16[4,2,192,128]{3,2,1,0:T(8,128)(2,1)S(1)} %get-tuple-element.89), channel_id=1, source_target_pairs={{0,3},{1,2},{2,1},{3,0},{4,7},{5,6},{6,5},{7,4},{8,11},{9,10},{10,... | collective-permute-start | bytes 1179656 | tf_op jit(solution)/shard_map/ppermute | solution.py:41
  45.0 16.3 %collective-permute-start.6 = (bf16[8,2,4,32,128]{4,3,2,1,0:T(8,128)(2,1)S(1)}, bf16[8,2,4,32,128]{4,3,2,1,0:T(8,128)(2,1)S(1)}, u32[]{:S(2)}, u32[]{:S(2)}) collective-permute-start(bf16[8,2,4,32,128]{4,3,2,1,0:T(8,128)(2,1)S(1)} %get-tuple-element.84), channel_id=1, source_target_pairs={{0,32},{32,0},{64,96},{96,64},{1,33},{33,1},{65,97},{97,65},{2,34}... | collective-permute-start | bytes 1572872 | tf_op jit(solution)/shard_map/ppermute | solution.py:41
  46.5 25.9 %collective-permute-start.7 = (bf16[8,2,4,32,128]{4,3,2,1,0:T(8,128)(2,1)S(1)}, bf16[8,2,4,32,128]{4,3,2,1,0:T(8,128)(2,1)S(1)}, u32[]{:S(2)}, u32[]{:S(2)}) collective-permute-start(bf16[8,2,4,32,128]{4,3,2,1,0:T(8,128)(2,1)S(1)} %get-tuple-element.85), channel_id=1, source_target_pairs={{0,64},{32,96},{64,0},{96,32},{1,65},{33,97},{65,1},{97,33},{2,66}... | collective-permute-start | bytes 1572872 | tf_op jit(solution)/shard_map/ppermute | solution.py:41
  57.0 23.8 %collective-permute-start.8 = (bf16[8,2,4,32,128]{4,3,2,1,0:T(8,128)(2,1)S(1)}, bf16[8,2,4,32,128]{4,3,2,1,0:T(8,128)(2,1)S(1)}, u32[]{:S(2)}, u32[]{:S(2)}) collective-permute-start(bf16[8,2,4,32,128]{4,3,2,1,0:T(8,128)(2,1)S(1)} %get-tuple-element.86), channel_id=1, source_target_pairs={{0,96},{32,64},{64,32},{96,0},{1,97},{33,65},{65,33},{97,1},{2,98}... | collective-permute-start | bytes 1572872 | tf_op jit(solution)/shard_map/ppermute | solution.py:41
  59.7 21.1 %copy-start.4 = (s32[8]{0:T(128)S(1)}, s32[8]{0:T(128)}, u32[]{:S(2)}) copy-start(s32[8]{0:T(128)} %param.5) | copy-start | bytes 100
  61.2 48.0 %collective-permute-start.18 = (bf16[4,3,4,96,128]{4,3,2,1,0:T(8,128)(2,1)S(1)}, bf16[4,3,4,96,128]{4,3,2,1,0:T(8,128)(2,1)S(1)}, u32[]{:S(2)}, u32[]{:S(2)}) collective-permute-start(bf16[4,3,4,96,128]{4,3,2,1,0:T(8,128)(2,1)S(1)} %get-tuple-element.98), channel_id=1, source_target_pairs={{0,1},{1,0},{2,3},{3,2},{4,5},{5,4},{6,7},{7,6},{8,9},{9,8},{10,11... | collective-permute-start | bytes 3538952 | tf_op jit(solution)/shard_map/ppermute | solution.py:41
  61.3 20.7 %collective-permute-start.11 = (bf16[4,2,192,128]{3,2,1,0:T(8,128)(2,1)S(1)}, bf16[4,2,192,128]{3,2,1,0:T(8,128)(2,1)S(1)}, u32[]{:S(2)}, u32[]{:S(2)}) collective-permute-start(bf16[4,2,192,128]{3,2,1,0:T(8,128)(2,1)S(1)} %get-tuple-element.90), channel_id=1, source_target_pairs={{0,5},{1,4},{2,7},{3,6},{4,1},{5,0},{6,3},{7,2},{8,13},{9,12},{10,... | collective-permute-start | bytes 1179656 | tf_op jit(solution)/shard_map/ppermute | solution.py:41
  72.4 10.8 %collective-permute-start.12 = (bf16[4,2,192,128]{3,2,1,0:T(8,128)(2,1)S(1)}, bf16[4,2,192,128]{3,2,1,0:T(8,128)(2,1)S(1)}, u32[]{:S(2)}, u32[]{:S(2)}) collective-permute-start(bf16[4,2,192,128]{3,2,1,0:T(8,128)(2,1)S(1)} %get-tuple-element.91), channel_id=1, source_target_pairs={{0,7},{1,6},{2,5},{3,4},{4,3},{5,2},{6,1},{7,0},{8,15},{9,14},{10,... | collective-permute-start | bytes 1179656 | tf_op jit(solution)/shard_map/ppermute | solution.py:41
  80.8 6.1 %collective-permute-start.14 = (bf16[4,4,96,128]{3,2,1,0:T(8,128)(2,1)S(1)}, bf16[4,4,96,128]{3,2,1,0:T(8,128)(2,1)S(1)}, u32[]{:S(2)}, u32[]{:S(2)}) collective-permute-start(bf16[4,4,96,128]{3,2,1,0:T(8,128)(2,1)S(1)} %get-tuple-element.94), channel_id=1, source_target_pairs={{0,1},{1,0},{2,3},{3,2},{4,5},{5,4},{6,7},{7,6},{8,9},{9,8},{10,11... | collective-permute-start | bytes 1179656 | tf_op jit(solution)/shard_map/ppermute | solution.py:41
  82.0 13.2 %collective-permute-start.15 = (bf16[4,4,96,128]{3,2,1,0:T(8,128)(2,1)S(1)}, bf16[4,4,96,128]{3,2,1,0:T(8,128)(2,1)S(1)}, u32[]{:S(2)}, u32[]{:S(2)}) collective-permute-start(bf16[4,4,96,128]{3,2,1,0:T(8,128)(2,1)S(1)} %get-tuple-element.95), channel_id=1, source_target_pairs={{0,17},{1,16},{8,25},{9,24},{16,1},{17,0},{24,9},{25,8},{2,19},{3,... | collective-permute-start | bytes 1179656 | tf_op jit(solution)/shard_map/ppermute | solution.py:41
  83.2 21.2 %collective-permute-start.16 = (bf16[4,4,96,128]{3,2,1,0:T(8,128)(2,1)S(1)}, bf16[4,4,96,128]{3,2,1,0:T(8,128)(2,1)S(1)}, u32[]{:S(2)}, u32[]{:S(2)}) collective-permute-start(bf16[4,4,96,128]{3,2,1,0:T(8,128)(2,1)S(1)} %get-tuple-element.96), channel_id=1, source_target_pairs={{0,9},{1,8},{8,1},{9,0},{16,25},{17,24},{24,17},{25,16},{2,11},{3,... | collective-permute-start | bytes 1179656 | tf_op jit(solution)/shard_map/ppermute | solution.py:41
  86.9 20.4 %collective-permute-start.17 = (bf16[4,4,96,128]{3,2,1,0:T(8,128)(2,1)S(1)}, bf16[4,4,96,128]{3,2,1,0:T(8,128)(2,1)S(1)}, u32[]{:S(2)}, u32[]{:S(2)}) collective-permute-start(bf16[4,4,96,128]{3,2,1,0:T(8,128)(2,1)S(1)} %get-tuple-element.97), channel_id=1, source_target_pairs={{0,25},{1,24},{8,17},{9,16},{16,9},{17,8},{24,1},{25,0},{2,27},{3,... | collective-permute-start | bytes 1179656 | tf_op jit(solution)/shard_map/ppermute | solution.py:41
  87.5 36.9 %collective-permute-start.23 = (bf16[4,4,2,4,32,128]{5,4,3,2,1,0:T(8,128)(2,1)S(1)}, bf16[4,4,2,4,32,128]{5,4,3,2,1,0:T(8,128)(2,1)S(1)}, u32[]{:S(2)}, u32[]{:S(2)}) collective-permute-start(bf16[4,4,2,4,32,128]{5,4,3,2,1,0:T(8,128)(2,1)S(1)} %get-tuple-element.104), channel_id=1, source_target_pairs={{0,1},{1,0},{2,3},{3,2},{4,5},{5,4},{6,7},{7,6},{8,9},{9,8},{10,11... | collective-permute-start | bytes 3145736 | tf_op jit(solution)/shard_map/ppermute | solution.py:41
  95.2 22.4 %collective-permute-start.19 = (bf16[4,2,4,32,128]{4,3,2,1,0:T(8,128)(2,1)S(1)}, bf16[4,2,4,32,128]{4,3,2,1,0:T(8,128)(2,1)S(1)}, u32[]{:S(2)}, u32[]{:S(2)}) collective-permute-start(bf16[4,2,4,32,128]{4,3,2,1,0:T(8,128)(2,1)S(1)} %get-tuple-element.100), channel_id=1, source_target_pairs={{0,1},{1,0},{2,3},{3,2},{4,5},{5,4},{6,7},{7,6},{8,9},{9,8},{10,11... | collective-permute-start | bytes 786440 | tf_op jit(solution)/shard_map/ppermute | solution.py:41
  104.4 14.3 %collective-permute-start.20 = (bf16[4,2,4,32,128]{4,3,2,1,0:T(8,128)(2,1)S(1)}, bf16[4,2,4,32,128]{4,3,2,1,0:T(8,128)(2,1)S(1)}, u32[]{:S(2)}, u32[]{:S(2)}) collective-permute-start(bf16[4,2,4,32,128]{4,3,2,1,0:T(8,128)(2,1)S(1)} %get-tuple-element.101), channel_id=1, source_target_pairs={{0,33},{1,32},{32,1},{33,0},{64,97},{65,96},{96,65},{97,64},{2,35}... | collective-permute-start | bytes 786440 | tf_op jit(solution)/shard_map/ppermute | solution.py:41
  107.3 13.0 %collective-permute-start.21 = (bf16[4,2,4,32,128]{4,3,2,1,0:T(8,128)(2,1)S(1)}, bf16[4,2,4,32,128]{4,3,2,1,0:T(8,128)(2,1)S(1)}, u32[]{:S(2)}, u32[]{:S(2)}) collective-permute-start(bf16[4,2,4,32,128]{4,3,2,1,0:T(8,128)(2,1)S(1)} %get-tuple-element.102), channel_id=1, source_target_pairs={{0,65},{1,64},{32,97},{33,96},{64,1},{65,0},{96,33},{97,32},{2,67}... | collective-permute-start | bytes 786440 | tf_op jit(solution)/shard_map/ppermute | solution.py:41
  109.2 15.2 %collective-permute-start.22 = (bf16[4,2,4,32,128]{4,3,2,1,0:T(8,128)(2,1)S(1)}, bf16[4,2,4,32,128]{4,3,2,1,0:T(8,128)(2,1)S(1)}, u32[]{:S(2)}, u32[]{:S(2)}) collective-permute-start(bf16[4,2,4,32,128]{4,3,2,1,0:T(8,128)(2,1)S(1)} %get-tuple-element.103), channel_id=1, source_target_pairs={{0,97},{1,96},{32,65},{33,64},{64,33},{65,32},{96,1},{97,0},{2,99}... | collective-permute-start | bytes 786440 | tf_op jit(solution)/shard_map/ppermute | solution.py:41
  117.7 41.2 %collective-permute-start.39 = (bf16[8,96,512]{2,1,0:T(8,128)(2,1)S(1)}, bf16[8,96,512]{2,1,0:T(8,128)(2,1)S(1)}, u32[]{:S(2)}, u32[]{:S(2)}) collective-permute-start(bf16[8,96,512]{2,1,0:T(8,128)(2,1)S(1)} %get-tuple-element.126), channel_id=1, source_target_pairs={{0,2},{2,0},{4,6},{6,4},{1,3},{3,1},{5,7},{7,5},{8,10},{10,8},{12,... | collective-permute-start | bytes 2359304 | tf_op jit(solution)/shard_map/ppermute | solution.py:41
  130.1 14.9 %collective-permute-start.24 = (bf16[4,128,512]{2,1,0:T(8,128)(2,1)S(1)}, bf16[4,128,512]{2,1,0:T(8,128)(2,1)S(1)}, u32[]{:S(2)}, u32[]{:S(2)}) collective-permute-start(bf16[4,128,512]{2,1,0:T(8,128)(2,1)S(1)} %get-tuple-element.106), channel_id=1, source_target_pairs={{0,16},{8,24},{16,0},{24,8},{1,17},{9,25},{17,1},{25,9},{2,18},{10... | collective-permute-start | bytes 1572872 | tf_op jit(solution)/shard_map/ppermute | solution.py:41
  130.2 25.1 %collective-permute-start.25 = (bf16[4,128,512]{2,1,0:T(8,128)(2,1)S(1)}, bf16[4,128,512]{2,1,0:T(8,128)(2,1)S(1)}, u32[]{:S(2)}, u32[]{:S(2)}) collective-permute-start(bf16[4,128,512]{2,1,0:T(8,128)(2,1)S(1)} %get-tuple-element.107), channel_id=1, source_target_pairs={{0,8},{8,0},{16,24},{24,16},{1,9},{9,1},{17,25},{25,17},{2,10},{10... | collective-permute-start | bytes 1572872 | tf_op jit(solution)/shard_map/ppermute | solution.py:41
  132.0 25.9 %collective-permute-start.26 = (bf16[4,128,512]{2,1,0:T(8,128)(2,1)S(1)}, bf16[4,128,512]{2,1,0:T(8,128)(2,1)S(1)}, u32[]{:S(2)}, u32[]{:S(2)}) collective-permute-start(bf16[4,128,512]{2,1,0:T(8,128)(2,1)S(1)} %get-tuple-element.108), channel_id=1, source_target_pairs={{0,24},{8,16},{16,8},{24,0},{1,25},{9,17},{17,9},{25,1},{2,26},{10... | collective-permute-start | bytes 1572872 | tf_op jit(solution)/shard_map/ppermute | solution.py:41
  134.9 27.2 %collective-permute-start.40 = (bf16[8,96,512]{2,1,0:T(8,128)(2,1)S(1)}, bf16[8,96,512]{2,1,0:T(8,128)(2,1)S(1)}, u32[]{:S(2)}, u32[]{:S(2)}) collective-permute-start(bf16[8,96,512]{2,1,0:T(8,128)(2,1)S(1)} %get-tuple-element.127), channel_id=1, source_target_pairs={{0,4},{2,6},{4,0},{6,2},{1,5},{3,7},{5,1},{7,3},{8,12},{10,14},{12... | collective-permute-start | bytes 2359304 | tf_op jit(solution)/shard_map/ppermute | solution.py:41
  145.0 27.2 %collective-permute-start.41 = (bf16[8,96,512]{2,1,0:T(8,128)(2,1)S(1)}, bf16[8,96,512]{2,1,0:T(8,128)(2,1)S(1)}, u32[]{:S(2)}, u32[]{:S(2)}) collective-permute-start(bf16[8,96,512]{2,1,0:T(8,128)(2,1)S(1)} %get-tuple-element.128), channel_id=1, source_target_pairs={{0,6},{2,4},{4,2},{6,0},{1,7},{3,5},{5,3},{7,1},{8,14},{10,12},{12... | collective-permute-start | bytes 2359304 | tf_op jit(solution)/shard_map/ppermute | solution.py:41
  155.3 20.4 %collective-permute-start.33 = (bf16[2,384,512]{2,1,0:T(8,128)(2,1)S(1)}, bf16[2,384,512]{2,1,0:T(8,128)(2,1)S(1)}, u32[]{:S(2)}, u32[]{:S(2)}) collective-permute-start(bf16[2,384,512]{2,1,0:T(8,128)(2,1)S(1)} %get-tuple-element.118), channel_id=1, source_target_pairs={{0,32},{32,0},{64,96},{96,64},{1,33},{33,1},{65,97},{97,65},{2,34}... | collective-permute-start | bytes 2359304 | tf_op jit(solution)/shard_map/ppermute | solution.py:41
  157.9 35.4 %collective-permute-start.34 = (bf16[2,384,512]{2,1,0:T(8,128)(2,1)S(1)}, bf16[2,384,512]{2,1,0:T(8,128)(2,1)S(1)}, u32[]{:S(2)}, u32[]{:S(2)}) collective-permute-start(bf16[2,384,512]{2,1,0:T(8,128)(2,1)S(1)} %get-tuple-element.119), channel_id=1, source_target_pairs={{0,64},{32,96},{64,0},{96,32},{1,65},{33,97},{65,1},{97,33},{2,66}... | collective-permute-start | bytes 2359304 | tf_op jit(solution)/shard_map/ppermute | solution.py:41
  158.8 36.7 %collective-permute-start.35 = (bf16[2,384,512]{2,1,0:T(8,128)(2,1)S(1)}, bf16[2,384,512]{2,1,0:T(8,128)(2,1)S(1)}, u32[]{:S(2)}, u32[]{:S(2)}) collective-permute-start(bf16[2,384,512]{2,1,0:T(8,128)(2,1)S(1)} %get-tuple-element.120), channel_id=1, source_target_pairs={{0,96},{32,64},{64,32},{96,0},{1,97},{33,65},{65,33},{97,1},{2,98}... | collective-permute-start | bytes 2359304 | tf_op jit(solution)/shard_map/ppermute | solution.py:41
  162.1 11.7 %collective-permute-start.27 = (bf16[4,32,512]{2,1,0:T(8,128)(2,1)S(1)}, bf16[4,32,512]{2,1,0:T(8,128)(2,1)S(1)}, u32[]{:S(2)}, u32[]{:S(2)}) collective-permute-start(bf16[4,32,512]{2,1,0:T(8,128)(2,1)S(1)} %get-tuple-element.110), channel_id=1, source_target_pairs={{0,2},{2,0},{4,6},{6,4},{1,3},{3,1},{5,7},{7,5},{8,10},{10,8},{12,... | collective-permute-start | bytes 393224 | tf_op jit(solution)/shard_map/ppermute | solution.py:41
  173.1 31.3 %collective-permute-start.42 = (bf16[2,96,512]{2,1,0:T(8,128)(2,1)S(1)}, bf16[2,96,512]{2,1,0:T(8,128)(2,1)S(1)}, u32[]{:S(2)}, u32[]{:S(2)}) collective-permute-start(bf16[2,96,512]{2,1,0:T(8,128)(2,1)S(1)} %get-tuple-element.130), channel_id=1, source_target_pairs={{0,32},{32,0},{64,96},{96,64},{1,33},{33,1},{65,97},{97,65},{2,34}... | collective-permute-start | bytes 589832 | tf_op jit(solution)/shard_map/ppermute | solution.py:41
  173.8 26.1 %collective-permute-start.28 = (bf16[4,32,512]{2,1,0:T(8,128)(2,1)S(1)}, bf16[4,32,512]{2,1,0:T(8,128)(2,1)S(1)}, u32[]{:S(2)}, u32[]{:S(2)}) collective-permute-start(bf16[4,32,512]{2,1,0:T(8,128)(2,1)S(1)} %get-tuple-element.111), channel_id=1, source_target_pairs={{0,4},{2,6},{4,0},{6,2},{1,5},{3,7},{5,1},{7,3},{8,12},{10,14},{12... | collective-permute-start | bytes 393224 | tf_op jit(solution)/shard_map/ppermute | solution.py:41
  175.7 24.3 %collective-permute-start.29 = (bf16[4,32,512]{2,1,0:T(8,128)(2,1)S(1)}, bf16[4,32,512]{2,1,0:T(8,128)(2,1)S(1)}, u32[]{:S(2)}, u32[]{:S(2)}) collective-permute-start(bf16[4,32,512]{2,1,0:T(8,128)(2,1)S(1)} %get-tuple-element.112), channel_id=1, source_target_pairs={{0,6},{2,4},{4,2},{6,0},{1,7},{3,5},{5,3},{7,1},{8,14},{10,12},{12... | collective-permute-start | bytes 393224 | tf_op jit(solution)/shard_map/ppermute | solution.py:41
  193.3 12.0 %collective-permute-start.43 = (bf16[2,96,512]{2,1,0:T(8,128)(2,1)S(1)}, bf16[2,96,512]{2,1,0:T(8,128)(2,1)S(1)}, u32[]{:S(2)}, u32[]{:S(2)}) collective-permute-start(bf16[2,96,512]{2,1,0:T(8,128)(2,1)S(1)} %get-tuple-element.131), channel_id=1, source_target_pairs={{0,64},{32,96},{64,0},{96,32},{1,65},{33,97},{65,1},{97,33},{2,66}... | collective-permute-start | bytes 589832 | tf_op jit(solution)/shard_map/ppermute | solution.py:41
  195.6 9.8 %collective-permute-start.44 = (bf16[2,96,512]{2,1,0:T(8,128)(2,1)S(1)}, bf16[2,96,512]{2,1,0:T(8,128)(2,1)S(1)}, u32[]{:S(2)}, u32[]{:S(2)}) collective-permute-start(bf16[2,96,512]{2,1,0:T(8,128)(2,1)S(1)} %get-tuple-element.132), channel_id=1, source_target_pairs={{0,96},{32,64},{64,32},{96,0},{1,97},{33,65},{65,33},{97,1},{2,98}... | collective-permute-start | bytes 589832 | tf_op jit(solution)/shard_map/ppermute | solution.py:41
  199.9 19.9 %collective-permute-start.36 = (bf16[192,512]{1,0:T(8,128)(2,1)S(1)}, bf16[192,512]{1,0:T(8,128)(2,1)S(1)}, u32[]{:S(2)}, u32[]{:S(2)}) collective-permute-start(bf16[192,512]{1,0:T(8,128)(2,1)S(1)} %get-tuple-element.122), channel_id=1, source_target_pairs={{0,16},{8,24},{16,0},{24,8},{1,17},{9,25},{17,1},{25,9},{2,18},{10... | collective-permute-start | bytes 589832 | tf_op jit(solution)/shard_map/ppermute | solution.py:41
  200.0 19.8 %collective-permute-start.37 = (bf16[192,512]{1,0:T(8,128)(2,1)S(1)}, bf16[192,512]{1,0:T(8,128)(2,1)S(1)}, u32[]{:S(2)}, u32[]{:S(2)}) collective-permute-start(bf16[192,512]{1,0:T(8,128)(2,1)S(1)} %get-tuple-element.123), channel_id=1, source_target_pairs={{0,8},{8,0},{16,24},{24,16},{1,9},{9,1},{17,25},{25,17},{2,10},{10... | collective-permute-start | bytes 589832 | tf_op jit(solution)/shard_map/ppermute | solution.py:41
  204.4 15.4 %collective-permute-start.38 = (bf16[192,512]{1,0:T(8,128)(2,1)S(1)}, bf16[192,512]{1,0:T(8,128)(2,1)S(1)}, u32[]{:S(2)}, u32[]{:S(2)}) collective-permute-start(bf16[192,512]{1,0:T(8,128)(2,1)S(1)} %get-tuple-element.124), channel_id=1, source_target_pairs={{0,24},{8,16},{16,8},{24,0},{1,25},{9,17},{17,9},{25,1},{2,26},{10... | collective-permute-start | bytes 589832 | tf_op jit(solution)/shard_map/ppermute | solution.py:41
  205.3 4.0 %collective-permute-start.30 = (bf16[32,512]{1,0:T(8,128)(2,1)S(1)}, bf16[32,512]{1,0:T(8,128)(2,1)S(1)}, u32[]{:S(2)}, u32[]{:S(2)}) collective-permute-start(bf16[32,512]{1,0:T(8,128)(2,1)S(1)} %get-tuple-element.114), channel_id=1, source_target_pairs={{0,32},{32,0},{64,96},{96,64},{1,33},{33,1},{65,97},{97,65},{2,34}... | collective-permute-start | bytes 98312 | tf_op jit(solution)/shard_map/ppermute | solution.py:41
  206.0 13.8 %collective-permute-start.45 = (bf16[96,512]{1,0:T(8,128)(2,1)S(1)}, bf16[96,512]{1,0:T(8,128)(2,1)S(1)}, u32[]{:S(2)}, u32[]{:S(2)}) collective-permute-start(bf16[96,512]{1,0:T(8,128)(2,1)S(1)} %get-tuple-element.134), channel_id=1, source_target_pairs={{0,16},{8,24},{16,0},{24,8},{1,17},{9,25},{17,1},{25,9},{2,18},{10... | collective-permute-start | bytes 294920 | tf_op jit(solution)/shard_map/ppermute | solution.py:41
  209.3 5.4 %collective-permute-start.31 = (bf16[32,512]{1,0:T(8,128)(2,1)S(1)}, bf16[32,512]{1,0:T(8,128)(2,1)S(1)}, u32[]{:S(2)}, u32[]{:S(2)}) collective-permute-start(bf16[32,512]{1,0:T(8,128)(2,1)S(1)} %get-tuple-element.115), channel_id=1, source_target_pairs={{0,64},{32,96},{64,0},{96,32},{1,65},{33,97},{65,1},{97,33},{2,66}... | collective-permute-start | bytes 98312 | tf_op jit(solution)/shard_map/ppermute | solution.py:41
  214.7 5.1 %collective-permute-start.32 = (bf16[32,512]{1,0:T(8,128)(2,1)S(1)}, bf16[32,512]{1,0:T(8,128)(2,1)S(1)}, u32[]{:S(2)}, u32[]{:S(2)}) collective-permute-start(bf16[32,512]{1,0:T(8,128)(2,1)S(1)} %get-tuple-element.116), channel_id=1, source_target_pairs={{0,96},{32,64},{64,32},{96,0},{1,97},{33,65},{65,33},{97,1},{2,98}... | collective-permute-start | bytes 98312 | tf_op jit(solution)/shard_map/ppermute | solution.py:41
  (3 other events, 9.8 us)
where the time goes:
time: 222 us; the launch traced here: 221 us
  waiting for transfers between devices  120 us (54%)
  starting transfers between devices  62 us (28%)
  Pallas kernels  35.1 us (16%)
  local copies, waits for them, and re-layouts  4.43 us (2%)
    ppermute x46, waiting for transfers between devices, flip(): return lax.ppermute(value, tuple(over), pairs)  120 us
    ppermute x46, starting transfers between devices, flip(): return lax.ppermute(value, tuple(over), pairs)  62 us
    pallas_call x3, Pallas kernels, product(): pl.pallas_call(functools.partial(product_kernel, family), out_shape=[jax....  20.7 us
    pallas_call x3, Pallas kernels, pack(): pl.pallas_call(functools.partial(pack_kernel, family), out_shape=shapes +...  5.36 us
  transfers between devices with their start and end apart: 46, of which 20 were waited for; matrix products, arithmetic and copies ran while one was open for 0% of the time, Pallas kernels for 14%

commit v1 on v0

--- a/solution.py
+++ b/solution.py
@@ -13,7 +13,7 @@
 AXES = ("x", "zl", "zh", "y", "c")
 SIZES = {"x": 4, "zl": 2, "zh": 2, "y": 4, "c": 2}
 TOKENS = 512
-FAMILIES = "yzx"
+FAMILIES = "zyx"
 ROWS_X, ROWS_Y, ROWS_Z = 128, 192, 192
 AT_Y, AT_Z = ROWS_X, ROWS_X + ROWS_Y
 VMEM = pl.BlockSpec(memory_space=pltpu.VMEM)
@@ -253,16 +253,35 @@
     )(where, *parts)
 
 
+def sum_kernel(*refs):
+    total = refs[0][...].astype(F32)
+    for part in refs[1:4]:
+        total = total + part[...].astype(F32)
+    refs[4][...] = total.astype(BF16)
+
+
+def sum_all(parts):
+    return pl.pallas_call(
+        sum_kernel,
+        out_shape=jax.ShapeDtypeStruct(parts[0].shape, BF16),
+        in_specs=[VMEM] * 4,
+        out_specs=VMEM,
+        cost_estimate=pl.CostEstimate(flops=1 << 18, bytes_accessed=1 << 20, transcendentals=0),
+        compiler_params=pltpu.CompilerParams(vmem_limit_bytes=8 << 20),
+        name="sum2_x",
+    )(*parts)
+
+
 def exchange(parts, axis):
     return [parts[0]] + [flip(parts[d], axis, d) for d in range(1, len(parts))]
 
 
 def final_kernel(where, *refs):
-    fx, fy, fz, out = refs[:4], refs[4:8], refs[8:10], refs[10]
-    x, zl = where[0], where[2]
+    fx, fy, fz, out = refs[0], refs[1:5], refs[5:7], refs[7]
+    zl = where[2]
     quarter, half = ROWS_X // 4, ROWS_Z // 2
-    for d in range(4):
-        out[0, pl.ds(pl.multiple_of((x ^ d) * quarter, 16), quarter), :] = fx[d][...].astype(F32)
+    for source in range(4):
+        out[0, source * quarter : (source + 1) * quarter, :] = fx[source].astype(F32)
     total = fy[0][...]
     for part in fy[1:]:
         total = total + part[...].astype(F32)
@@ -309,19 +328,19 @@
     px = exchange(px, "y")
     py = exchange(py, "z")
     pz = exchange(pz, "x")
-    px = sum_and_cut(px, where, lambda pos, d: (pos[0] ^ d,), (ROWS_X // 4, TOKENS), 3)
+    px = sum_all(px)
     pz = sum_and_cut(pz, where, lambda pos, d: (pos[2] ^ d,), (ROWS_Z // 2, TOKENS), 1)
-    px = exchange(px, "x")
+    px = lax.all_to_all(px, "x", split_axis=0, concat_axis=0, tiled=True)
     pz = exchange(pz, "z")
     return pl.pallas_call(
         final_kernel,
         out_shape=jax.ShapeDtypeStruct((1, 512, TOKENS), F32),
-        in_specs=[SMEM] + [VMEM] * 10,
+        in_specs=[SMEM] + [VMEM] * 7,
         out_specs=VMEM,
         cost_estimate=pl.CostEstimate(flops=1 << 20, bytes_accessed=3 << 20, transcendentals=0),
         compiler_params=pltpu.CompilerParams(vmem_limit_bytes=8 << 20),
         name="final",
-    )(where, *px, *py, *pz)
+    )(where, px, *py, *pz)
 
 
 def solution(mesh):

time: 222 us -> 217 us (0.977); the launches traced: 221 us -> 214 us
  starting transfers between devices: 62 us -> 57.4 us
  waiting for transfers between devices: 120 us -> 117 us
    ppermute x46 -> x43, starting transfers between devices: 62 us -> 53.2 us  [flip(): return lax.ppermute(value, tuple(over), pairs)]
    ppermute x46 -> x43, waiting for transfers between devices: 120 us -> 111 us  [flip(): return lax.ppermute(value, tuple(over), pairs)]
    all_to_all x0 -> x1, waiting for transfers between devices: none -> 5.24 us  [per_device(): px = lax.all_to_all(px, 'x', split_axis=0, concat_axis=0, tiled=True)]
    all_to_all x0 -> x1, starting transfers between devices: none -> 4.14 us  [per_device(): px = lax.all_to_all(px, 'x', split_axis=0, concat_axis=0, tiled=True)]
  transfers between devices with their start and end apart: 46 -> 44, of which waited for: 20 -> 18; matrix products, arithmetic and copies ran while one was open for 0% -> 0% of each run, Pallas kernels for 14% -> 15%
where the time goes in v1:
time: 217 us; the launch traced here: 214 us
  waiting for transfers between devices  117 us (54%)
  starting transfers between devices  57.4 us (26%)
  Pallas kernels  35.5 us (16%)
  local copies, waits for them, and re-layouts  4.43 us (2%)
    ppermute x43, waiting for transfers between devices, flip(): return lax.ppermute(value, tuple(over), pairs)  111 us
    ppermute x43, starting transfers between devices, flip(): return lax.ppermute(value, tuple(over), pairs)  53.2 us
    pallas_call x3, Pallas kernels, product(): pl.pallas_call(functools.partial(product_kernel, family), out_shape=[jax....  20.8 us
    pallas_call x3, Pallas kernels, pack(): pl.pallas_call(functools.partial(pack_kernel, family), out_shape=shapes +...  5.36 us
    all_to_all x1, waiting for transfers between devices, per_device(): px = lax.all_to_all(px, 'x', split_axis=0, concat_axis=0, tiled=True)  5.24 us
    unnamed x10, local copies, waits for them, and re-layouts  4.34 us
  transfers between devices with their start and end apart: 44, of which 18 were waited for; matrix products, arithmetic and copies ran while one was open for 0% of the time, Pallas kernels for 15%

profile of v1, /device:TPU:8, one launch (start us, length us, event | category | flops | bytes accessed | tf_op | source)
XLA Modules:
  0.0 214.2 jit_solution(5020876500746224875)
XLA Ops:
  0.1 3.4 %copy-done = bf16[4,8192,128]{2,1,0:T(8,128)(2,1)S(1)} copy-done((bf16[4,8192,128]{2,1,0:T(8,128)(2,1)S(1)}, bf16[4,8192,128]{2,1,0:T(8,128)(2,1)}, u32[]{:S(2)}) %copy-start) | copy-done | bytes 8388632
  4.4 1.9 shard_map.37
  6.3 2.0 collective-permute-start
  8.3 3.6 %collective-permute-start.1 = (bf16[7,4,96,128]{3,2,1,0:T(8,128)(2,1)S(1)}, bf16[7,4,96,128]{3,2,1,0:T(8,128)(2,1)S(1)}, u32[]{:S(2)}, u32[]{:S(2)}) collective-permute-start(bf16[7,4,96,128]{3,2,1,0:T(8,128)(2,1)S(1)} %get-tuple-element.71), channel_id=1, source_target_pairs={{0,8},{8,0},{16,24},{24,16},{1,9},{9,1},{17,25},{25,17},{2,10},{10... | collective-permute-start | bytes 2064392 | tf_op jit(solution)/shard_map/ppermute | solution.py:41
  11.9 1.9 shard_map.38
  14.4 2.6 %collective-permute-start.4 = (bf16[7,2,192,128]{3,2,1,0:T(8,128)(2,1)S(1)}, bf16[7,2,192,128]{3,2,1,0:T(8,128)(2,1)S(1)}, u32[]{:S(2)}, u32[]{:S(2)}) collective-permute-start(bf16[7,2,192,128]{3,2,1,0:T(8,128)(2,1)S(1)} %get-tuple-element.76), channel_id=1, source_target_pairs={{0,4},{2,6},{4,0},{6,2},{1,5},{3,7},{5,1},{7,3},{8,12},{10,14},{12... | collective-permute-start | bytes 2064392 | tf_op jit(solution)/shard_map/ppermute | solution.py:41
  16.9 7.8 %collective-permute-done.refs_1_ = bf16[7,4,96,128]{3,2,1,0:T(8,128)(2,1)S(1)} collective-permute-done((bf16[7,4,96,128]{3,2,1,0:T(8,128)(2,1)S(1)}, bf16[7,4,96,128]{3,2,1,0:T(8,128)(2,1)S(1)}, u32[]{:S(2)}, u32[]{:S(2)}) %collective-permute-start) | collective-permute-done | bytes 688160 | tf_op jit(solution)/shard_map/ppermute | solution.py:41
  24.7 1.6 collective-permute-start.5
  26.3 15.6 %collective-permute-done.1.refs_2_ = bf16[7,4,96,128]{3,2,1,0:T(8,128)(2,1)S(1)} collective-permute-done((bf16[7,4,96,128]{3,2,1,0:T(8,128)(2,1)S(1)}, bf16[7,4,96,128]{3,2,1,0:T(8,128)(2,1)S(1)}, u32[]{:S(2)}, u32[]{:S(2)}) %collective-permute-start.1) | collective-permute-done | bytes 688160 | tf_op jit(solution)/shard_map/ppermute | solution.py:41
  41.9 1.6 shard_map.39
  45.5 1.6 collective-permute-start.6
  47.1 2.7 %collective-permute-start.7 = (bf16[8,2,4,32,128]{4,3,2,1,0:T(8,128)(2,1)S(1)}, bf16[8,2,4,32,128]{4,3,2,1,0:T(8,128)(2,1)S(1)}, u32[]{:S(2)}, u32[]{:S(2)}) collective-permute-start(bf16[8,2,4,32,128]{4,3,2,1,0:T(8,128)(2,1)S(1)} %get-tuple-element.81), channel_id=1, source_target_pairs={{0,64},{32,96},{64,0},{96,32},{1,65},{33,97},{65,1},{97,33},{2,66}... | collective-permute-start | bytes 1572872 | tf_op jit(solution)/shard_map/ppermute | solution.py:41
  49.8 5.2 %collective-permute-done.5.refs_3_ = bf16[7,2,192,128]{3,2,1,0:T(8,128)(2,1)S(1)} collective-permute-done((bf16[7,2,192,128]{3,2,1,0:T(8,128)(2,1)S(1)}, bf16[7,2,192,128]{3,2,1,0:T(8,128)(2,1)S(1)}, u32[]{:S(2)}, u32[]{:S(2)}) %collective-permute-start.5) | collective-permute-done | bytes 688160 | tf_op jit(solution)/shard_map/ppermute | solution.py:41
  55.0 2.8 %collective-permute-start.8 = (bf16[8,2,4,32,128]{4,3,2,1,0:T(8,128)(2,1)S(1)}, bf16[8,2,4,32,128]{4,3,2,1,0:T(8,128)(2,1)S(1)}, u32[]{:S(2)}, u32[]{:S(2)}) collective-permute-start(bf16[8,2,4,32,128]{4,3,2,1,0:T(8,128)(2,1)S(1)} %get-tuple-element.82), channel_id=1, source_target_pairs={{0,96},{32,64},{64,32},{96,0},{1,97},{33,65},{65,33},{97,1},{2,98}... | collective-permute-start | bytes 1572872 | tf_op jit(solution)/shard_map/ppermute | solution.py:41
  57.7 1.5 shard_map.41
  59.3 1.1 collective-permute-done.6.refs_1_
  60.4 2.6 %collective-permute-start.11 = (bf16[4,4,96,128]{3,2,1,0:T(8,128)(2,1)S(1)}, bf16[4,4,96,128]{3,2,1,0:T(8,128)(2,1)S(1)}, u32[]{:S(2)}, u32[]{:S(2)}) collective-permute-start(bf16[4,4,96,128]{3,2,1,0:T(8,128)(2,1)S(1)} %get-tuple-element.86), channel_id=1, source_target_pairs={{0,9},{1,8},{8,1},{9,0},{16,25},{17,24},{24,17},{25,16},{2,11},{3,... | collective-permute-start | bytes 1179656 | tf_op jit(solution)/shard_map/ppermute | solution.py:41
  63.0 10.4 %collective-permute-done.7.refs_2_ = bf16[8,2,4,32,128]{4,3,2,1,0:T(8,128)(2,1)S(1)} collective-permute-done((bf16[8,2,4,32,128]{4,3,2,1,0:T(8,128)(2,1)S(1)}, bf16[8,2,4,32,128]{4,3,2,1,0:T(8,128)(2,1)S(1)}, u32[]{:S(2)}, u32[]{:S(2)}) %collective-permute-start.7) | collective-permute-done | bytes 524320 | tf_op jit(solution)/shard_map/ppermute | solution.py:41
  73.4 5.3 %collective-permute-done.8.refs_3_ = bf16[8,2,4,32,128]{4,3,2,1,0:T(8,128)(2,1)S(1)} collective-permute-done((bf16[8,2,4,32,128]{4,3,2,1,0:T(8,128)(2,1)S(1)}, bf16[8,2,4,32,128]{4,3,2,1,0:T(8,128)(2,1)S(1)}, u32[]{:S(2)}, u32[]{:S(2)}) %collective-permute-start.8) | collective-permute-done | bytes 524320 | tf_op jit(solution)/shard_map/ppermute | solution.py:41
  78.6 1.3 shard_map.42
  80.0 2.2 %collective-permute-start.15 = (bf16[4,2,192,128]{3,2,1,0:T(8,128)(2,1)S(1)}, bf16[4,2,192,128]{3,2,1,0:T(8,128)(2,1)S(1)}, u32[]{:S(2)}, u32[]{:S(2)}) collective-permute-start(bf16[4,2,192,128]{3,2,1,0:T(8,128)(2,1)S(1)} %get-tuple-element.91), channel_id=1, source_target_pairs={{0,3},{1,2},{2,1},{3,0},{4,7},{5,6},{6,5},{7,4},{8,11},{9,10},{10,... | collective-permute-start | bytes 1179656 | tf_op jit(solution)/shard_map/ppermute | solution.py:41
  82.1 3.5 %collective-permute-done.12 = bf16[4,4,96,128]{3,2,1,0:T(8,128)(2,1)S(1)} collective-permute-done((bf16[4,4,96,128]{3,2,1,0:T(8,128)(2,1)S(1)}, bf16[4,4,96,128]{3,2,1,0:T(8,128)(2,1)S(1)}, u32[]{:S(2)}, u32[]{:S(2)}) %collective-permute-start.12) | collective-permute-done | bytes 393248 | tf_op jit(solution)/shard_map/ppermute | solution.py:41
  85.6 1.7 collective-permute-start.16
  88.3 7.6 %shard_map.43 = (bf16[8,96,512]{2,1,0:T(8,128)(2,1)S(1)}, bf16[8,96,512]{2,1,0:T(8,128)(2,1)S(1)}, bf16[8,96,512]{2,1,0:T(8,128)(2,1)S(1)}, bf16[8,96,512]{2,1,0:T(8,128)(2,1)S(1)}, s32[1]{0:T(128)}) custom-call(s32[5]{0:T(128)S(1)} %stack.23.where, f32[8]{0:T(128)S(1)} %convert_multiply_fusion.factors, s32[1]{0:T(128)} %get-tuple-element.83.order, ...), custom_call_target="tpu_custom_call" | custom-call | flops 6442450944 | bytes 8388608 | tf_op jit(solution)/shard_map/pallas_call | solution.py:221
  96.0 6.2 %collective-permute-done.16 = bf16[4,2,192,128]{3,2,1,0:T(8,128)(2,1)S(1)} collective-permute-done((bf16[4,2,192,128]{3,2,1,0:T(8,128)(2,1)S(1)}, bf16[4,2,192,128]{3,2,1,0:T(8,128)(2,1)S(1)}, u32[]{:S(2)}, u32[]{:S(2)}) %collective-permute-start.16) | collective-permute-done | bytes 393248 | tf_op jit(solution)/shard_map/ppermute | solution.py:41
  102.2 4.1 %collective-permute-done.17 = bf16[4,2,192,128]{3,2,1,0:T(8,128)(2,1)S(1)} collective-permute-done((bf16[4,2,192,128]{3,2,1,0:T(8,128)(2,1)S(1)}, bf16[4,2,192,128]{3,2,1,0:T(8,128)(2,1)S(1)}, u32[]{:S(2)}, u32[]{:S(2)}) %collective-permute-start.17) | collective-permute-done | bytes 393248 | tf_op jit(solution)/shard_map/ppermute | solution.py:41
  106.3 1.4 collective-permute-start.21
  107.7 1.2 collective-permute-start.22
  108.9 7.6 %shard_map.44 = (bf16[2,384,512]{2,1,0:T(8,128)(2,1)S(1)}, bf16[2,384,512]{2,1,0:T(8,128)(2,1)S(1)}, bf16[2,384,512]{2,1,0:T(8,128)(2,1)S(1)}, bf16[2,384,512]{2,1,0:T(8,128)(2,1)S(1)}, s32[1]{0:T(128)}) custom-call(s32[5]{0:T(128)S(1)} %stack.23.where, f32[8]{0:T(128)S(1)} %convert_multiply_fusion.factors, s32[1]{0:T(128)} %get-tuple-element.89.order, ...), custom_call_target="tpu_custom_call" | custom-call | flops 6442450944 | bytes 8388608 | tf_op jit(solution)/shard_map/pallas_call | solution.py:221
  116.5 2.6 %collective-permute-start.36 = (bf16[8,96,512]{2,1,0:T(8,128)(2,1)S(1)}, bf16[8,96,512]{2,1,0:T(8,128)(2,1)S(1)}, u32[]{:S(2)}, u32[]{:S(2)}) collective-permute-start(bf16[8,96,512]{2,1,0:T(8,128)(2,1)S(1)} %get-tuple-element.118), channel_id=1, source_target_pairs={{0,2},{2,0},{4,6},{6,4},{1,3},{3,1},{5,7},{7,5},{8,10},{10,8},{12,... | collective-permute-start | bytes 2359304 | tf_op jit(solution)/shard_map/ppermute | solution.py:41
  119.1 3.8 %collective-permute-done.22 = bf16[4,2,4,32,128]{4,3,2,1,0:T(8,128)(2,1)S(1)} collective-permute-done((bf16[4,2,4,32,128]{4,3,2,1,0:T(8,128)(2,1)S(1)}, bf16[4,2,4,32,128]{4,3,2,1,0:T(8,128)(2,1)S(1)}, u32[]{:S(2)}, u32[]{:S(2)}) %collective-permute-start.22) | collective-permute-done | bytes 262176 | tf_op jit(solution)/shard_map/ppermute | solution.py:41
  122.9 5.7 %shard_map.45 = (bf16[4,128,512]{2,1,0:T(8,128)(2,1)S(1)}, bf16[4,128,512]{2,1,0:T(8,128)(2,1)S(1)}, bf16[4,128,512]{2,1,0:T(8,128)(2,1)S(1)}, bf16[4,128,512]{2,1,0:T(8,128)(2,1)S(1)}, s32[1]{0:T(128)}) custom-call(s32[5]{0:T(128)S(1)} %stack.23.where, f32[8]{0:T(128)S(1)} %convert_multiply_fusion.factors, s32[1]{0:T(128)} %get-tuple-element.95.order, ...), custom_call_target="tpu_custom_call" | custom-call | flops 4294967296 | bytes 8388608 | tf_op jit(solution)/shard_map/pallas_call | solution.py:221
  129.3 1.7 collective-permute-start.25
  131.0 2.4 %collective-permute-start.26 = (bf16[4,128,512]{2,1,0:T(8,128)(2,1)S(1)}, bf16[4,128,512]{2,1,0:T(8,128)(2,1)S(1)}, u32[]{:S(2)}, u32[]{:S(2)}) collective-permute-start(bf16[4,128,512]{2,1,0:T(8,128)(2,1)S(1)} %get-tuple-element.104), channel_id=1, source_target_pairs={{0,24},{8,16},{16,8},{24,0},{1,25},{9,17},{17,9},{25,1},{2,26},{10... | collective-permute-start | bytes 1572872 | tf_op jit(solution)/shard_map/ppermute | solution.py:41
  133.3 1.7 collective-permute-start.37
  135.1 8.4 %collective-permute-done.24 = bf16[4,128,512]{2,1,0:T(8,128)(2,1)S(1)} collective-permute-done((bf16[4,128,512]{2,1,0:T(8,128)(2,1)S(1)}, bf16[4,128,512]{2,1,0:T(8,128)(2,1)S(1)}, u32[]{:S(2)}, u32[]{:S(2)}) %collective-permute-start.24) | collective-permute-done | bytes 524320 | tf_op jit(solution)/shard_map/ppermute | solution.py:41
  144.1 10.4 %collective-permute-done.25 = bf16[4,128,512]{2,1,0:T(8,128)(2,1)S(1)} collective-permute-done((bf16[4,128,512]{2,1,0:T(8,128)(2,1)S(1)}, bf16[4,128,512]{2,1,0:T(8,128)(2,1)S(1)}, u32[]{:S(2)}, u32[]{:S(2)}) %collective-permute-start.25) | collective-permute-done | bytes 524320 | tf_op jit(solution)/shard_map/ppermute | solution.py:41
  154.5 2.6 %collective-permute-done.26 = bf16[4,128,512]{2,1,0:T(8,128)(2,1)S(1)} collective-permute-done((bf16[4,128,512]{2,1,0:T(8,128)(2,1)S(1)}, bf16[4,128,512]{2,1,0:T(8,128)(2,1)S(1)}, u32[]{:S(2)}, u32[]{:S(2)}) %collective-permute-start.26) | collective-permute-done | bytes 524320 | tf_op jit(solution)/shard_map/ppermute | solution.py:41
  157.1 1.2 collective-permute-start.31
  160.1 3.4 %collective-permute-start.27 = (bf16[4,32,512]{2,1,0:T(8,128)(2,1)S(1)}, bf16[4,32,512]{2,1,0:T(8,128)(2,1)S(1)}, u32[]{:S(2)}, u32[]{:S(2)}) collective-permute-start(bf16[4,32,512]{2,1,0:T(8,128)(2,1)S(1)} %get-tuple-element.106), channel_id=1, source_target_pairs={{0,2},{2,0},{4,6},{6,4},{1,3},{3,1},{5,7},{7,5},{8,10},{10,8},{12,... | collective-permute-start | bytes 393224 | tf_op jit(solution)/shard_map/ppermute | solution.py:41
  163.5 7.7 %collective-permute-done.38 = bf16[8,96,512]{2,1,0:T(8,128)(2,1)S(1)} collective-permute-done((bf16[8,96,512]{2,1,0:T(8,128)(2,1)S(1)}, bf16[8,96,512]{2,1,0:T(8,128)(2,1)S(1)}, u32[]{:S(2)}, u32[]{:S(2)}) %collective-permute-start.38) | collective-permute-done | bytes 786464 | tf_op jit(solution)/shard_map/ppermute | solution.py:41
  172.8 3.4 %collective-permute-start.28 = (bf16[4,32,512]{2,1,0:T(8,128)(2,1)S(1)}, bf16[4,32,512]{2,1,0:T(8,128)(2,1)S(1)}, u32[]{:S(2)}, u32[]{:S(2)}) collective-permute-start(bf16[4,32,512]{2,1,0:T(8,128)(2,1)S(1)} %get-tuple-element.107), channel_id=1, source_target_pairs={{0,4},{2,6},{4,0},{6,2},{1,5},{3,7},{5,1},{7,3},{8,12},{10,14},{12... | collective-permute-start | bytes 393224 | tf_op jit(solution)/shard_map/ppermute | solution.py:41
  176.6 16.3 %collective-permute-done.31 = bf16[2,384,512]{2,1,0:T(8,128)(2,1)S(1)} collective-permute-done((bf16[2,384,512]{2,1,0:T(8,128)(2,1)S(1)}, bf16[2,384,512]{2,1,0:T(8,128)(2,1)S(1)}, u32[]{:S(2)}, u32[]{:S(2)}) %collective-permute-start.31) | collective-permute-done | bytes 786464 | tf_op jit(solution)/shard_map/ppermute | solution.py:41
  193.3 2.3 %collective-permute-done.32 = bf16[2,384,512]{2,1,0:T(8,128)(2,1)S(1)} collective-permute-done((bf16[2,384,512]{2,1,0:T(8,128)(2,1)S(1)}, bf16[2,384,512]{2,1,0:T(8,128)(2,1)S(1)}, u32[]{:S(2)}, u32[]{:S(2)}) %collective-permute-start.32) | collective-permute-done | bytes 786464 | tf_op jit(solution)/shard_map/ppermute | solution.py:41
  197.1 4.7 %collective-permute-start.34 = (bf16[192,512]{1,0:T(8,128)(2,1)S(1)}, bf16[192,512]{1,0:T(8,128)(2,1)S(1)}, u32[]{:S(2)}, u32[]{:S(2)}) collective-permute-start(bf16[192,512]{1,0:T(8,128)(2,1)S(1)} %get-tuple-element.115), channel_id=1, source_target_pairs={{0,8},{8,0},{16,24},{24,16},{1,9},{9,1},{17,25},{25,17},{2,10},{10... | collective-permute-start | bytes 589832 | tf_op jit(solution)/shard_map/ppermute | solution.py:41
  202.5 4.1 %all-to-all-start = ((bf16[4,32,512]{2,1,0:T(8,128)(2,1)}), bf16[4,32,512]{2,1,0:T(8,128)(2,1)S(1)}, u32[]{:S(2)}, u32[]{:S(2)}) async-start(bf16[4,32,512]{2,1,0:T(8,128)(2,1)} %sum2_x.1), calls=%async_computation | async-start | bytes 262144 | tf_op jit(solution)/shard_map/all_to_all | solution.py:333
  207.4 5.2 %all-to-all-done.refs_0_ = bf16[4,32,512]{2,1,0:T(8,128)(2,1)S(1)} async-done(((bf16[4,32,512]{2,1,0:T(8,128)(2,1)}), bf16[4,32,512]{2,1,0:T(8,128)(2,1)S(1)}, u32[]{:S(2)}, u32[]{:S(2)}) %all-to-all-start) | async-done | bytes 131104 | tf_op jit(solution)/shard_map/all_to_all | solution.py:333
  212.6 1.6 final.1
  (67 shorter events, 13.3 us)
Async XLA Ops:
  0.1 3.4 %copy-start = (bf16[4,8192,128]{2,1,0:T(8,128)(2,1)S(1)}, bf16[4,8192,128]{2,1,0:T(8,128)(2,1)}, u32[]{:S(2)}) copy-start(bf16[4,8192,128]{2,1,0:T(8,128)(2,1)} %param.3) | copy-start | bytes 25165828
  4.4 7.5 %copy-start.1 = (bf16[4,8192,128]{2,1,0:T(8,128)(2,1)S(1)}, bf16[4,8192,128]{2,1,0:T(8,128)(2,1)}, u32[]{:S(2)}) copy-start(bf16[4,8192,128]{2,1,0:T(8,128)(2,1)} %param.3) | copy-start | bytes 25165828
  4.4 7.5 %copy-start.3 = (bf16[2,128,512]{2,1,0:T(8,128)(2,1)S(1)}, bf16[2,128,512]{2,1,0:T(8,128)(2,1)}, u32[]{:S(2)}) copy-start(bf16[2,128,512]{2,1,0:T(8,128)(2,1)} %act.5) | copy-start | bytes 786436
  6.3 18.4 %collective-permute-start = (bf16[7,4,96,128]{3,2,1,0:T(8,128)(2,1)S(1)}, bf16[7,4,96,128]{3,2,1,0:T(8,128)(2,1)S(1)}, u32[]{:S(2)}, u32[]{:S(2)}) collective-permute-start(bf16[7,4,96,128]{3,2,1,0:T(8,128)(2,1)S(1)} %get-tuple-element.70), channel_id=1, source_target_pairs={{0,16},{8,24},{16,0},{24,8},{1,17},{9,25},{17,1},{25,9},{2,18},{10... | collective-permute-start | bytes 2064392 | tf_op jit(solution)/shard_map/ppermute | solution.py:41
  8.3 33.6 %collective-permute-start.1 = (bf16[7,4,96,128]{3,2,1,0:T(8,128)(2,1)S(1)}, bf16[7,4,96,128]{3,2,1,0:T(8,128)(2,1)S(1)}, u32[]{:S(2)}, u32[]{:S(2)}) collective-permute-start(bf16[7,4,96,128]{3,2,1,0:T(8,128)(2,1)S(1)} %get-tuple-element.71), channel_id=1, source_target_pairs={{0,8},{8,0},{16,24},{24,16},{1,9},{9,1},{17,25},{25,17},{2,10},{10... | collective-permute-start | bytes 2064392 | tf_op jit(solution)/shard_map/ppermute | solution.py:41
  11.9 32.6 %collective-permute-start.2 = (bf16[7,4,96,128]{3,2,1,0:T(8,128)(2,1)S(1)}, bf16[7,4,96,128]{3,2,1,0:T(8,128)(2,1)S(1)}, u32[]{:S(2)}, u32[]{:S(2)}) collective-permute-start(bf16[7,4,96,128]{3,2,1,0:T(8,128)(2,1)S(1)} %get-tuple-element.72), channel_id=1, source_target_pairs={{0,24},{8,16},{16,8},{24,0},{1,25},{9,17},{17,9},{25,1},{2,26},{10... | collective-permute-start | bytes 2064392 | tf_op jit(solution)/shard_map/ppermute | solution.py:41
  13.8 31.7 %collective-permute-start.3 = (bf16[7,2,192,128]{3,2,1,0:T(8,128)(2,1)S(1)}, bf16[7,2,192,128]{3,2,1,0:T(8,128)(2,1)S(1)}, u32[]{:S(2)}, u32[]{:S(2)}) collective-permute-start(bf16[7,2,192,128]{3,2,1,0:T(8,128)(2,1)S(1)} %get-tuple-element.75), channel_id=1, source_target_pairs={{0,2},{2,0},{4,6},{6,4},{1,3},{3,1},{5,7},{7,5},{8,10},{10,8},{12,... | collective-permute-start | bytes 2064392 | tf_op jit(solution)/shard_map/ppermute | solution.py:41
  14.4 32.7 %collective-permute-start.4 = (bf16[7,2,192,128]{3,2,1,0:T(8,128)(2,1)S(1)}, bf16[7,2,192,128]{3,2,1,0:T(8,128)(2,1)S(1)}, u32[]{:S(2)}, u32[]{:S(2)}) collective-permute-start(bf16[7,2,192,128]{3,2,1,0:T(8,128)(2,1)S(1)} %get-tuple-element.76), channel_id=1, source_target_pairs={{0,4},{2,6},{4,0},{6,2},{1,5},{3,7},{5,1},{7,3},{8,12},{10,14},{12... | collective-permute-start | bytes 2064392 | tf_op jit(solution)/shard_map/ppermute | solution.py:41
  24.7 30.3 %collective-permute-start.5 = (bf16[7,2,192,128]{3,2,1,0:T(8,128)(2,1)S(1)}, bf16[7,2,192,128]{3,2,1,0:T(8,128)(2,1)S(1)}, u32[]{:S(2)}, u32[]{:S(2)}) collective-permute-start(bf16[7,2,192,128]{3,2,1,0:T(8,128)(2,1)S(1)} %get-tuple-element.77), channel_id=1, source_target_pairs={{0,6},{2,4},{4,2},{6,0},{1,7},{3,5},{5,3},{7,1},{8,14},{10,12},{12... | collective-permute-start | bytes 2064392 | tf_op jit(solution)/shard_map/ppermute | solution.py:41
  41.9 3.5 %collective-permute-start.9 = (bf16[4,4,96,128]{3,2,1,0:T(8,128)(2,1)S(1)}, bf16[4,4,96,128]{3,2,1,0:T(8,128)(2,1)S(1)}, u32[]{:S(2)}, u32[]{:S(2)}) collective-permute-start(bf16[4,4,96,128]{3,2,1,0:T(8,128)(2,1)S(1)} %get-tuple-element.84), channel_id=1, source_target_pairs={{0,1},{1,0},{2,3},{3,2},{4,5},{5,4},{6,7},{7,6},{8,9},{9,8},{10,11... | collective-permute-start | bytes 1179656 | tf_op jit(solution)/shard_map/ppermute | solution.py:41
  45.3 42.0 %collective-permute-start.13 = (bf16[4,3,4,96,128]{4,3,2,1,0:T(8,128)(2,1)S(1)}, bf16[4,3,4,96,128]{4,3,2,1,0:T(8,128)(2,1)S(1)}, u32[]{:S(2)}, u32[]{:S(2)}) collective-permute-start(bf16[4,3,4,96,128]{4,3,2,1,0:T(8,128)(2,1)S(1)} %get-tuple-element.88), channel_id=1, source_target_pairs={{0,1},{1,0},{2,3},{3,2},{4,5},{5,4},{6,7},{7,6},{8,9},{9,8},{10,11... | collective-permute-start | bytes 3538952 | tf_op jit(solution)/shard_map/ppermute | solution.py:41
  45.4 13.8 %collective-permute-start.10 = (bf16[4,4,96,128]{3,2,1,0:T(8,128)(2,1)S(1)}, bf16[4,4,96,128]{3,2,1,0:T(8,128)(2,1)S(1)}, u32[]{:S(2)}, u32[]{:S(2)}) collective-permute-start(bf16[4,4,96,128]{3,2,1,0:T(8,128)(2,1)S(1)} %get-tuple-element.85), channel_id=1, source_target_pairs={{0,17},{1,16},{8,25},{9,24},{16,1},{17,0},{24,9},{25,8},{2,19},{3,... | collective-permute-start | bytes 1179656 | tf_op jit(solution)/shard_map/ppermute | solution.py:41
  45.5 14.9 %collective-permute-start.6 = (bf16[8,2,4,32,128]{4,3,2,1,0:T(8,128)(2,1)S(1)}, bf16[8,2,4,32,128]{4,3,2,1,0:T(8,128)(2,1)S(1)}, u32[]{:S(2)}, u32[]{:S(2)}) collective-permute-start(bf16[8,2,4,32,128]{4,3,2,1,0:T(8,128)(2,1)S(1)} %get-tuple-element.80), channel_id=1, source_target_pairs={{0,32},{32,0},{64,96},{96,64},{1,33},{33,1},{65,97},{97,65},{2,34}... | collective-permute-start | bytes 1572872 | tf_op jit(solution)/shard_map/ppermute | solution.py:41
  47.1 26.3 %collective-permute-start.7 = (bf16[8,2,4,32,128]{4,3,2,1,0:T(8,128)(2,1)S(1)}, bf16[8,2,4,32,128]{4,3,2,1,0:T(8,128)(2,1)S(1)}, u32[]{:S(2)}, u32[]{:S(2)}) collective-permute-start(bf16[8,2,4,32,128]{4,3,2,1,0:T(8,128)(2,1)S(1)} %get-tuple-element.81), channel_id=1, source_target_pairs={{0,64},{32,96},{64,0},{96,32},{1,65},{33,97},{65,1},{97,33},{2,66}... | collective-permute-start | bytes 1572872 | tf_op jit(solution)/shard_map/ppermute | solution.py:41
  55.0 23.6 %collective-permute-start.8 = (bf16[8,2,4,32,128]{4,3,2,1,0:T(8,128)(2,1)S(1)}, bf16[8,2,4,32,128]{4,3,2,1,0:T(8,128)(2,1)S(1)}, u32[]{:S(2)}, u32[]{:S(2)}) collective-permute-start(bf16[8,2,4,32,128]{4,3,2,1,0:T(8,128)(2,1)S(1)} %get-tuple-element.82), channel_id=1, source_target_pairs={{0,96},{32,64},{64,32},{96,0},{1,97},{33,65},{65,33},{97,1},{2,98}... | collective-permute-start | bytes 1572872 | tf_op jit(solution)/shard_map/ppermute | solution.py:41
  57.7 20.9 %copy-start.4 = (s32[8]{0:T(128)S(1)}, s32[8]{0:T(128)}, u32[]{:S(2)}) copy-start(s32[8]{0:T(128)} %param.5) | copy-start | bytes 100
  59.2 48.5 %collective-permute-start.18 = (bf16[4,3,2,192,128]{4,3,2,1,0:T(8,128)(2,1)S(1)}, bf16[4,3,2,192,128]{4,3,2,1,0:T(8,128)(2,1)S(1)}, u32[]{:S(2)}, u32[]{:S(2)}) collective-permute-start(bf16[4,3,2,192,128]{4,3,2,1,0:T(8,128)(2,1)S(1)} %get-tuple-element.94), channel_id=1, source_target_pairs={{0,1},{1,0},{2,3},{3,2},{4,5},{5,4},{6,7},{7,6},{8,9},{9,8},{10,11... | collective-permute-start | bytes 3538952 | tf_op jit(solution)/shard_map/ppermute | solution.py:41
  60.4 19.6 %collective-permute-start.11 = (bf16[4,4,96,128]{3,2,1,0:T(8,128)(2,1)S(1)}, bf16[4,4,96,128]{3,2,1,0:T(8,128)(2,1)S(1)}, u32[]{:S(2)}, u32[]{:S(2)}) collective-permute-start(bf16[4,4,96,128]{3,2,1,0:T(8,128)(2,1)S(1)} %get-tuple-element.86), channel_id=1, source_target_pairs={{0,9},{1,8},{8,1},{9,0},{16,25},{17,24},{24,17},{25,16},{2,11},{3,... | collective-permute-start | bytes 1179656 | tf_op jit(solution)/shard_map/ppermute | solution.py:41
  73.4 12.3 %collective-permute-start.12 = (bf16[4,4,96,128]{3,2,1,0:T(8,128)(2,1)S(1)}, bf16[4,4,96,128]{3,2,1,0:T(8,128)(2,1)S(1)}, u32[]{:S(2)}, u32[]{:S(2)}) collective-permute-start(bf16[4,4,96,128]{3,2,1,0:T(8,128)(2,1)S(1)} %get-tuple-element.87), channel_id=1, source_target_pairs={{0,25},{1,24},{8,17},{9,16},{16,9},{17,8},{24,1},{25,0},{2,27},{3,... | collective-permute-start | bytes 1179656 | tf_op jit(solution)/shard_map/ppermute | solution.py:41
  78.6 8.7 %collective-permute-start.14 = (bf16[4,2,192,128]{3,2,1,0:T(8,128)(2,1)S(1)}, bf16[4,2,192,128]{3,2,1,0:T(8,128)(2,1)S(1)}, u32[]{:S(2)}, u32[]{:S(2)}) collective-permute-start(bf16[4,2,192,128]{3,2,1,0:T(8,128)(2,1)S(1)} %get-tuple-element.90), channel_id=1, source_target_pairs={{0,1},{1,0},{2,3},{3,2},{4,5},{5,4},{6,7},{7,6},{8,9},{9,8},{10,11... | collective-permute-start | bytes 1179656 | tf_op jit(solution)/shard_map/ppermute | solution.py:41
  80.0 15.9 %collective-permute-start.15 = (bf16[4,2,192,128]{3,2,1,0:T(8,128)(2,1)S(1)}, bf16[4,2,192,128]{3,2,1,0:T(8,128)(2,1)S(1)}, u32[]{:S(2)}, u32[]{:S(2)}) collective-permute-start(bf16[4,2,192,128]{3,2,1,0:T(8,128)(2,1)S(1)} %get-tuple-element.91), channel_id=1, source_target_pairs={{0,3},{1,2},{2,1},{3,0},{4,7},{5,6},{6,5},{7,4},{8,11},{9,10},{10,... | collective-permute-start | bytes 1179656 | tf_op jit(solution)/shard_map/ppermute | solution.py:41
  85.6 16.5 %collective-permute-start.16 = (bf16[4,2,192,128]{3,2,1,0:T(8,128)(2,1)S(1)}, bf16[4,2,192,128]{3,2,1,0:T(8,128)(2,1)S(1)}, u32[]{:S(2)}, u32[]{:S(2)}) collective-permute-start(bf16[4,2,192,128]{3,2,1,0:T(8,128)(2,1)S(1)} %get-tuple-element.92), channel_id=1, source_target_pairs={{0,5},{1,4},{2,7},{3,6},{4,1},{5,0},{6,3},{7,2},{8,13},{9,12},{10,... | collective-permute-start | bytes 1179656 | tf_op jit(solution)/shard_map/ppermute | solution.py:41
  87.3 18.9 %collective-permute-start.17 = (bf16[4,2,192,128]{3,2,1,0:T(8,128)(2,1)S(1)}, bf16[4,2,192,128]{3,2,1,0:T(8,128)(2,1)S(1)}, u32[]{:S(2)}, u32[]{:S(2)}) collective-permute-start(bf16[4,2,192,128]{3,2,1,0:T(8,128)(2,1)S(1)} %get-tuple-element.93), channel_id=1, source_target_pairs={{0,7},{1,6},{2,5},{3,4},{4,3},{5,2},{6,1},{7,0},{8,15},{9,14},{10,... | collective-permute-start | bytes 1179656 | tf_op jit(solution)/shard_map/ppermute | solution.py:41
  87.3 35.6 %collective-permute-start.23 = (bf16[4,4,2,4,32,128]{5,4,3,2,1,0:T(8,128)(2,1)S(1)}, bf16[4,4,2,4,32,128]{5,4,3,2,1,0:T(8,128)(2,1)S(1)}, u32[]{:S(2)}, u32[]{:S(2)}) collective-permute-start(bf16[4,4,2,4,32,128]{5,4,3,2,1,0:T(8,128)(2,1)S(1)} %get-tuple-element.100), channel_id=1, source_target_pairs={{0,1},{1,0},{2,3},{3,2},{4,5},{5,4},{6,7},{7,6},{8,9},{9,8},{10,11... | collective-permute-start | bytes 3145736 | tf_op jit(solution)/shard_map/ppermute | solution.py:41
  95.9 20.6 %collective-permute-start.19 = (bf16[4,2,4,32,128]{4,3,2,1,0:T(8,128)(2,1)S(1)}, bf16[4,2,4,32,128]{4,3,2,1,0:T(8,128)(2,1)S(1)}, u32[]{:S(2)}, u32[]{:S(2)}) collective-permute-start(bf16[4,2,4,32,128]{4,3,2,1,0:T(8,128)(2,1)S(1)} %get-tuple-element.96), channel_id=1, source_target_pairs={{0,1},{1,0},{2,3},{3,2},{4,5},{5,4},{6,7},{7,6},{8,9},{9,8},{10,11... | collective-permute-start | bytes 786440 | tf_op jit(solution)/shard_map/ppermute | solution.py:41
  102.2 17.0 %collective-permute-start.20 = (bf16[4,2,4,32,128]{4,3,2,1,0:T(8,128)(2,1)S(1)}, bf16[4,2,4,32,128]{4,3,2,1,0:T(8,128)(2,1)S(1)}, u32[]{:S(2)}, u32[]{:S(2)}) collective-permute-start(bf16[4,2,4,32,128]{4,3,2,1,0:T(8,128)(2,1)S(1)} %get-tuple-element.97), channel_id=1, source_target_pairs={{0,33},{1,32},{32,1},{33,0},{64,97},{65,96},{96,65},{97,64},{2,35}... | collective-permute-start | bytes 786440 | tf_op jit(solution)/shard_map/ppermute | solution.py:41
  106.3 12.9 %collective-permute-start.21 = (bf16[4,2,4,32,128]{4,3,2,1,0:T(8,128)(2,1)S(1)}, bf16[4,2,4,32,128]{4,3,2,1,0:T(8,128)(2,1)S(1)}, u32[]{:S(2)}, u32[]{:S(2)}) collective-permute-start(bf16[4,2,4,32,128]{4,3,2,1,0:T(8,128)(2,1)S(1)} %get-tuple-element.98), channel_id=1, source_target_pairs={{0,65},{1,64},{32,97},{33,96},{64,1},{65,0},{96,33},{97,32},{2,67}... | collective-permute-start | bytes 786440 | tf_op jit(solution)/shard_map/ppermute | solution.py:41
  107.7 15.2 %collective-permute-start.22 = (bf16[4,2,4,32,128]{4,3,2,1,0:T(8,128)(2,1)S(1)}, bf16[4,2,4,32,128]{4,3,2,1,0:T(8,128)(2,1)S(1)}, u32[]{:S(2)}, u32[]{:S(2)}) collective-permute-start(bf16[4,2,4,32,128]{4,3,2,1,0:T(8,128)(2,1)S(1)} %get-tuple-element.99), channel_id=1, source_target_pairs={{0,97},{1,96},{32,65},{33,64},{64,33},{65,32},{96,1},{97,0},{2,99}... | collective-permute-start | bytes 786440 | tf_op jit(solution)/shard_map/ppermute | solution.py:41
  116.5 41.8 %collective-permute-start.36 = (bf16[8,96,512]{2,1,0:T(8,128)(2,1)S(1)}, bf16[8,96,512]{2,1,0:T(8,128)(2,1)S(1)}, u32[]{:S(2)}, u32[]{:S(2)}) collective-permute-start(bf16[8,96,512]{2,1,0:T(8,128)(2,1)S(1)} %get-tuple-element.118), channel_id=1, source_target_pairs={{0,2},{2,0},{4,6},{6,4},{1,3},{3,1},{5,7},{7,5},{8,10},{10,8},{12,... | collective-permute-start | bytes 2359304 | tf_op jit(solution)/shard_map/ppermute | solution.py:41
  128.6 14.9 %collective-permute-start.24 = (bf16[4,128,512]{2,1,0:T(8,128)(2,1)S(1)}, bf16[4,128,512]{2,1,0:T(8,128)(2,1)S(1)}, u32[]{:S(2)}, u32[]{:S(2)}) collective-permute-start(bf16[4,128,512]{2,1,0:T(8,128)(2,1)S(1)} %get-tuple-element.102), channel_id=1, source_target_pairs={{0,16},{8,24},{16,0},{24,8},{1,17},{9,25},{17,1},{25,9},{2,18},{10... | collective-permute-start | bytes 1572872 | tf_op jit(solution)/shard_map/ppermute | solution.py:41
  129.3 25.2 %collective-permute-start.25 = (bf16[4,128,512]{2,1,0:T(8,128)(2,1)S(1)}, bf16[4,128,512]{2,1,0:T(8,128)(2,1)S(1)}, u32[]{:S(2)}, u32[]{:S(2)}) collective-permute-start(bf16[4,128,512]{2,1,0:T(8,128)(2,1)S(1)} %get-tuple-element.103), channel_id=1, source_target_pairs={{0,8},{8,0},{16,24},{24,16},{1,9},{9,1},{17,25},{25,17},{2,10},{10... | collective-permute-start | bytes 1572872 | tf_op jit(solution)/shard_map/ppermute | solution.py:41
  131.0 26.1 %collective-permute-start.26 = (bf16[4,128,512]{2,1,0:T(8,128)(2,1)S(1)}, bf16[4,128,512]{2,1,0:T(8,128)(2,1)S(1)}, u32[]{:S(2)}, u32[]{:S(2)}) collective-permute-start(bf16[4,128,512]{2,1,0:T(8,128)(2,1)S(1)} %get-tuple-element.104), channel_id=1, source_target_pairs={{0,24},{8,16},{16,8},{24,0},{1,25},{9,17},{17,9},{25,1},{2,26},{10... | collective-permute-start | bytes 1572872 | tf_op jit(solution)/shard_map/ppermute | solution.py:41
  133.3 26.8 %collective-permute-start.37 = (bf16[8,96,512]{2,1,0:T(8,128)(2,1)S(1)}, bf16[8,96,512]{2,1,0:T(8,128)(2,1)S(1)}, u32[]{:S(2)}, u32[]{:S(2)}) collective-permute-start(bf16[8,96,512]{2,1,0:T(8,128)(2,1)S(1)} %get-tuple-element.119), channel_id=1, source_target_pairs={{0,4},{2,6},{4,0},{6,2},{1,5},{3,7},{5,1},{7,3},{8,12},{10,14},{12... | collective-permute-start | bytes 2359304 | tf_op jit(solution)/shard_map/ppermute | solution.py:41
  143.4 27.7 %collective-permute-start.38 = (bf16[8,96,512]{2,1,0:T(8,128)(2,1)S(1)}, bf16[8,96,512]{2,1,0:T(8,128)(2,1)S(1)}, u32[]{:S(2)}, u32[]{:S(2)}) collective-permute-start(bf16[8,96,512]{2,1,0:T(8,128)(2,1)S(1)} %get-tuple-element.120), channel_id=1, source_target_pairs={{0,6},{2,4},{4,2},{6,0},{1,7},{3,5},{5,3},{7,1},{8,14},{10,12},{12... | collective-permute-start | bytes 2359304 | tf_op jit(solution)/shard_map/ppermute | solution.py:41
  154.5 21.7 %collective-permute-start.30 = (bf16[2,384,512]{2,1,0:T(8,128)(2,1)S(1)}, bf16[2,384,512]{2,1,0:T(8,128)(2,1)S(1)}, u32[]{:S(2)}, u32[]{:S(2)}) collective-permute-start(bf16[2,384,512]{2,1,0:T(8,128)(2,1)S(1)} %get-tuple-element.110), channel_id=1, source_target_pairs={{0,32},{32,0},{64,96},{96,64},{1,33},{33,1},{65,97},{97,65},{2,34}... | collective-permute-start | bytes 2359304 | tf_op jit(solution)/shard_map/ppermute | solution.py:41
  157.1 35.8 %collective-permute-start.31 = (bf16[2,384,512]{2,1,0:T(8,128)(2,1)S(1)}, bf16[2,384,512]{2,1,0:T(8,128)(2,1)S(1)}, u32[]{:S(2)}, u32[]{:S(2)}) collective-permute-start(bf16[2,384,512]{2,1,0:T(8,128)(2,1)S(1)} %get-tuple-element.111), channel_id=1, source_target_pairs={{0,64},{32,96},{64,0},{96,32},{1,65},{33,97},{65,1},{97,33},{2,66}... | collective-permute-start | bytes 2359304 | tf_op jit(solution)/shard_map/ppermute | solution.py:41
  158.3 37.4 %collective-permute-start.32 = (bf16[2,384,512]{2,1,0:T(8,128)(2,1)S(1)}, bf16[2,384,512]{2,1,0:T(8,128)(2,1)S(1)}, u32[]{:S(2)}, u32[]{:S(2)}) collective-permute-start(bf16[2,384,512]{2,1,0:T(8,128)(2,1)S(1)} %get-tuple-element.112), channel_id=1, source_target_pairs={{0,96},{32,64},{64,32},{96,0},{1,97},{33,65},{65,33},{97,1},{2,98}... | collective-permute-start | bytes 2359304 | tf_op jit(solution)/shard_map/ppermute | solution.py:41
  160.1 12.7 %collective-permute-start.27 = (bf16[4,32,512]{2,1,0:T(8,128)(2,1)S(1)}, bf16[4,32,512]{2,1,0:T(8,128)(2,1)S(1)}, u32[]{:S(2)}, u32[]{:S(2)}) collective-permute-start(bf16[4,32,512]{2,1,0:T(8,128)(2,1)S(1)} %get-tuple-element.106), channel_id=1, source_target_pairs={{0,2},{2,0},{4,6},{6,4},{1,3},{3,1},{5,7},{7,5},{8,10},{10,8},{12,... | collective-permute-start | bytes 393224 | tf_op jit(solution)/shard_map/ppermute | solution.py:41
  172.1 29.6 %collective-permute-start.39 = (bf16[2,96,512]{2,1,0:T(8,128)(2,1)S(1)}, bf16[2,96,512]{2,1,0:T(8,128)(2,1)S(1)}, u32[]{:S(2)}, u32[]{:S(2)}) collective-permute-start(bf16[2,96,512]{2,1,0:T(8,128)(2,1)S(1)} %get-tuple-element.122), channel_id=1, source_target_pairs={{0,32},{32,0},{64,96},{96,64},{1,33},{33,1},{65,97},{97,65},{2,34}... | collective-permute-start | bytes 589832 | tf_op jit(solution)/shard_map/ppermute | solution.py:41
  172.8 23.8 %collective-permute-start.28 = (bf16[4,32,512]{2,1,0:T(8,128)(2,1)S(1)}, bf16[4,32,512]{2,1,0:T(8,128)(2,1)S(1)}, u32[]{:S(2)}, u32[]{:S(2)}) collective-permute-start(bf16[4,32,512]{2,1,0:T(8,128)(2,1)S(1)} %get-tuple-element.107), channel_id=1, source_target_pairs={{0,4},{2,6},{4,0},{6,2},{1,5},{3,7},{5,1},{7,3},{8,12},{10,14},{12... | collective-permute-start | bytes 393224 | tf_op jit(solution)/shard_map/ppermute | solution.py:41
  176.2 20.9 %collective-permute-start.29 = (bf16[4,32,512]{2,1,0:T(8,128)(2,1)S(1)}, bf16[4,32,512]{2,1,0:T(8,128)(2,1)S(1)}, u32[]{:S(2)}, u32[]{:S(2)}) collective-permute-start(bf16[4,32,512]{2,1,0:T(8,128)(2,1)S(1)} %get-tuple-element.108), channel_id=1, source_target_pairs={{0,6},{2,4},{4,2},{6,0},{1,7},{3,5},{5,3},{7,1},{8,14},{10,12},{12... | collective-permute-start | bytes 393224 | tf_op jit(solution)/shard_map/ppermute | solution.py:41
  192.9 13.7 %collective-permute-start.40 = (bf16[2,96,512]{2,1,0:T(8,128)(2,1)S(1)}, bf16[2,96,512]{2,1,0:T(8,128)(2,1)S(1)}, u32[]{:S(2)}, u32[]{:S(2)}) collective-permute-start(bf16[2,96,512]{2,1,0:T(8,128)(2,1)S(1)} %get-tuple-element.123), channel_id=1, source_target_pairs={{0,64},{32,96},{64,0},{96,32},{1,65},{33,97},{65,1},{97,33},{2,66}... | collective-permute-start | bytes 589832 | tf_op jit(solution)/shard_map/ppermute | solution.py:41
  195.6 11.0 %collective-permute-start.41 = (bf16[2,96,512]{2,1,0:T(8,128)(2,1)S(1)}, bf16[2,96,512]{2,1,0:T(8,128)(2,1)S(1)}, u32[]{:S(2)}, u32[]{:S(2)}) collective-permute-start(bf16[2,96,512]{2,1,0:T(8,128)(2,1)S(1)} %get-tuple-element.124), channel_id=1, source_target_pairs={{0,96},{32,64},{64,32},{96,0},{1,97},{33,65},{65,33},{97,1},{2,98}... | collective-permute-start | bytes 589832 | tf_op jit(solution)/shard_map/ppermute | solution.py:41
  196.6 16.0 %collective-permute-start.33 = (bf16[192,512]{1,0:T(8,128)(2,1)S(1)}, bf16[192,512]{1,0:T(8,128)(2,1)S(1)}, u32[]{:S(2)}, u32[]{:S(2)}) collective-permute-start(bf16[192,512]{1,0:T(8,128)(2,1)S(1)} %get-tuple-element.114), channel_id=1, source_target_pairs={{0,16},{8,24},{16,0},{24,8},{1,17},{9,25},{17,1},{25,9},{2,18},{10... | collective-permute-start | bytes 589832 | tf_op jit(solution)/shard_map/ppermute | solution.py:41
  197.1 15.5 %collective-permute-start.34 = (bf16[192,512]{1,0:T(8,128)(2,1)S(1)}, bf16[192,512]{1,0:T(8,128)(2,1)S(1)}, u32[]{:S(2)}, u32[]{:S(2)}) collective-permute-start(bf16[192,512]{1,0:T(8,128)(2,1)S(1)} %get-tuple-element.115), channel_id=1, source_target_pairs={{0,8},{8,0},{16,24},{24,16},{1,9},{9,1},{17,25},{25,17},{2,10},{10... | collective-permute-start | bytes 589832 | tf_op jit(solution)/shard_map/ppermute | solution.py:41
  201.8 10.8 %collective-permute-start.35 = (bf16[192,512]{1,0:T(8,128)(2,1)S(1)}, bf16[192,512]{1,0:T(8,128)(2,1)S(1)}, u32[]{:S(2)}, u32[]{:S(2)}) collective-permute-start(bf16[192,512]{1,0:T(8,128)(2,1)S(1)} %get-tuple-element.116), channel_id=1, source_target_pairs={{0,24},{8,16},{16,8},{24,0},{1,25},{9,17},{17,9},{25,1},{2,26},{10... | collective-permute-start | bytes 589832 | tf_op jit(solution)/shard_map/ppermute | solution.py:41
  202.5 10.1 %all-to-all-start = ((bf16[4,32,512]{2,1,0:T(8,128)(2,1)}), bf16[4,32,512]{2,1,0:T(8,128)(2,1)S(1)}, u32[]{:S(2)}, u32[]{:S(2)}) async-start(bf16[4,32,512]{2,1,0:T(8,128)(2,1)} %sum2_x.1), calls=%async_computation | async-start | bytes 262144 | tf_op jit(solution)/shard_map/all_to_all | solution.py:333
  207.3 5.3 %collective-permute-start.42 = (bf16[96,512]{1,0:T(8,128)(2,1)S(1)}, bf16[96,512]{1,0:T(8,128)(2,1)S(1)}, u32[]{:S(2)}, u32[]{:S(2)}) collective-permute-start(bf16[96,512]{1,0:T(8,128)(2,1)S(1)} %get-tuple-element.126), channel_id=1, source_target_pairs={{0,16},{8,24},{16,0},{24,8},{1,17},{9,25},{17,1},{25,9},{2,18},{10... | collective-permute-start | bytes 294920 | tf_op jit(solution)/shard_map/ppermute | solution.py:41
  (1 other events, 0.9 us)

commit v2 on v0

--- a/solution.py
+++ b/solution.py
@@ -170,26 +170,65 @@
 TILE = {"x": 64, "y": 96, "z": 96}
 
 
-def product_kernel(family, where, factors, order, *refs):
-    w, xd = refs[:8], refs[8]
-    outs, token, xcat, prods = refs[9:13], refs[13], refs[14], refs[15:17]
-    token[0] = order[0]
-    rows, tile = rows_of(family), TILE[family]
-    for s in range(8):
+EARLY = FAMILIES[:2]
+
+
+def fill(family, xcat, pieces, first):
+    for s, (ref, *at) in enumerate(pieces):
         for k in range(2):
             for ct in range(4):
                 for r in range(0, 128, CHUNK):
-                    at = plane_at((rows,), (k * 4 + ct) * 128 + r)
-                    piece = w[s][at] if s < 4 else xd[(s - 4, at[0] - 4, *at[1:])]
-                    xcat[s * 128 + r : s * 128 + r + CHUNK, k * TOKENS + ct * 128 : k * TOKENS + (ct + 1) * 128] = piece
+                    plane, rows = plane_at((rows_of(family),), (k * 4 + ct) * 128 + r)
+                    xcat[s * 128 + r : s * 128 + r + CHUNK, k * TOKENS + ct * 128 : k * TOKENS + (ct + 1) * 128] = ref[
+                        (*at, plane - 4 + (0 if at else first), rows)
+                    ]
+
+
+def times(family, w, start, xcat):
+    tile = TILE[family]
+    here = pl.ds(start if isinstance(start, int) else pl.multiple_of(start, 16), tile)
+    left = [jnp.concatenate([ref[j, here, :] for ref in w], axis=1) for j in range(4)]
+    return jnp.dot(jnp.concatenate(left, axis=0), xcat[...], preferred_element_type=F32)
+
+
+def begin_kernel(family, where, order, *refs):
+    w, out, token, xcat = refs[:4], refs[4], refs[5], refs[6]
+    token[0] = order[0]
+    fill(family, xcat, [(ref,) for ref in w], 4)
+    for t, (start, *_) in enumerate(plan_of(family, where)):
+        out[t] = times(family, w, start, xcat)
+
+
+def begin(family, pieces, where, order):
+    rows = rows_of(family)
+    pieces = [p.reshape(-1, rows, 128) for p in pieces]
+    return pl.pallas_call(
+        functools.partial(begin_kernel, family),
+        out_shape=[jax.ShapeDtypeStruct((4, 4 * TILE[family], 1024), F32), jax.ShapeDtypeStruct((1,), jnp.int32)],
+        in_specs=[SMEM, SMEM] + [VMEM] * 4,
+        out_specs=[VMEM, SMEM],
+        scratch_shapes=[pltpu.VMEM((512, 1024), BF16)],
+        cost_estimate=pl.CostEstimate(flops=4 * rows * 1024 * 1024, bytes_accessed=8 << 20, transcendentals=0),
+        compiler_params=pltpu.CompilerParams(vmem_limit_bytes=11 << 20),
+    )(where, order, *pieces)
+
+
+def product_kernel(family, where, factors, order, *refs):
+    early = family in EARLY
+    n = 4 if early else 8
+    w, xd, begun = refs[:n], refs[n], refs[n + 1] if early else None
+    refs = refs[n + 1 + early :]
+    outs, token, xcat, prods = refs[:4], refs[4], refs[5], refs[6:8]
+    token[0] = order[0]
+    tile = TILE[family]
+    shared = [(xd, d) for d in range(4)]
+    fill(family, xcat, shared if early else [(ref,) for ref in w[:4]] + shared, 4)
     plan = plan_of(family, where)
-
-    def multiply(start, prod):
-        here = pl.ds(start if isinstance(start, int) else pl.multiple_of(start, 16), tile)
-        left = [jnp.concatenate([w[s][j, here, :] for s in range(8)], axis=1) for j in range(4)]
-        prod[...] = jnp.dot(jnp.concatenate(left, axis=0), xcat[...], preferred_element_type=F32)
-
     anchors = [factors[g] for g in range(8)] if family == "z" else None
+
+    def multiply(t, prod):
+        total = times(family, w, plan[t][0], xcat)
+        prod[...] = begun[t] + total if early else total
 
     def combine(first, sends, prod):
         at = anchors or [factors[group] for _, _, group in sends]
@@ -205,28 +244,30 @@
                         total = total * anchor + terms[p]
                     outs[d][slot, first + r : first + r + 8, col : col + 256] = total.astype(BF16)
 
-    multiply(plan[0][0], prods[0])
+    multiply(0, prods[0])
     for t in range(4):
         if t < 3:
-            multiply(plan[t + 1][0], prods[(t + 1) % 2])
+            multiply(t + 1, prods[(t + 1) % 2])
         combine(plan[t][2], plan[t][3], prods[t % 2])
 
 
-def product(family, pieces, xd, where, factors, order):
+def product(family, pieces, xd, where, factors, order, begun):
     rows = rows_of(family)
     planes = planes_of(family)
-    pieces = [p.reshape(-1, rows, 128) for p in pieces]
+    pieces = [p.reshape(-1, rows, 128) for p in (pieces[4:] if begun else pieces)]
     xd = xd.reshape(4, planes - 4, rows, 128)
     flops = 2 * 4 * rows * 1024 * 1024
+    args = [*pieces, xd, *begun]
     out = pl.pallas_call(
         functools.partial(product_kernel, family),
         out_shape=[jax.ShapeDtypeStruct(OUT[family], BF16)] * 4 + [jax.ShapeDtypeStruct((1,), jnp.int32)],
-        in_specs=[SMEM, SMEM, SMEM] + [VMEM] * 9,
+        in_specs=[SMEM, SMEM, SMEM] + [VMEM] * len(args),
         out_specs=[VMEM] * 4 + [SMEM],
-        scratch_shapes=[pltpu.VMEM((1024, 1024), BF16)] + [pltpu.VMEM((4 * TILE[family], 1024), F32)] * 2,
+        scratch_shapes=[pltpu.VMEM((512 if begun else 1024, 1024), BF16)]
+        + [pltpu.VMEM((4 * TILE[family], 1024), F32)] * 2,
         cost_estimate=pl.CostEstimate(flops=2 * flops, bytes_accessed=8 << 20, transcendentals=0),
-        compiler_params=pltpu.CompilerParams(vmem_limit_bytes=22 << 20),
-    )(where, factors, order, *pieces, xd)
+        compiler_params=pltpu.CompilerParams(vmem_limit_bytes=12 << 20),
+    )(where, factors, order, *args)
     return out[:4], out[4]
 
 
@@ -257,12 +298,9 @@
     return [parts[0]] + [flip(parts[d], axis, d) for d in range(1, len(parts))]
 
 
-def final_kernel(where, *refs):
-    fx, fy, fz, out = refs[:4], refs[4:8], refs[8:10], refs[10]
-    x, zl = where[0], where[2]
-    quarter, half = ROWS_X // 4, ROWS_Z // 2
-    for d in range(4):
-        out[0, pl.ds(pl.multiple_of((x ^ d) * quarter, 16), quarter), :] = fx[d][...].astype(F32)
+def close_kernel(where, *refs):
+    fy, fz, out = refs[:4], refs[4:6], refs[6]
+    zl, half = where[2], ROWS_Z // 2
     total = fy[0][...]
     for part in fy[1:]:
         total = total + part[...].astype(F32)
@@ -271,6 +309,16 @@
         out[0, pl.ds(pl.multiple_of(AT_Z + (zl ^ d) * half, 16), half), :] = fz[d][...].astype(F32)
 
 
+def final_kernel(where, *refs):
+    fx, out, rows, sem = refs[:4], refs[5], refs[6], refs[7]
+    x, quarter = where[0], ROWS_X // 4
+    for d in range(4):
+        rows[pl.ds(pl.multiple_of((x ^ d) * quarter, 16), quarter), :] = fx[d][...].astype(F32)
+    copy = pltpu.make_async_copy(rows, out.at[0, pl.ds(0, ROWS_X)], sem.at[0])
+    copy.start()
+    copy.wait()
+
+
 def per_device(weight, activation, points):
     x, y, c = lax.axis_index("x"), lax.axis_index("y"), lax.axis_index("c")
     zl, zh = lax.axis_index("zl"), lax.axis_index("zh")
@@ -290,10 +338,20 @@
         shared[family] = flip(xd, "c", 0, 1)
         return order
 
+    begun = {family: [] for family in FAMILIES}
+
+    def early(family, order):
+        product_so_far, order = begin(family, pieces[family][:4], where, order)
+        begun[family] = [product_so_far]
+        return order
+
+    order = early(FAMILIES[0], share(FAMILIES[0], order))
+    order = share(FAMILIES[2], share(FAMILIES[1], order))
+    order = early(FAMILIES[1], order)
     for family in FAMILIES:
-        order = share(family, order)
-    for family in FAMILIES:
-        parts[family], order = product(family, pieces[family], shared[family], where, factors, order)
+        parts[family], order = product(
+            family, pieces[family], shared[family], where, factors, order, begun[family]
+        )
 
     px = exchange(parts["x"], "z")
     py = exchange(parts["y"], "x")
@@ -313,15 +371,26 @@
     pz = sum_and_cut(pz, where, lambda pos, d: (pos[2] ^ d,), (ROWS_Z // 2, TOKENS), 1)
     px = exchange(px, "x")
     pz = exchange(pz, "z")
+    out = pl.pallas_call(
+        close_kernel,
+        out_shape=jax.ShapeDtypeStruct((1, 512, TOKENS), F32),
+        in_specs=[SMEM] + [VMEM] * 6,
+        out_specs=VMEM,
+        cost_estimate=pl.CostEstimate(flops=1 << 20, bytes_accessed=3 << 20, transcendentals=0),
+        compiler_params=pltpu.CompilerParams(vmem_limit_bytes=8 << 20),
+        name="close",
+    )(where, *py, *pz)
     return pl.pallas_call(
         final_kernel,
         out_shape=jax.ShapeDtypeStruct((1, 512, TOKENS), F32),
-        in_specs=[SMEM] + [VMEM] * 10,
-        out_specs=VMEM,
-        cost_estimate=pl.CostEstimate(flops=1 << 20, bytes_accessed=3 << 20, transcendentals=0),
-        compiler_params=pltpu.CompilerParams(vmem_limit_bytes=8 << 20),
+        in_specs=[SMEM] + [VMEM] * 4 + [HBM],
+        out_specs=HBM,
+        input_output_aliases={5: 0},
+        scratch_shapes=[pltpu.VMEM((ROWS_X, TOKENS), F32), pltpu.SemaphoreType.DMA((1,))],
+        cost_estimate=pl.CostEstimate(flops=1 << 16, bytes_accessed=1 << 19, transcendentals=0),
+        compiler_params=pltpu.CompilerParams(vmem_limit_bytes=4 << 20),
         name="final",
-    )(where, *px, *py, *pz)
+    )(where, *px, out)
 
 
 def solution(mesh):

time: 222 us -> 216 us (0.973)
  waiting for transfers between devices: 120 us -> 111 us
  Pallas kernels: 35.1 us -> 40.4 us
  starting transfers between devices: 62 us -> 57.7 us
    ppermute x46, waiting for transfers between devices: 120 us -> 111 us  [flip(): return lax.ppermute(value, tuple(over), pairs)]
    pallas_call x0 -> x3, Pallas kernels: none -> 7.8 us  [the longest x2 6.18 us: begin(): pl.pallas_call(functools.partial(begin_kernel, family), out_shape=[jax.Sh...]
    ppermute x46, starting transfers between devices: 62 us -> 57.7 us  [flip(): return lax.ppermute(value, tuple(over), pairs)]
  transfers between devices with their start and end apart: 46 -> 46, of which waited for: 20 -> 19; matrix products, arithmetic and copies ran while one was open for 0% -> 0% of each run, Pallas kernels for 14% -> 17%
where the time goes in v2:
time: 216 us; the launch traced here: 214 us
  waiting for transfers between devices  111 us (51%)
  starting transfers between devices  57.7 us (27%)
  Pallas kernels  40.4 us (19%)
  local copies, waits for them, and re-layouts  4.43 us (2%)
    ppermute x46, waiting for transfers between devices, flip(): return lax.ppermute(value, tuple(over), pairs)  111 us
    ppermute x46, starting transfers between devices, flip(): return lax.ppermute(value, tuple(over), pairs)  57.7 us
    pallas_call x3, Pallas kernels, product(): pl.pallas_call(functools.partial(product_kernel, family), out_shape=[jax....  18.5 us
    pallas_call x2, Pallas kernels, begin(): pl.pallas_call(functools.partial(begin_kernel, family), out_shape=[jax.Sh...  6.18 us
    pallas_call x3, Pallas kernels, pack(): pl.pallas_call(functools.partial(pack_kernel, family), out_shape=shapes +...  5.36 us
    unnamed x10, local copies, waits for them, and re-layouts  4.34 us
  transfers between devices with their start and end apart: 46, of which 19 were waited for; matrix products, arithmetic and copies ran while one was open for 0% of the time, Pallas kernels for 17%

profile of v2, /device:TPU:8, one launch (start us, length us, event | category | flops | bytes accessed | tf_op | source)
XLA Modules:
  0.0 213.7 jit_solution(14600705388835599703)
XLA Ops:
  0.1 3.4 %copy-done = bf16[4,8192,128]{2,1,0:T(8,128)(2,1)S(1)} copy-done((bf16[4,8192,128]{2,1,0:T(8,128)(2,1)S(1)}, bf16[4,8192,128]{2,1,0:T(8,128)(2,1)}, u32[]{:S(2)}) %copy-start) | copy-done | bytes 8388632
  4.4 1.9 shard_map.37
  6.8 2.7 %collective-permute-start.1 = (bf16[7,2,192,128]{3,2,1,0:T(8,128)(2,1)S(1)}, bf16[7,2,192,128]{3,2,1,0:T(8,128)(2,1)S(1)}, u32[]{:S(2)}, u32[]{:S(2)}) collective-permute-start(bf16[7,2,192,128]{3,2,1,0:T(8,128)(2,1)S(1)} %get-tuple-element.79), channel_id=1, source_target_pairs={{0,4},{2,6},{4,0},{6,2},{1,5},{3,7},{5,1},{7,3},{8,12},{10,14},{12... | collective-permute-start | bytes 2064392 | tf_op jit(solution)/shard_map/ppermute | solution.py:41
  9.9 1.9 shard_map.38
  11.8 2.0 collective-permute-start.3
  13.8 3.6 %collective-permute-start.4 = (bf16[7,4,96,128]{3,2,1,0:T(8,128)(2,1)S(1)}, bf16[7,4,96,128]{3,2,1,0:T(8,128)(2,1)S(1)}, u32[]{:S(2)}, u32[]{:S(2)}) collective-permute-start(bf16[7,4,96,128]{3,2,1,0:T(8,128)(2,1)S(1)} %get-tuple-element.85), channel_id=1, source_target_pairs={{0,8},{8,0},{16,24},{24,16},{1,9},{9,1},{17,25},{25,17},{2,10},{10... | collective-permute-start | bytes 2064392 | tf_op jit(solution)/shard_map/ppermute | solution.py:41
  17.4 7.3 %collective-permute-done.refs_1_ = bf16[7,2,192,128]{3,2,1,0:T(8,128)(2,1)S(1)} collective-permute-done((bf16[7,2,192,128]{3,2,1,0:T(8,128)(2,1)S(1)}, bf16[7,2,192,128]{3,2,1,0:T(8,128)(2,1)S(1)}, u32[]{:S(2)}, u32[]{:S(2)}) %collective-permute-start) | collective-permute-done | bytes 688160 | tf_op jit(solution)/shard_map/ppermute | solution.py:41
  24.7 4.0 %collective-permute-start.5 = (bf16[7,4,96,128]{3,2,1,0:T(8,128)(2,1)S(1)}, bf16[7,4,96,128]{3,2,1,0:T(8,128)(2,1)S(1)}, u32[]{:S(2)}, u32[]{:S(2)}) collective-permute-start(bf16[7,4,96,128]{3,2,1,0:T(8,128)(2,1)S(1)} %get-tuple-element.86), channel_id=1, source_target_pairs={{0,24},{8,16},{16,8},{24,0},{1,25},{9,17},{17,9},{25,1},{2,26},{10... | collective-permute-start | bytes 2064392 | tf_op jit(solution)/shard_map/ppermute | solution.py:41
  28.8 10.7 %collective-permute-done.1.refs_2_ = bf16[7,2,192,128]{3,2,1,0:T(8,128)(2,1)S(1)} collective-permute-done((bf16[7,2,192,128]{3,2,1,0:T(8,128)(2,1)S(1)}, bf16[7,2,192,128]{3,2,1,0:T(8,128)(2,1)S(1)}, u32[]{:S(2)}, u32[]{:S(2)}) %collective-permute-start.1) | collective-permute-done | bytes 688160 | tf_op jit(solution)/shard_map/ppermute | solution.py:41
  39.5 1.6 shard_map.39
  42.5 2.5 %collective-permute-start.10 = (bf16[4,2,192,128]{3,2,1,0:T(8,128)(2,1)S(1)}, bf16[4,2,192,128]{3,2,1,0:T(8,128)(2,1)S(1)}, u32[]{:S(2)}, u32[]{:S(2)}) collective-permute-start(bf16[4,2,192,128]{3,2,1,0:T(8,128)(2,1)S(1)} %get-tuple-element.95), channel_id=1, source_target_pairs={{0,3},{1,2},{2,1},{3,0},{4,7},{5,6},{6,5},{7,4},{8,11},{9,10},{10,... | collective-permute-start | bytes 1179656 | tf_op jit(solution)/shard_map/ppermute | solution.py:41
  45.0 1.5 collective-permute-start.6
  46.5 3.0 %collective-permute-start.7 = (bf16[8,2,4,32,128]{4,3,2,1,0:T(8,128)(2,1)S(1)}, bf16[8,2,4,32,128]{4,3,2,1,0:T(8,128)(2,1)S(1)}, u32[]{:S(2)}, u32[]{:S(2)}) collective-permute-start(bf16[8,2,4,32,128]{4,3,2,1,0:T(8,128)(2,1)S(1)} %get-tuple-element.90), channel_id=1, source_target_pairs={{0,64},{32,96},{64,0},{96,32},{1,65},{33,97},{65,1},{97,33},{2,66}... | collective-permute-start | bytes 1572872 | tf_op jit(solution)/shard_map/ppermute | solution.py:41
  49.6 7.4 %collective-permute-done.5.refs_3_ = bf16[7,4,96,128]{3,2,1,0:T(8,128)(2,1)S(1)} collective-permute-done((bf16[7,4,96,128]{3,2,1,0:T(8,128)(2,1)S(1)}, bf16[7,4,96,128]{3,2,1,0:T(8,128)(2,1)S(1)}, u32[]{:S(2)}, u32[]{:S(2)}) %collective-permute-start.5) | collective-permute-done | bytes 688160 | tf_op jit(solution)/shard_map/ppermute | solution.py:41
  57.0 2.8 %collective-permute-start.8 = (bf16[8,2,4,32,128]{4,3,2,1,0:T(8,128)(2,1)S(1)}, bf16[8,2,4,32,128]{4,3,2,1,0:T(8,128)(2,1)S(1)}, u32[]{:S(2)}, u32[]{:S(2)}) collective-permute-start(bf16[8,2,4,32,128]{4,3,2,1,0:T(8,128)(2,1)S(1)} %get-tuple-element.91), channel_id=1, source_target_pairs={{0,96},{32,64},{64,32},{96,0},{1,97},{33,65},{65,33},{97,1},{2,98}... | collective-permute-start | bytes 1572872 | tf_op jit(solution)/shard_map/ppermute | solution.py:41
  59.7 3.1 %shard_map.41 = (f32[4,384,1024]{2,1,0:T(8,128)S(1)}, s32[1]{0:T(128)}) custom-call(s32[5]{0:T(128)S(1)} %stack.23.where, s32[1]{0:T(128)} %get-tuple-element.81.order, bf16[7,384,128]{2,1,0:T(8,128)(2,1)S(1)} %bitcast.61, bf16[7,384,128]{2,1,0:T(8,128)(2,1)S(1)} %bitcast.62, bf16[7,384,128]{2,1,0:T(8,128)(2,1)S(1)} %bitcast.63, ...), custom_call_target="tpu_custom_call" | custom-call | flops 1610612736 | bytes 8388608 | tf_op jit(solution)/shard_map/pallas_call | solution.py:205
  62.8 1.4 shard_map.42
  64.4 2.4 %collective-permute-start.11 = (bf16[4,2,192,128]{3,2,1,0:T(8,128)(2,1)S(1)}, bf16[4,2,192,128]{3,2,1,0:T(8,128)(2,1)S(1)}, u32[]{:S(2)}, u32[]{:S(2)}) collective-permute-start(bf16[4,2,192,128]{3,2,1,0:T(8,128)(2,1)S(1)} %get-tuple-element.96), channel_id=1, source_target_pairs={{0,5},{1,4},{2,7},{3,6},{4,1},{5,0},{6,3},{7,2},{8,13},{9,12},{10,... | collective-permute-start | bytes 1179656 | tf_op jit(solution)/shard_map/ppermute | solution.py:41
  66.8 5.6 %collective-permute-done.7.refs_2_ = bf16[8,2,4,32,128]{4,3,2,1,0:T(8,128)(2,1)S(1)} collective-permute-done((bf16[8,2,4,32,128]{4,3,2,1,0:T(8,128)(2,1)S(1)}, bf16[8,2,4,32,128]{4,3,2,1,0:T(8,128)(2,1)S(1)}, u32[]{:S(2)}, u32[]{:S(2)}) %collective-permute-start.7) | collective-permute-done | bytes 524320 | tf_op jit(solution)/shard_map/ppermute | solution.py:41
  72.4 8.4 %collective-permute-done.8.refs_3_ = bf16[8,2,4,32,128]{4,3,2,1,0:T(8,128)(2,1)S(1)} collective-permute-done((bf16[8,2,4,32,128]{4,3,2,1,0:T(8,128)(2,1)S(1)}, bf16[8,2,4,32,128]{4,3,2,1,0:T(8,128)(2,1)S(1)}, u32[]{:S(2)}, u32[]{:S(2)}) %collective-permute-start.8) | collective-permute-done | bytes 524320 | tf_op jit(solution)/shard_map/ppermute | solution.py:41
  80.8 1.3 shard_map.43
  82.1 3.1 %shard_map.44 = (f32[4,384,1024]{2,1,0:T(8,128)S(1)}, s32[1]{0:T(128)}) custom-call(s32[5]{0:T(128)S(1)} %stack.23.where, s32[1]{0:T(128)} %get-tuple-element.92.order, bf16[7,384,128]{2,1,0:T(8,128)(2,1)S(1)} %bitcast.57, bf16[7,384,128]{2,1,0:T(8,128)(2,1)S(1)} %bitcast.58, bf16[7,384,128]{2,1,0:T(8,128)(2,1)S(1)} %bitcast.59, ...), custom_call_target="tpu_custom_call" | custom-call | flops 1610612736 | bytes 8388608 | tf_op jit(solution)/shard_map/pallas_call | solution.py:205
  85.8 4.2 %collective-permute-start.16 = (bf16[4,4,96,128]{3,2,1,0:T(8,128)(2,1)S(1)}, bf16[4,4,96,128]{3,2,1,0:T(8,128)(2,1)S(1)}, u32[]{:S(2)}, u32[]{:S(2)}) collective-permute-start(bf16[4,4,96,128]{3,2,1,0:T(8,128)(2,1)S(1)} %get-tuple-element.103), channel_id=1, source_target_pairs={{0,9},{1,8},{8,1},{9,0},{16,25},{17,24},{24,17},{25,16},{2,11},{3,... | collective-permute-start | bytes 1179656 | tf_op jit(solution)/shard_map/ppermute | solution.py:41
  90.8 6.4 %shard_map.45 = (bf16[2,384,512]{2,1,0:T(8,128)(2,1)S(1)}, bf16[2,384,512]{2,1,0:T(8,128)(2,1)S(1)}, bf16[2,384,512]{2,1,0:T(8,128)(2,1)S(1)}, bf16[2,384,512]{2,1,0:T(8,128)(2,1)S(1)}, s32[1]{0:T(128)}) custom-call(s32[5]{0:T(128)S(1)} %stack.23.where, f32[8]{0:T(128)S(1)} %convert_multiply_fusion.factors, s32[1]{0:T(128)} %get-tuple-element.93.order, ...), custom_call_target="tpu_custom_call" | custom-call | flops 6442450944 | bytes 8388608 | tf_op jit(solution)/shard_map/pallas_call | solution.py:261
  97.5 10.1 %collective-permute-done.16 = bf16[4,4,96,128]{3,2,1,0:T(8,128)(2,1)S(1)} collective-permute-done((bf16[4,4,96,128]{3,2,1,0:T(8,128)(2,1)S(1)}, bf16[4,4,96,128]{3,2,1,0:T(8,128)(2,1)S(1)}, u32[]{:S(2)}, u32[]{:S(2)}) %collective-permute-start.16) | collective-permute-done | bytes 393248 | tf_op jit(solution)/shard_map/ppermute | solution.py:41
  108.0 2.5 %collective-permute-done.17 = bf16[4,4,96,128]{3,2,1,0:T(8,128)(2,1)S(1)} collective-permute-done((bf16[4,4,96,128]{3,2,1,0:T(8,128)(2,1)S(1)}, bf16[4,4,96,128]{3,2,1,0:T(8,128)(2,1)S(1)}, u32[]{:S(2)}, u32[]{:S(2)}) %collective-permute-start.17) | collective-permute-done | bytes 393248 | tf_op jit(solution)/shard_map/ppermute | solution.py:41
  110.4 1.9 collective-permute-start.21
  113.3 6.4 %shard_map.46 = (bf16[8,96,512]{2,1,0:T(8,128)(2,1)S(1)}, bf16[8,96,512]{2,1,0:T(8,128)(2,1)S(1)}, bf16[8,96,512]{2,1,0:T(8,128)(2,1)S(1)}, bf16[8,96,512]{2,1,0:T(8,128)(2,1)S(1)}, s32[1]{0:T(128)}) custom-call(s32[5]{0:T(128)S(1)} %stack.23.where, f32[8]{0:T(128)S(1)} %convert_multiply_fusion.factors, s32[1]{0:T(128)} %get-tuple-element.100.order, ...), custom_call_target="tpu_custom_call" | custom-call | flops 6442450944 | bytes 8388608 | tf_op jit(solution)/shard_map/pallas_call | solution.py:261
  120.5 2.2 %collective-permute-start.40 = (bf16[8,96,512]{2,1,0:T(8,128)(2,1)S(1)}, bf16[8,96,512]{2,1,0:T(8,128)(2,1)S(1)}, u32[]{:S(2)}, u32[]{:S(2)}) collective-permute-start(bf16[8,96,512]{2,1,0:T(8,128)(2,1)S(1)} %get-tuple-element.135), channel_id=1, source_target_pairs={{0,4},{2,6},{4,0},{6,2},{1,5},{3,7},{5,1},{7,3},{8,12},{10,14},{12... | collective-permute-start | bytes 2359304 | tf_op jit(solution)/shard_map/ppermute | solution.py:41
  124.0 3.6 %collective-permute-done.22 = bf16[4,2,4,32,128]{4,3,2,1,0:T(8,128)(2,1)S(1)} collective-permute-done((bf16[4,2,4,32,128]{4,3,2,1,0:T(8,128)(2,1)S(1)}, bf16[4,2,4,32,128]{4,3,2,1,0:T(8,128)(2,1)S(1)}, u32[]{:S(2)}, u32[]{:S(2)}) %collective-permute-start.22) | collective-permute-done | bytes 262176 | tf_op jit(solution)/shard_map/ppermute | solution.py:41
  127.6 5.7 %shard_map.47 = (bf16[4,128,512]{2,1,0:T(8,128)(2,1)S(1)}, bf16[4,128,512]{2,1,0:T(8,128)(2,1)S(1)}, bf16[4,128,512]{2,1,0:T(8,128)(2,1)S(1)}, bf16[4,128,512]{2,1,0:T(8,128)(2,1)S(1)}, s32[1]{0:T(128)}) custom-call(s32[5]{0:T(128)S(1)} %stack.23.where, f32[8]{0:T(128)S(1)} %convert_multiply_fusion.factors, s32[1]{0:T(128)} %get-tuple-element.107.order, ...), custom_call_target="tpu_custom_call" | custom-call | flops 4294967296 | bytes 8388608 | tf_op jit(solution)/shard_map/pallas_call | solution.py:261
  134.1 13.3 %collective-permute-done.24 = bf16[4,128,512]{2,1,0:T(8,128)(2,1)S(1)} collective-permute-done((bf16[4,128,512]{2,1,0:T(8,128)(2,1)S(1)}, bf16[4,128,512]{2,1,0:T(8,128)(2,1)S(1)}, u32[]{:S(2)}, u32[]{:S(2)}) %collective-permute-start.24) | collective-permute-done | bytes 524320 | tf_op jit(solution)/shard_map/ppermute | solution.py:41
  148.1 2.7 %collective-permute-start.35 = (bf16[2,384,512]{2,1,0:T(8,128)(2,1)S(1)}, bf16[2,384,512]{2,1,0:T(8,128)(2,1)S(1)}, u32[]{:S(2)}, u32[]{:S(2)}) collective-permute-start(bf16[2,384,512]{2,1,0:T(8,128)(2,1)S(1)} %get-tuple-element.128), channel_id=1, source_target_pairs={{0,96},{32,64},{64,32},{96,0},{1,97},{33,65},{65,33},{97,1},{2,98}... | collective-permute-start | bytes 2359304 | tf_op jit(solution)/shard_map/ppermute | solution.py:41
  150.8 6.7 %collective-permute-done.40 = bf16[8,96,512]{2,1,0:T(8,128)(2,1)S(1)} collective-permute-done((bf16[8,96,512]{2,1,0:T(8,128)(2,1)S(1)}, bf16[8,96,512]{2,1,0:T(8,128)(2,1)S(1)}, u32[]{:S(2)}, u32[]{:S(2)}) %collective-permute-start.40) | collective-permute-done | bytes 786464 | tf_op jit(solution)/shard_map/ppermute | solution.py:41
  157.5 2.7 %collective-permute-done.41 = bf16[8,96,512]{2,1,0:T(8,128)(2,1)S(1)} collective-permute-done((bf16[8,96,512]{2,1,0:T(8,128)(2,1)S(1)}, bf16[8,96,512]{2,1,0:T(8,128)(2,1)S(1)}, u32[]{:S(2)}, u32[]{:S(2)}) %collective-permute-start.41) | collective-permute-done | bytes 786464 | tf_op jit(solution)/shard_map/ppermute | solution.py:41
  161.2 11.4 %collective-permute-done.25 = bf16[4,128,512]{2,1,0:T(8,128)(2,1)S(1)} collective-permute-done((bf16[4,128,512]{2,1,0:T(8,128)(2,1)S(1)}, bf16[4,128,512]{2,1,0:T(8,128)(2,1)S(1)}, u32[]{:S(2)}, u32[]{:S(2)}) %collective-permute-start.25) | collective-permute-done | bytes 524320 | tf_op jit(solution)/shard_map/ppermute | solution.py:41
  173.1 10.6 %collective-permute-done.26 = bf16[4,128,512]{2,1,0:T(8,128)(2,1)S(1)} collective-permute-done((bf16[4,128,512]{2,1,0:T(8,128)(2,1)S(1)}, bf16[4,128,512]{2,1,0:T(8,128)(2,1)S(1)}, u32[]{:S(2)}, u32[]{:S(2)}) %collective-permute-start.26) | collective-permute-done | bytes 524320 | tf_op jit(solution)/shard_map/ppermute | solution.py:41
  183.7 1.8 collective-permute-start.43
  185.4 1.5 collective-permute-start.44
  187.7 2.0 collective-permute-start.27
  190.7 3.5 %collective-permute-done.27.refs_1_ = bf16[4,32,512]{2,1,0:T(8,128)(2,1)S(1)} collective-permute-done((bf16[4,32,512]{2,1,0:T(8,128)(2,1)S(1)}, bf16[4,32,512]{2,1,0:T(8,128)(2,1)S(1)}, u32[]{:S(2)}, u32[]{:S(2)}) %collective-permute-start.27) | collective-permute-done | bytes 131104 | tf_op jit(solution)/shard_map/ppermute | solution.py:41
  195.3 3.6 %collective-permute-start.38 = (bf16[192,512]{1,0:T(8,128)(2,1)S(1)}, bf16[192,512]{1,0:T(8,128)(2,1)S(1)}, u32[]{:S(2)}, u32[]{:S(2)}) collective-permute-start(bf16[192,512]{1,0:T(8,128)(2,1)S(1)} %get-tuple-element.132), channel_id=1, source_target_pairs={{0,24},{8,16},{16,8},{24,0},{1,25},{9,17},{17,9},{25,1},{2,26},{10... | collective-permute-start | bytes 589832 | tf_op jit(solution)/shard_map/ppermute | solution.py:41
  199.6 4.2 %collective-permute-done.29.refs_3_ = bf16[4,32,512]{2,1,0:T(8,128)(2,1)S(1)} collective-permute-done((bf16[4,32,512]{2,1,0:T(8,128)(2,1)S(1)}, bf16[4,32,512]{2,1,0:T(8,128)(2,1)S(1)}, u32[]{:S(2)}, u32[]{:S(2)}) %collective-permute-start.29) | collective-permute-done | bytes 131104 | tf_op jit(solution)/shard_map/ppermute | solution.py:41
  204.8 2.3 %collective-permute-start.31 = (bf16[32,512]{1,0:T(8,128)(2,1)S(1)}, bf16[32,512]{1,0:T(8,128)(2,1)S(1)}, u32[]{:S(2)}, u32[]{:S(2)}) collective-permute-start(bf16[32,512]{1,0:T(8,128)(2,1)S(1)} %get-tuple-element.123), channel_id=1, source_target_pairs={{0,64},{32,96},{64,0},{96,32},{1,65},{33,97},{65,1},{97,33},{2,66}... | collective-permute-start | bytes 98312 | tf_op jit(solution)/shard_map/ppermute | solution.py:41
  207.1 2.2 %collective-permute-start.32 = (bf16[32,512]{1,0:T(8,128)(2,1)S(1)}, bf16[32,512]{1,0:T(8,128)(2,1)S(1)}, u32[]{:S(2)}, u32[]{:S(2)}) collective-permute-start(bf16[32,512]{1,0:T(8,128)(2,1)S(1)} %get-tuple-element.124), channel_id=1, source_target_pairs={{0,96},{32,64},{64,32},{96,0},{1,97},{33,65},{65,33},{97,1},{2,98}... | collective-permute-start | bytes 98312 | tf_op jit(solution)/shard_map/ppermute | solution.py:41
  209.2 1.6 close.1.refs_4_
  210.9 1.3 collective-permute-done.32.refs_3_
  212.2 1.3 final.1
  (74 shorter events, 16.2 us)
Async XLA Ops:
  4.4 5.5 %copy-start.3 = (bf16[2,128,512]{2,1,0:T(8,128)(2,1)S(1)}, bf16[2,128,512]{2,1,0:T(8,128)(2,1)}, u32[]{:S(2)}) copy-start(bf16[2,128,512]{2,1,0:T(8,128)(2,1)} %act.5) | copy-start | bytes 786436
  6.3 18.4 %collective-permute-start = (bf16[7,2,192,128]{3,2,1,0:T(8,128)(2,1)S(1)}, bf16[7,2,192,128]{3,2,1,0:T(8,128)(2,1)S(1)}, u32[]{:S(2)}, u32[]{:S(2)}) collective-permute-start(bf16[7,2,192,128]{3,2,1,0:T(8,128)(2,1)S(1)} %get-tuple-element.78), channel_id=1, source_target_pairs={{0,2},{2,0},{4,6},{6,4},{1,3},{3,1},{5,7},{7,5},{8,10},{10,8},{12,... | collective-permute-start | bytes 2064392 | tf_op jit(solution)/shard_map/ppermute | solution.py:41
  6.8 32.7 %collective-permute-start.1 = (bf16[7,2,192,128]{3,2,1,0:T(8,128)(2,1)S(1)}, bf16[7,2,192,128]{3,2,1,0:T(8,128)(2,1)S(1)}, u32[]{:S(2)}, u32[]{:S(2)}) collective-permute-start(bf16[7,2,192,128]{3,2,1,0:T(8,128)(2,1)S(1)} %get-tuple-element.79), channel_id=1, source_target_pairs={{0,4},{2,6},{4,0},{6,2},{1,5},{3,7},{5,1},{7,3},{8,12},{10,14},{12... | collective-permute-start | bytes 2064392 | tf_op jit(solution)/shard_map/ppermute | solution.py:41
  9.5 31.6 %collective-permute-start.2 = (bf16[7,2,192,128]{3,2,1,0:T(8,128)(2,1)S(1)}, bf16[7,2,192,128]{3,2,1,0:T(8,128)(2,1)S(1)}, u32[]{:S(2)}, u32[]{:S(2)}) collective-permute-start(bf16[7,2,192,128]{3,2,1,0:T(8,128)(2,1)S(1)} %get-tuple-element.80), channel_id=1, source_target_pairs={{0,6},{2,4},{4,2},{6,0},{1,7},{3,5},{5,3},{7,1},{8,14},{10,12},{12... | collective-permute-start | bytes 2064392 | tf_op jit(solution)/shard_map/ppermute | solution.py:41
  11.8 33.2 %collective-permute-start.3 = (bf16[7,4,96,128]{3,2,1,0:T(8,128)(2,1)S(1)}, bf16[7,4,96,128]{3,2,1,0:T(8,128)(2,1)S(1)}, u32[]{:S(2)}, u32[]{:S(2)}) collective-permute-start(bf16[7,4,96,128]{3,2,1,0:T(8,128)(2,1)S(1)} %get-tuple-element.84), channel_id=1, source_target_pairs={{0,16},{8,24},{16,0},{24,8},{1,17},{9,25},{17,1},{25,9},{2,18},{10... | collective-permute-start | bytes 2064392 | tf_op jit(solution)/shard_map/ppermute | solution.py:41
  13.8 32.7 %collective-permute-start.4 = (bf16[7,4,96,128]{3,2,1,0:T(8,128)(2,1)S(1)}, bf16[7,4,96,128]{3,2,1,0:T(8,128)(2,1)S(1)}, u32[]{:S(2)}, u32[]{:S(2)}) collective-permute-start(bf16[7,4,96,128]{3,2,1,0:T(8,128)(2,1)S(1)} %get-tuple-element.85), channel_id=1, source_target_pairs={{0,8},{8,0},{16,24},{24,16},{1,9},{9,1},{17,25},{25,17},{2,10},{10... | collective-permute-start | bytes 2064392 | tf_op jit(solution)/shard_map/ppermute | solution.py:41
  24.7 32.2 %collective-permute-start.5 = (bf16[7,4,96,128]{3,2,1,0:T(8,128)(2,1)S(1)}, bf16[7,4,96,128]{3,2,1,0:T(8,128)(2,1)S(1)}, u32[]{:S(2)}, u32[]{:S(2)}) collective-permute-start(bf16[7,4,96,128]{3,2,1,0:T(8,128)(2,1)S(1)} %get-tuple-element.86), channel_id=1, source_target_pairs={{0,24},{8,16},{16,8},{24,0},{1,25},{9,17},{17,9},{25,1},{2,26},{10... | collective-permute-start | bytes 2064392 | tf_op jit(solution)/shard_map/ppermute | solution.py:41
  39.5 3.0 %collective-permute-start.9 = (bf16[4,2,192,128]{3,2,1,0:T(8,128)(2,1)S(1)}, bf16[4,2,192,128]{3,2,1,0:T(8,128)(2,1)S(1)}, u32[]{:S(2)}, u32[]{:S(2)}) collective-permute-start(bf16[4,2,192,128]{3,2,1,0:T(8,128)(2,1)S(1)} %get-tuple-element.94), channel_id=1, source_target_pairs={{0,1},{1,0},{2,3},{3,2},{4,5},{5,4},{6,7},{7,6},{8,9},{9,8},{10,11... | collective-permute-start | bytes 1179656 | tf_op jit(solution)/shard_map/ppermute | solution.py:41
  41.9 48.2 %collective-permute-start.13 = (bf16[4,3,2,192,128]{4,3,2,1,0:T(8,128)(2,1)S(1)}, bf16[4,3,2,192,128]{4,3,2,1,0:T(8,128)(2,1)S(1)}, u32[]{:S(2)}, u32[]{:S(2)}) collective-permute-start(bf16[4,3,2,192,128]{4,3,2,1,0:T(8,128)(2,1)S(1)} %get-tuple-element.98), channel_id=1, source_target_pairs={{0,1},{1,0},{2,3},{3,2},{4,5},{5,4},{6,7},{7,6},{8,9},{9,8},{10,11... | collective-permute-start | bytes 3538952 | tf_op jit(solution)/shard_map/ppermute | solution.py:41
  42.5 21.8 %collective-permute-start.10 = (bf16[4,2,192,128]{3,2,1,0:T(8,128)(2,1)S(1)}, bf16[4,2,192,128]{3,2,1,0:T(8,128)(2,1)S(1)}, u32[]{:S(2)}, u32[]{:S(2)}) collective-permute-start(bf16[4,2,192,128]{3,2,1,0:T(8,128)(2,1)S(1)} %get-tuple-element.95), channel_id=1, source_target_pairs={{0,3},{1,2},{2,1},{3,0},{4,7},{5,6},{6,5},{7,4},{8,11},{9,10},{10,... | collective-permute-start | bytes 1179656 | tf_op jit(solution)/shard_map/ppermute | solution.py:41
  45.0 19.4 %collective-permute-start.6 = (bf16[8,2,4,32,128]{4,3,2,1,0:T(8,128)(2,1)S(1)}, bf16[8,2,4,32,128]{4,3,2,1,0:T(8,128)(2,1)S(1)}, u32[]{:S(2)}, u32[]{:S(2)}) collective-permute-start(bf16[8,2,4,32,128]{4,3,2,1,0:T(8,128)(2,1)S(1)} %get-tuple-element.89), channel_id=1, source_target_pairs={{0,32},{32,0},{64,96},{96,64},{1,33},{33,1},{65,97},{97,65},{2,34}... | collective-permute-start | bytes 1572872 | tf_op jit(solution)/shard_map/ppermute | solution.py:41
  46.5 25.9 %collective-permute-start.7 = (bf16[8,2,4,32,128]{4,3,2,1,0:T(8,128)(2,1)S(1)}, bf16[8,2,4,32,128]{4,3,2,1,0:T(8,128)(2,1)S(1)}, u32[]{:S(2)}, u32[]{:S(2)}) collective-permute-start(bf16[8,2,4,32,128]{4,3,2,1,0:T(8,128)(2,1)S(1)} %get-tuple-element.90), channel_id=1, source_target_pairs={{0,64},{32,96},{64,0},{96,32},{1,65},{33,97},{65,1},{97,33},{2,66}... | collective-permute-start | bytes 1572872 | tf_op jit(solution)/shard_map/ppermute | solution.py:41
  57.0 23.8 %collective-permute-start.8 = (bf16[8,2,4,32,128]{4,3,2,1,0:T(8,128)(2,1)S(1)}, bf16[8,2,4,32,128]{4,3,2,1,0:T(8,128)(2,1)S(1)}, u32[]{:S(2)}, u32[]{:S(2)}) collective-permute-start(bf16[8,2,4,32,128]{4,3,2,1,0:T(8,128)(2,1)S(1)} %get-tuple-element.91), channel_id=1, source_target_pairs={{0,96},{32,64},{64,32},{96,0},{1,97},{33,65},{65,33},{97,1},{2,98}... | collective-permute-start | bytes 1572872 | tf_op jit(solution)/shard_map/ppermute | solution.py:41
  62.8 18.0 %copy-start.4 = (s32[8]{0:T(128)S(1)}, s32[8]{0:T(128)}, u32[]{:S(2)}) copy-start(s32[8]{0:T(128)} %param.5) | copy-start | bytes 100
  64.3 48.1 %collective-permute-start.18 = (bf16[4,3,4,96,128]{4,3,2,1,0:T(8,128)(2,1)S(1)}, bf16[4,3,4,96,128]{4,3,2,1,0:T(8,128)(2,1)S(1)}, u32[]{:S(2)}, u32[]{:S(2)}) collective-permute-start(bf16[4,3,4,96,128]{4,3,2,1,0:T(8,128)(2,1)S(1)} %get-tuple-element.105), channel_id=1, source_target_pairs={{0,1},{1,0},{2,3},{3,2},{4,5},{5,4},{6,7},{7,6},{8,9},{9,8},{10,11... | collective-permute-start | bytes 3538952 | tf_op jit(solution)/shard_map/ppermute | solution.py:41
  64.4 20.8 %collective-permute-start.11 = (bf16[4,2,192,128]{3,2,1,0:T(8,128)(2,1)S(1)}, bf16[4,2,192,128]{3,2,1,0:T(8,128)(2,1)S(1)}, u32[]{:S(2)}, u32[]{:S(2)}) collective-permute-start(bf16[4,2,192,128]{3,2,1,0:T(8,128)(2,1)S(1)} %get-tuple-element.96), channel_id=1, source_target_pairs={{0,5},{1,4},{2,7},{3,6},{4,1},{5,0},{6,3},{7,2},{8,13},{9,12},{10,... | collective-permute-start | bytes 1179656 | tf_op jit(solution)/shard_map/ppermute | solution.py:41
  72.4 13.4 %collective-permute-start.12 = (bf16[4,2,192,128]{3,2,1,0:T(8,128)(2,1)S(1)}, bf16[4,2,192,128]{3,2,1,0:T(8,128)(2,1)S(1)}, u32[]{:S(2)}, u32[]{:S(2)}) collective-permute-start(bf16[4,2,192,128]{3,2,1,0:T(8,128)(2,1)S(1)} %get-tuple-element.97), channel_id=1, source_target_pairs={{0,7},{1,6},{2,5},{3,4},{4,3},{5,2},{6,1},{7,0},{8,15},{9,14},{10,... | collective-permute-start | bytes 1179656 | tf_op jit(solution)/shard_map/ppermute | solution.py:41
  80.8 9.3 %collective-permute-start.14 = (bf16[4,4,96,128]{3,2,1,0:T(8,128)(2,1)S(1)}, bf16[4,4,96,128]{3,2,1,0:T(8,128)(2,1)S(1)}, u32[]{:S(2)}, u32[]{:S(2)}) collective-permute-start(bf16[4,4,96,128]{3,2,1,0:T(8,128)(2,1)S(1)} %get-tuple-element.101), channel_id=1, source_target_pairs={{0,1},{1,0},{2,3},{3,2},{4,5},{5,4},{6,7},{7,6},{8,9},{9,8},{10,11... | collective-permute-start | bytes 1179656 | tf_op jit(solution)/shard_map/ppermute | solution.py:41
  85.2 12.1 %collective-permute-start.15 = (bf16[4,4,96,128]{3,2,1,0:T(8,128)(2,1)S(1)}, bf16[4,4,96,128]{3,2,1,0:T(8,128)(2,1)S(1)}, u32[]{:S(2)}, u32[]{:S(2)}) collective-permute-start(bf16[4,4,96,128]{3,2,1,0:T(8,128)(2,1)S(1)} %get-tuple-element.102), channel_id=1, source_target_pairs={{0,17},{1,16},{8,25},{9,24},{16,1},{17,0},{24,9},{25,8},{2,19},{3,... | collective-permute-start | bytes 1179656 | tf_op jit(solution)/shard_map/ppermute | solution.py:41
  85.8 21.8 %collective-permute-start.16 = (bf16[4,4,96,128]{3,2,1,0:T(8,128)(2,1)S(1)}, bf16[4,4,96,128]{3,2,1,0:T(8,128)(2,1)S(1)}, u32[]{:S(2)}, u32[]{:S(2)}) collective-permute-start(bf16[4,4,96,128]{3,2,1,0:T(8,128)(2,1)S(1)} %get-tuple-element.103), channel_id=1, source_target_pairs={{0,9},{1,8},{8,1},{9,0},{16,25},{17,24},{24,17},{25,16},{2,11},{3,... | collective-permute-start | bytes 1179656 | tf_op jit(solution)/shard_map/ppermute | solution.py:41
  90.1 20.4 %collective-permute-start.17 = (bf16[4,4,96,128]{3,2,1,0:T(8,128)(2,1)S(1)}, bf16[4,4,96,128]{3,2,1,0:T(8,128)(2,1)S(1)}, u32[]{:S(2)}, u32[]{:S(2)}) collective-permute-start(bf16[4,4,96,128]{3,2,1,0:T(8,128)(2,1)S(1)} %get-tuple-element.104), channel_id=1, source_target_pairs={{0,25},{1,24},{8,17},{9,16},{16,9},{17,8},{24,1},{25,0},{2,27},{3,... | collective-permute-start | bytes 1179656 | tf_op jit(solution)/shard_map/ppermute | solution.py:41
  90.1 37.5 %collective-permute-start.23 = (bf16[4,4,2,4,32,128]{5,4,3,2,1,0:T(8,128)(2,1)S(1)}, bf16[4,4,2,4,32,128]{5,4,3,2,1,0:T(8,128)(2,1)S(1)}, u32[]{:S(2)}, u32[]{:S(2)}) collective-permute-start(bf16[4,4,2,4,32,128]{5,4,3,2,1,0:T(8,128)(2,1)S(1)} %get-tuple-element.112), channel_id=1, source_target_pairs={{0,1},{1,0},{2,3},{3,2},{4,5},{5,4},{6,7},{7,6},{8,9},{9,8},{10,11... | collective-permute-start | bytes 3145736 | tf_op jit(solution)/shard_map/ppermute | solution.py:41
  97.3 22.4 %collective-permute-start.19 = (bf16[4,2,4,32,128]{4,3,2,1,0:T(8,128)(2,1)S(1)}, bf16[4,2,4,32,128]{4,3,2,1,0:T(8,128)(2,1)S(1)}, u32[]{:S(2)}, u32[]{:S(2)}) collective-permute-start(bf16[4,2,4,32,128]{4,3,2,1,0:T(8,128)(2,1)S(1)} %get-tuple-element.108), channel_id=1, source_target_pairs={{0,1},{1,0},{2,3},{3,2},{4,5},{5,4},{6,7},{7,6},{8,9},{9,8},{10,11... | collective-permute-start | bytes 786440 | tf_op jit(solution)/shard_map/ppermute | solution.py:41
  107.6 12.9 %collective-permute-start.20 = (bf16[4,2,4,32,128]{4,3,2,1,0:T(8,128)(2,1)S(1)}, bf16[4,2,4,32,128]{4,3,2,1,0:T(8,128)(2,1)S(1)}, u32[]{:S(2)}, u32[]{:S(2)}) collective-permute-start(bf16[4,2,4,32,128]{4,3,2,1,0:T(8,128)(2,1)S(1)} %get-tuple-element.109), channel_id=1, source_target_pairs={{0,33},{1,32},{32,1},{33,0},{64,97},{65,96},{96,65},{97,64},{2,35}... | collective-permute-start | bytes 786440 | tf_op jit(solution)/shard_map/ppermute | solution.py:41
  110.4 13.0 %collective-permute-start.21 = (bf16[4,2,4,32,128]{4,3,2,1,0:T(8,128)(2,1)S(1)}, bf16[4,2,4,32,128]{4,3,2,1,0:T(8,128)(2,1)S(1)}, u32[]{:S(2)}, u32[]{:S(2)}) collective-permute-start(bf16[4,2,4,32,128]{4,3,2,1,0:T(8,128)(2,1)S(1)} %get-tuple-element.110), channel_id=1, source_target_pairs={{0,65},{1,64},{32,97},{33,96},{64,1},{65,0},{96,33},{97,32},{2,67}... | collective-permute-start | bytes 786440 | tf_op jit(solution)/shard_map/ppermute | solution.py:41
  112.4 15.2 %collective-permute-start.22 = (bf16[4,2,4,32,128]{4,3,2,1,0:T(8,128)(2,1)S(1)}, bf16[4,2,4,32,128]{4,3,2,1,0:T(8,128)(2,1)S(1)}, u32[]{:S(2)}, u32[]{:S(2)}) collective-permute-start(bf16[4,2,4,32,128]{4,3,2,1,0:T(8,128)(2,1)S(1)} %get-tuple-element.111), channel_id=1, source_target_pairs={{0,97},{1,96},{32,65},{33,64},{64,33},{65,32},{96,1},{97,0},{2,99}... | collective-permute-start | bytes 786440 | tf_op jit(solution)/shard_map/ppermute | solution.py:41
  119.7 28.3 %collective-permute-start.39 = (bf16[8,96,512]{2,1,0:T(8,128)(2,1)S(1)}, bf16[8,96,512]{2,1,0:T(8,128)(2,1)S(1)}, u32[]{:S(2)}, u32[]{:S(2)}) collective-permute-start(bf16[8,96,512]{2,1,0:T(8,128)(2,1)S(1)} %get-tuple-element.134), channel_id=1, source_target_pairs={{0,2},{2,0},{4,6},{6,4},{1,3},{3,1},{5,7},{7,5},{8,10},{10,8},{12,... | collective-permute-start | bytes 2359304 | tf_op jit(solution)/shard_map/ppermute | solution.py:41
  120.5 37.0 %collective-permute-start.40 = (bf16[8,96,512]{2,1,0:T(8,128)(2,1)S(1)}, bf16[8,96,512]{2,1,0:T(8,128)(2,1)S(1)}, u32[]{:S(2)}, u32[]{:S(2)}) collective-permute-start(bf16[8,96,512]{2,1,0:T(8,128)(2,1)S(1)} %get-tuple-element.135), channel_id=1, source_target_pairs={{0,4},{2,6},{4,0},{6,2},{1,5},{3,7},{5,1},{7,3},{8,12},{10,14},{12... | collective-permute-start | bytes 2359304 | tf_op jit(solution)/shard_map/ppermute | solution.py:41
  123.4 36.8 %collective-permute-start.41 = (bf16[8,96,512]{2,1,0:T(8,128)(2,1)S(1)}, bf16[8,96,512]{2,1,0:T(8,128)(2,1)S(1)}, u32[]{:S(2)}, u32[]{:S(2)}) collective-permute-start(bf16[8,96,512]{2,1,0:T(8,128)(2,1)S(1)} %get-tuple-element.136), channel_id=1, source_target_pairs={{0,6},{2,4},{4,2},{6,0},{1,7},{3,5},{5,3},{7,1},{8,14},{10,12},{12... | collective-permute-start | bytes 2359304 | tf_op jit(solution)/shard_map/ppermute | solution.py:41
  133.3 14.0 %collective-permute-start.24 = (bf16[4,128,512]{2,1,0:T(8,128)(2,1)S(1)}, bf16[4,128,512]{2,1,0:T(8,128)(2,1)S(1)}, u32[]{:S(2)}, u32[]{:S(2)}) collective-permute-start(bf16[4,128,512]{2,1,0:T(8,128)(2,1)S(1)} %get-tuple-element.114), channel_id=1, source_target_pairs={{0,16},{8,24},{16,0},{24,8},{1,17},{9,25},{17,1},{25,9},{2,18},{10... | collective-permute-start | bytes 1572872 | tf_op jit(solution)/shard_map/ppermute | solution.py:41
  133.4 52.0 %collective-permute-start.33 = (bf16[2,384,512]{2,1,0:T(8,128)(2,1)S(1)}, bf16[2,384,512]{2,1,0:T(8,128)(2,1)S(1)}, u32[]{:S(2)}, u32[]{:S(2)}) collective-permute-start(bf16[2,384,512]{2,1,0:T(8,128)(2,1)S(1)} %get-tuple-element.126), channel_id=1, source_target_pairs={{0,32},{32,0},{64,96},{96,64},{1,33},{33,1},{65,97},{97,65},{2,34}... | collective-permute-start | bytes 2359304 | tf_op jit(solution)/shard_map/ppermute | solution.py:41
  147.3 40.4 %collective-permute-start.34 = (bf16[2,384,512]{2,1,0:T(8,128)(2,1)S(1)}, bf16[2,384,512]{2,1,0:T(8,128)(2,1)S(1)}, u32[]{:S(2)}, u32[]{:S(2)}) collective-permute-start(bf16[2,384,512]{2,1,0:T(8,128)(2,1)S(1)} %get-tuple-element.127), channel_id=1, source_target_pairs={{0,64},{32,96},{64,0},{96,32},{1,65},{33,97},{65,1},{97,33},{2,66}... | collective-permute-start | bytes 2359304 | tf_op jit(solution)/shard_map/ppermute | solution.py:41
  148.1 41.7 %collective-permute-start.35 = (bf16[2,384,512]{2,1,0:T(8,128)(2,1)S(1)}, bf16[2,384,512]{2,1,0:T(8,128)(2,1)S(1)}, u32[]{:S(2)}, u32[]{:S(2)}) collective-permute-start(bf16[2,384,512]{2,1,0:T(8,128)(2,1)S(1)} %get-tuple-element.128), channel_id=1, source_target_pairs={{0,96},{32,64},{64,32},{96,0},{1,97},{33,65},{65,33},{97,1},{2,98}... | collective-permute-start | bytes 2359304 | tf_op jit(solution)/shard_map/ppermute | solution.py:41
  157.5 15.0 %collective-permute-start.25 = (bf16[4,128,512]{2,1,0:T(8,128)(2,1)S(1)}, bf16[4,128,512]{2,1,0:T(8,128)(2,1)S(1)}, u32[]{:S(2)}, u32[]{:S(2)}) collective-permute-start(bf16[4,128,512]{2,1,0:T(8,128)(2,1)S(1)} %get-tuple-element.115), channel_id=1, source_target_pairs={{0,8},{8,0},{16,24},{24,16},{1,9},{9,1},{17,25},{25,17},{2,10},{10... | collective-permute-start | bytes 1572872 | tf_op jit(solution)/shard_map/ppermute | solution.py:41
  160.2 23.5 %collective-permute-start.26 = (bf16[4,128,512]{2,1,0:T(8,128)(2,1)S(1)}, bf16[4,128,512]{2,1,0:T(8,128)(2,1)S(1)}, u32[]{:S(2)}, u32[]{:S(2)}) collective-permute-start(bf16[4,128,512]{2,1,0:T(8,128)(2,1)S(1)} %get-tuple-element.116), channel_id=1, source_target_pairs={{0,24},{8,16},{16,8},{24,0},{1,25},{9,17},{17,9},{25,1},{2,26},{10... | collective-permute-start | bytes 1572872 | tf_op jit(solution)/shard_map/ppermute | solution.py:41
  172.5 21.6 %collective-permute-start.42 = (bf16[2,96,512]{2,1,0:T(8,128)(2,1)S(1)}, bf16[2,96,512]{2,1,0:T(8,128)(2,1)S(1)}, u32[]{:S(2)}, u32[]{:S(2)}) collective-permute-start(bf16[2,96,512]{2,1,0:T(8,128)(2,1)S(1)} %get-tuple-element.138), channel_id=1, source_target_pairs={{0,32},{32,0},{64,96},{96,64},{1,33},{33,1},{65,97},{97,65},{2,34}... | collective-permute-start | bytes 589832 | tf_op jit(solution)/shard_map/ppermute | solution.py:41
  183.7 11.6 %collective-permute-start.43 = (bf16[2,96,512]{2,1,0:T(8,128)(2,1)S(1)}, bf16[2,96,512]{2,1,0:T(8,128)(2,1)S(1)}, u32[]{:S(2)}, u32[]{:S(2)}) collective-permute-start(bf16[2,96,512]{2,1,0:T(8,128)(2,1)S(1)} %get-tuple-element.139), channel_id=1, source_target_pairs={{0,64},{32,96},{64,0},{96,32},{1,65},{33,97},{65,1},{97,33},{2,66}... | collective-permute-start | bytes 589832 | tf_op jit(solution)/shard_map/ppermute | solution.py:41
  185.4 13.4 %collective-permute-start.44 = (bf16[2,96,512]{2,1,0:T(8,128)(2,1)S(1)}, bf16[2,96,512]{2,1,0:T(8,128)(2,1)S(1)}, u32[]{:S(2)}, u32[]{:S(2)}) collective-permute-start(bf16[2,96,512]{2,1,0:T(8,128)(2,1)S(1)} %get-tuple-element.140), channel_id=1, source_target_pairs={{0,96},{32,64},{64,32},{96,0},{1,97},{33,65},{65,33},{97,1},{2,98}... | collective-permute-start | bytes 589832 | tf_op jit(solution)/shard_map/ppermute | solution.py:41
  187.7 6.5 %collective-permute-start.27 = (bf16[4,32,512]{2,1,0:T(8,128)(2,1)S(1)}, bf16[4,32,512]{2,1,0:T(8,128)(2,1)S(1)}, u32[]{:S(2)}, u32[]{:S(2)}) collective-permute-start(bf16[4,32,512]{2,1,0:T(8,128)(2,1)S(1)} %get-tuple-element.118), channel_id=1, source_target_pairs={{0,2},{2,0},{4,6},{6,4},{1,3},{3,1},{5,7},{7,5},{8,10},{10,8},{12,... | collective-permute-start | bytes 393224 | tf_op jit(solution)/shard_map/ppermute | solution.py:41
  189.7 9.8 %collective-permute-start.28 = (bf16[4,32,512]{2,1,0:T(8,128)(2,1)S(1)}, bf16[4,32,512]{2,1,0:T(8,128)(2,1)S(1)}, u32[]{:S(2)}, u32[]{:S(2)}) collective-permute-start(bf16[4,32,512]{2,1,0:T(8,128)(2,1)S(1)} %get-tuple-element.119), channel_id=1, source_target_pairs={{0,4},{2,6},{4,0},{6,2},{1,5},{3,7},{5,1},{7,3},{8,12},{10,14},{12... | collective-permute-start | bytes 393224 | tf_op jit(solution)/shard_map/ppermute | solution.py:41
  194.2 10.6 %collective-permute-start.36 = (bf16[192,512]{1,0:T(8,128)(2,1)S(1)}, bf16[192,512]{1,0:T(8,128)(2,1)S(1)}, u32[]{:S(2)}, u32[]{:S(2)}) collective-permute-start(bf16[192,512]{1,0:T(8,128)(2,1)S(1)} %get-tuple-element.130), channel_id=1, source_target_pairs={{0,16},{8,24},{16,0},{24,8},{1,17},{9,25},{17,1},{25,9},{2,18},{10... | collective-permute-start | bytes 589832 | tf_op jit(solution)/shard_map/ppermute | solution.py:41
  194.2 12.9 %collective-permute-start.37 = (bf16[192,512]{1,0:T(8,128)(2,1)S(1)}, bf16[192,512]{1,0:T(8,128)(2,1)S(1)}, u32[]{:S(2)}, u32[]{:S(2)}) collective-permute-start(bf16[192,512]{1,0:T(8,128)(2,1)S(1)} %get-tuple-element.131), channel_id=1, source_target_pairs={{0,8},{8,0},{16,24},{24,16},{1,9},{9,1},{17,25},{25,17},{2,10},{10... | collective-permute-start | bytes 589832 | tf_op jit(solution)/shard_map/ppermute | solution.py:41
  195.3 14.0 %collective-permute-start.38 = (bf16[192,512]{1,0:T(8,128)(2,1)S(1)}, bf16[192,512]{1,0:T(8,128)(2,1)S(1)}, u32[]{:S(2)}, u32[]{:S(2)}) collective-permute-start(bf16[192,512]{1,0:T(8,128)(2,1)S(1)} %get-tuple-element.132), channel_id=1, source_target_pairs={{0,24},{8,16},{16,8},{24,0},{1,25},{9,17},{17,9},{25,1},{2,26},{10... | collective-permute-start | bytes 589832 | tf_op jit(solution)/shard_map/ppermute | solution.py:41
  198.9 5.0 %collective-permute-start.29 = (bf16[4,32,512]{2,1,0:T(8,128)(2,1)S(1)}, bf16[4,32,512]{2,1,0:T(8,128)(2,1)S(1)}, u32[]{:S(2)}, u32[]{:S(2)}) collective-permute-start(bf16[4,32,512]{2,1,0:T(8,128)(2,1)S(1)} %get-tuple-element.120), channel_id=1, source_target_pairs={{0,6},{2,4},{4,2},{6,0},{1,7},{3,5},{5,3},{7,1},{8,14},{10,12},{12... | collective-permute-start | bytes 393224 | tf_op jit(solution)/shard_map/ppermute | solution.py:41
  199.5 9.7 %collective-permute-start.45 = (bf16[96,512]{1,0:T(8,128)(2,1)S(1)}, bf16[96,512]{1,0:T(8,128)(2,1)S(1)}, u32[]{:S(2)}, u32[]{:S(2)}) collective-permute-start(bf16[96,512]{1,0:T(8,128)(2,1)S(1)} %get-tuple-element.142), channel_id=1, source_target_pairs={{0,16},{8,24},{16,0},{24,8},{1,17},{9,25},{17,1},{25,9},{2,18},{10... | collective-permute-start | bytes 294920 | tf_op jit(solution)/shard_map/ppermute | solution.py:41
  204.4 6.4 %collective-permute-start.30 = (bf16[32,512]{1,0:T(8,128)(2,1)S(1)}, bf16[32,512]{1,0:T(8,128)(2,1)S(1)}, u32[]{:S(2)}, u32[]{:S(2)}) collective-permute-start(bf16[32,512]{1,0:T(8,128)(2,1)S(1)} %get-tuple-element.122), channel_id=1, source_target_pairs={{0,32},{32,0},{64,96},{96,64},{1,33},{33,1},{65,97},{97,65},{2,34}... | collective-permute-start | bytes 98312 | tf_op jit(solution)/shard_map/ppermute | solution.py:41
  204.8 6.1 %collective-permute-start.31 = (bf16[32,512]{1,0:T(8,128)(2,1)S(1)}, bf16[32,512]{1,0:T(8,128)(2,1)S(1)}, u32[]{:S(2)}, u32[]{:S(2)}) collective-permute-start(bf16[32,512]{1,0:T(8,128)(2,1)S(1)} %get-tuple-element.123), channel_id=1, source_target_pairs={{0,64},{32,96},{64,0},{96,32},{1,65},{33,97},{65,1},{97,33},{2,66}... | collective-permute-start | bytes 98312 | tf_op jit(solution)/shard_map/ppermute | solution.py:41
  207.1 5.1 %collective-permute-start.32 = (bf16[32,512]{1,0:T(8,128)(2,1)S(1)}, bf16[32,512]{1,0:T(8,128)(2,1)S(1)}, u32[]{:S(2)}, u32[]{:S(2)}) collective-permute-start(bf16[32,512]{1,0:T(8,128)(2,1)S(1)} %get-tuple-element.124), channel_id=1, source_target_pairs={{0,96},{32,64},{64,32},{96,0},{1,97},{33,65},{65,33},{97,1},{2,98}... | collective-permute-start | bytes 98312 | tf_op jit(solution)/shard_map/ppermute | solution.py:41
  (3 other events, 9.8 us)

commit v3 on v2

--- a/solution.py
+++ b/solution.py
@@ -295,7 +295,11 @@
 
 
 def exchange(parts, axis):
-    return [parts[0]] + [flip(parts[d], axis, d) for d in range(1, len(parts))]
+    arrived = {0: parts[0]}
+    for d in (2, 1, 3):
+        if d < len(parts):
+            arrived[d] = flip(parts[d], axis, d)
+    return [arrived[d] for d in range(len(parts))]
 
 
 def close_kernel(where, *refs):
@@ -330,7 +334,8 @@
     for family in FAMILIES:
         sent, order = pack(family, view, activation, order)
         same = exchange(sent[:4], family)
-        pieces[family] = same + [flip(sent[4 + d], family, d, 1) for d in range(4)]
+        cross = {d: flip(sent[4 + d], family, d, 1) for d in (2, 1, 3, 0)}
+        pieces[family] = same + [cross[d] for d in range(4)]
     order, shared = order[:1], {}
 
     def share(family, order):
@@ -346,9 +351,10 @@
         return order
 
     order = early(FAMILIES[0], share(FAMILIES[0], order))
-    order = share(FAMILIES[2], share(FAMILIES[1], order))
-    order = early(FAMILIES[1], order)
+    order = early(FAMILIES[1], share(FAMILIES[1], order))
     for family in FAMILIES:
+        if family == FAMILIES[2]:
+            order = share(family, order)
         parts[family], order = product(
             family, pieces[family], shared[family], where, factors, order, begun[family]
         )

time: 216 us -> 248 us (1.15)
  waiting for transfers between devices: 111 us -> 137 us
  starting transfers between devices: 57.7 us -> 62.1 us
    ppermute x46, waiting for transfers between devices: 111 us -> 137 us  [flip(): return lax.ppermute(value, tuple(over), pairs)]
    ppermute x46, starting transfers between devices: 57.7 us -> 62.1 us  [flip(): return lax.ppermute(value, tuple(over), pairs)]
  transfers between devices with their start and end apart: 46 -> 46, of which waited for: 19 -> 21; matrix products, arithmetic and copies ran while one was open for 0% -> 0% of each run, Pallas kernels for 17% -> 15%
where the time goes in v3:
time: 248 us; the launch traced here: 244 us
  waiting for transfers between devices  137 us (55%)
  starting transfers between devices  62.1 us (25%)
  Pallas kernels  40.4 us (16%)
  local copies, waits for them, and re-layouts  4.43 us (2%)
    ppermute x46, waiting for transfers between devices, flip(): return lax.ppermute(value, tuple(over), pairs)  137 us
    ppermute x46, starting transfers between devices, flip(): return lax.ppermute(value, tuple(over), pairs)  62.1 us
    pallas_call x3, Pallas kernels, product(): pl.pallas_call(functools.partial(product_kernel, family), out_shape=[jax....  18.5 us
    pallas_call x2, Pallas kernels, begin(): pl.pallas_call(functools.partial(begin_kernel, family), out_shape=[jax.Sh...  6.19 us
    pallas_call x3, Pallas kernels, pack(): pl.pallas_call(functools.partial(pack_kernel, family), out_shape=shapes +...  5.36 us
  transfers between devices with their start and end apart: 46, of which 21 were waited for; matrix products, arithmetic and copies ran while one was open for 0% of the time, Pallas kernels for 15%

profile of v3, /device:TPU:8, one launch (start us, length us, event | category | flops | bytes accessed | tf_op | source)
XLA Modules:
  0.0 244.3 jit_solution(9188424577642236318)
XLA Ops:
  0.1 3.4 %copy-done = bf16[4,8192,128]{2,1,0:T(8,128)(2,1)S(1)} copy-done((bf16[4,8192,128]{2,1,0:T(8,128)(2,1)S(1)}, bf16[4,8192,128]{2,1,0:T(8,128)(2,1)}, u32[]{:S(2)}) %copy-start) | copy-done | bytes 8388632
  4.4 1.9 shard_map.37
  6.8 2.7 %collective-permute-start.1 = (bf16[7,2,192,128]{3,2,1,0:T(8,128)(2,1)S(1)}, bf16[7,2,192,128]{3,2,1,0:T(8,128)(2,1)S(1)}, u32[]{:S(2)}, u32[]{:S(2)}) collective-permute-start(bf16[7,2,192,128]{3,2,1,0:T(8,128)(2,1)S(1)} %get-tuple-element.79), channel_id=1, source_target_pairs={{0,4},{2,6},{4,0},{6,2},{1,5},{3,7},{5,1},{7,3},{8,12},{10,14},{12... | collective-permute-start | bytes 2064392 | tf_op jit(solution)/shard_map/ppermute | solution.py:41
  9.9 1.9 shard_map.38
  11.8 2.0 collective-permute-start.3
  13.8 3.6 %collective-permute-start.4 = (bf16[7,4,96,128]{3,2,1,0:T(8,128)(2,1)S(1)}, bf16[7,4,96,128]{3,2,1,0:T(8,128)(2,1)S(1)}, u32[]{:S(2)}, u32[]{:S(2)}) collective-permute-start(bf16[7,4,96,128]{3,2,1,0:T(8,128)(2,1)S(1)} %get-tuple-element.85), channel_id=1, source_target_pairs={{0,8},{8,0},{16,24},{24,16},{1,9},{9,1},{17,25},{25,17},{2,10},{10... | collective-permute-start | bytes 2064392 | tf_op jit(solution)/shard_map/ppermute | solution.py:41
  17.4 7.3 %collective-permute-done.refs_1_ = bf16[7,2,192,128]{3,2,1,0:T(8,128)(2,1)S(1)} collective-permute-done((bf16[7,2,192,128]{3,2,1,0:T(8,128)(2,1)S(1)}, bf16[7,2,192,128]{3,2,1,0:T(8,128)(2,1)S(1)}, u32[]{:S(2)}, u32[]{:S(2)}) %collective-permute-start) | collective-permute-done | bytes 688160 | tf_op jit(solution)/shard_map/ppermute | solution.py:41
  24.7 4.0 %collective-permute-start.5 = (bf16[7,4,96,128]{3,2,1,0:T(8,128)(2,1)S(1)}, bf16[7,4,96,128]{3,2,1,0:T(8,128)(2,1)S(1)}, u32[]{:S(2)}, u32[]{:S(2)}) collective-permute-start(bf16[7,4,96,128]{3,2,1,0:T(8,128)(2,1)S(1)} %get-tuple-element.86), channel_id=1, source_target_pairs={{0,24},{8,16},{16,8},{24,0},{1,25},{9,17},{17,9},{25,1},{2,26},{10... | collective-permute-start | bytes 2064392 | tf_op jit(solution)/shard_map/ppermute | solution.py:41
  28.8 1.6 shard_map.39
  30.3 9.1 %collective-permute-done.1.refs_2_ = bf16[7,2,192,128]{3,2,1,0:T(8,128)(2,1)S(1)} collective-permute-done((bf16[7,2,192,128]{3,2,1,0:T(8,128)(2,1)S(1)}, bf16[7,2,192,128]{3,2,1,0:T(8,128)(2,1)S(1)}, u32[]{:S(2)}, u32[]{:S(2)}) %collective-permute-start.1) | collective-permute-done | bytes 688160 | tf_op jit(solution)/shard_map/ppermute | solution.py:41
  42.3 3.1 %shard_map.41 = (f32[4,384,1024]{2,1,0:T(8,128)S(1)}, s32[1]{0:T(128)}) custom-call(s32[5]{0:T(128)S(1)} %stack.23.where, s32[1]{0:T(128)} %get-tuple-element.81.order, bf16[7,384,128]{2,1,0:T(8,128)(2,1)S(1)} %bitcast.61, bf16[7,384,128]{2,1,0:T(8,128)(2,1)S(1)} %bitcast.62, bf16[7,384,128]{2,1,0:T(8,128)(2,1)S(1)} %bitcast.63, ...), custom_call_target="tpu_custom_call" | custom-call | flops 1610612736 | bytes 8388608 | tf_op jit(solution)/shard_map/pallas_call | solution.py:205
  46.5 10.4 %collective-permute-done.5.refs_3_ = bf16[7,4,96,128]{3,2,1,0:T(8,128)(2,1)S(1)} collective-permute-done((bf16[7,4,96,128]{3,2,1,0:T(8,128)(2,1)S(1)}, bf16[7,4,96,128]{3,2,1,0:T(8,128)(2,1)S(1)}, u32[]{:S(2)}, u32[]{:S(2)}) %collective-permute-start.5) | collective-permute-done | bytes 688160 | tf_op jit(solution)/shard_map/ppermute | solution.py:41
  59.1 2.3 collective-permute-start.8
  61.8 3.1 %shard_map.43 = (f32[4,384,1024]{2,1,0:T(8,128)S(1)}, s32[1]{0:T(128)}) custom-call(s32[5]{0:T(128)S(1)} %stack.23.where, s32[1]{0:T(128)} %get-tuple-element.87.order, bf16[7,384,128]{2,1,0:T(8,128)(2,1)S(1)} %bitcast.57, bf16[7,384,128]{2,1,0:T(8,128)(2,1)S(1)} %bitcast.58, bf16[7,384,128]{2,1,0:T(8,128)(2,1)S(1)} %bitcast.59, ...), custom_call_target="tpu_custom_call" | custom-call | flops 1610612736 | bytes 8388608 | tf_op jit(solution)/shard_map/pallas_call | solution.py:205
  64.9 4.5 %collective-permute-done.7 = bf16[4,2,192,128]{3,2,1,0:T(8,128)(2,1)S(1)} collective-permute-done((bf16[4,2,192,128]{3,2,1,0:T(8,128)(2,1)S(1)}, bf16[4,2,192,128]{3,2,1,0:T(8,128)(2,1)S(1)}, u32[]{:S(2)}, u32[]{:S(2)}) %collective-permute-start.7) | collective-permute-done | bytes 393248 | tf_op jit(solution)/shard_map/ppermute | solution.py:41
  70.7 8.2 %collective-permute-done.8 = bf16[4,2,192,128]{3,2,1,0:T(8,128)(2,1)S(1)} collective-permute-done((bf16[4,2,192,128]{3,2,1,0:T(8,128)(2,1)S(1)}, bf16[4,2,192,128]{3,2,1,0:T(8,128)(2,1)S(1)}, u32[]{:S(2)}, u32[]{:S(2)}) %collective-permute-start.8) | collective-permute-done | bytes 393248 | tf_op jit(solution)/shard_map/ppermute | solution.py:41
  78.9 1.6 collective-permute-done.9
  80.6 2.2 collective-permute-start.13
  83.4 6.4 %shard_map.44 = (bf16[2,384,512]{2,1,0:T(8,128)(2,1)S(1)}, bf16[2,384,512]{2,1,0:T(8,128)(2,1)S(1)}, bf16[2,384,512]{2,1,0:T(8,128)(2,1)S(1)}, bf16[2,384,512]{2,1,0:T(8,128)(2,1)S(1)}, s32[1]{0:T(128)}) custom-call(s32[5]{0:T(128)S(1)} %stack.23.where, f32[8]{0:T(128)S(1)} %convert_multiply_fusion.factors, s32[1]{0:T(128)} %get-tuple-element.88.order, ...), custom_call_target="tpu_custom_call" | custom-call | flops 6442450944 | bytes 8388608 | tf_op jit(solution)/shard_map/pallas_call | solution.py:261
  89.8 1.6 collective-permute-start.16
  91.4 2.7 %collective-permute-start.17 = (bf16[8,2,4,32,128]{4,3,2,1,0:T(8,128)(2,1)S(1)}, bf16[8,2,4,32,128]{4,3,2,1,0:T(8,128)(2,1)S(1)}, u32[]{:S(2)}, u32[]{:S(2)}) collective-permute-start(bf16[8,2,4,32,128]{4,3,2,1,0:T(8,128)(2,1)S(1)} %get-tuple-element.105), channel_id=1, source_target_pairs={{0,64},{32,96},{64,0},{96,32},{1,65},{33,97},{65,1},{97,33},{2,66}... | collective-permute-start | bytes 1572872 | tf_op jit(solution)/shard_map/ppermute | solution.py:41
  94.1 6.4 %collective-permute-done.13 = bf16[4,4,96,128]{3,2,1,0:T(8,128)(2,1)S(1)} collective-permute-done((bf16[4,4,96,128]{3,2,1,0:T(8,128)(2,1)S(1)}, bf16[4,4,96,128]{3,2,1,0:T(8,128)(2,1)S(1)}, u32[]{:S(2)}, u32[]{:S(2)}) %collective-permute-start.13) | collective-permute-done | bytes 393248 | tf_op jit(solution)/shard_map/ppermute | solution.py:41
  100.5 2.8 %collective-permute-start.18 = (bf16[8,2,4,32,128]{4,3,2,1,0:T(8,128)(2,1)S(1)}, bf16[8,2,4,32,128]{4,3,2,1,0:T(8,128)(2,1)S(1)}, u32[]{:S(2)}, u32[]{:S(2)}) collective-permute-start(bf16[8,2,4,32,128]{4,3,2,1,0:T(8,128)(2,1)S(1)} %get-tuple-element.106), channel_id=1, source_target_pairs={{0,96},{32,64},{64,32},{96,0},{1,97},{33,65},{65,33},{97,1},{2,98}... | collective-permute-start | bytes 1572872 | tf_op jit(solution)/shard_map/ppermute | solution.py:41
  103.4 6.4 %shard_map.45 = (bf16[8,96,512]{2,1,0:T(8,128)(2,1)S(1)}, bf16[8,96,512]{2,1,0:T(8,128)(2,1)S(1)}, bf16[8,96,512]{2,1,0:T(8,128)(2,1)S(1)}, bf16[8,96,512]{2,1,0:T(8,128)(2,1)S(1)}, s32[1]{0:T(128)}) custom-call(s32[5]{0:T(128)S(1)} %stack.23.where, f32[8]{0:T(128)S(1)} %convert_multiply_fusion.factors, s32[1]{0:T(128)} %get-tuple-element.95.order, ...), custom_call_target="tpu_custom_call" | custom-call | flops 6442450944 | bytes 8388608 | tf_op jit(solution)/shard_map/pallas_call | solution.py:261
  109.8 7.6 %collective-permute-done.17.refs_2_ = bf16[8,2,4,32,128]{4,3,2,1,0:T(8,128)(2,1)S(1)} collective-permute-done((bf16[8,2,4,32,128]{4,3,2,1,0:T(8,128)(2,1)S(1)}, bf16[8,2,4,32,128]{4,3,2,1,0:T(8,128)(2,1)S(1)}, u32[]{:S(2)}, u32[]{:S(2)}) %collective-permute-start.17) | collective-permute-done | bytes 524320 | tf_op jit(solution)/shard_map/ppermute | solution.py:41
  117.3 9.7 %collective-permute-done.18.refs_3_ = bf16[8,2,4,32,128]{4,3,2,1,0:T(8,128)(2,1)S(1)} collective-permute-done((bf16[8,2,4,32,128]{4,3,2,1,0:T(8,128)(2,1)S(1)}, bf16[8,2,4,32,128]{4,3,2,1,0:T(8,128)(2,1)S(1)}, u32[]{:S(2)}, u32[]{:S(2)}) %collective-permute-start.18) | collective-permute-done | bytes 524320 | tf_op jit(solution)/shard_map/ppermute | solution.py:41
  130.4 1.9 collective-permute-start.21
  133.4 19.9 %collective-permute-done.20 = bf16[4,2,4,32,128]{4,3,2,1,0:T(8,128)(2,1)S(1)} collective-permute-done((bf16[4,2,4,32,128]{4,3,2,1,0:T(8,128)(2,1)S(1)}, bf16[4,2,4,32,128]{4,3,2,1,0:T(8,128)(2,1)S(1)}, u32[]{:S(2)}, u32[]{:S(2)}) %collective-permute-start.20) | collective-permute-done | bytes 262176 | tf_op jit(solution)/shard_map/ppermute | solution.py:41
  153.2 2.2 collective-permute-start.39
  155.4 4.7 %collective-permute-done.21 = bf16[4,2,4,32,128]{4,3,2,1,0:T(8,128)(2,1)S(1)} collective-permute-done((bf16[4,2,4,32,128]{4,3,2,1,0:T(8,128)(2,1)S(1)}, bf16[4,2,4,32,128]{4,3,2,1,0:T(8,128)(2,1)S(1)}, u32[]{:S(2)}, u32[]{:S(2)}) %collective-permute-start.21) | collective-permute-done | bytes 262176 | tf_op jit(solution)/shard_map/ppermute | solution.py:41
  160.1 1.9 collective-permute-start.40
  162.1 2.3 collective-permute-start.41
  164.8 2.2 collective-permute-start.35
  167.0 5.7 %shard_map.47 = (bf16[4,128,512]{2,1,0:T(8,128)(2,1)S(1)}, bf16[4,128,512]{2,1,0:T(8,128)(2,1)S(1)}, bf16[4,128,512]{2,1,0:T(8,128)(2,1)S(1)}, bf16[4,128,512]{2,1,0:T(8,128)(2,1)S(1)}, s32[1]{0:T(128)}) custom-call(s32[5]{0:T(128)S(1)} %stack.23.where, f32[8]{0:T(128)S(1)} %convert_multiply_fusion.factors, s32[1]{0:T(128)} %get-tuple-element.107.order, ...), custom_call_target="tpu_custom_call" | custom-call | flops 4294967296 | bytes 8388608 | tf_op jit(solution)/shard_map/pallas_call | solution.py:261
  172.9 16.7 %collective-permute-done.40 = bf16[8,96,512]{2,1,0:T(8,128)(2,1)S(1)} collective-permute-done((bf16[8,96,512]{2,1,0:T(8,128)(2,1)S(1)}, bf16[8,96,512]{2,1,0:T(8,128)(2,1)S(1)}, u32[]{:S(2)}, u32[]{:S(2)}) %collective-permute-start.40) | collective-permute-done | bytes 786464 | tf_op jit(solution)/shard_map/ppermute | solution.py:41
  189.6 9.7 %collective-permute-done.41 = bf16[8,96,512]{2,1,0:T(8,128)(2,1)S(1)} collective-permute-done((bf16[8,96,512]{2,1,0:T(8,128)(2,1)S(1)}, bf16[8,96,512]{2,1,0:T(8,128)(2,1)S(1)}, u32[]{:S(2)}, u32[]{:S(2)}) %collective-permute-start.41) | collective-permute-done | bytes 786464 | tf_op jit(solution)/shard_map/ppermute | solution.py:41
  201.0 4.8 %collective-permute-done.25 = bf16[4,128,512]{2,1,0:T(8,128)(2,1)S(1)} collective-permute-done((bf16[4,128,512]{2,1,0:T(8,128)(2,1)S(1)}, bf16[4,128,512]{2,1,0:T(8,128)(2,1)S(1)}, u32[]{:S(2)}, u32[]{:S(2)}) %collective-permute-start.25) | collective-permute-done | bytes 524320 | tf_op jit(solution)/shard_map/ppermute | solution.py:41
  205.8 2.6 %collective-permute-start.43 = (bf16[2,96,512]{2,1,0:T(8,128)(2,1)S(1)}, bf16[2,96,512]{2,1,0:T(8,128)(2,1)S(1)}, u32[]{:S(2)}, u32[]{:S(2)}) collective-permute-start(bf16[2,96,512]{2,1,0:T(8,128)(2,1)S(1)} %get-tuple-element.139), channel_id=1, source_target_pairs={{0,64},{32,96},{64,0},{96,32},{1,65},{33,97},{65,1},{97,33},{2,66}... | collective-permute-start | bytes 589832 | tf_op jit(solution)/shard_map/ppermute | solution.py:41
  208.3 8.6 %collective-permute-done.26 = bf16[4,128,512]{2,1,0:T(8,128)(2,1)S(1)} collective-permute-done((bf16[4,128,512]{2,1,0:T(8,128)(2,1)S(1)}, bf16[4,128,512]{2,1,0:T(8,128)(2,1)S(1)}, u32[]{:S(2)}, u32[]{:S(2)}) %collective-permute-start.26) | collective-permute-done | bytes 524320 | tf_op jit(solution)/shard_map/ppermute | solution.py:41
  216.9 2.4 collective-permute-start.44
  220.1 2.1 collective-permute-start.27
  222.3 1.8 collective-permute-start.28
  225.1 2.0 collective-permute-start.37
  227.2 2.6 %collective-permute-start.38 = (bf16[192,512]{1,0:T(8,128)(2,1)S(1)}, bf16[192,512]{1,0:T(8,128)(2,1)S(1)}, u32[]{:S(2)}, u32[]{:S(2)}) collective-permute-start(bf16[192,512]{1,0:T(8,128)(2,1)S(1)} %get-tuple-element.132), channel_id=1, source_target_pairs={{0,24},{8,16},{16,8},{24,0},{1,25},{9,17},{17,9},{25,1},{2,26},{10... | collective-permute-start | bytes 589832 | tf_op jit(solution)/shard_map/ppermute | solution.py:41
  231.0 3.8 %collective-permute-done.29.refs_3_ = bf16[4,32,512]{2,1,0:T(8,128)(2,1)S(1)} collective-permute-done((bf16[4,32,512]{2,1,0:T(8,128)(2,1)S(1)}, bf16[4,32,512]{2,1,0:T(8,128)(2,1)S(1)}, u32[]{:S(2)}, u32[]{:S(2)}) %collective-permute-start.29) | collective-permute-done | bytes 131104 | tf_op jit(solution)/shard_map/ppermute | solution.py:41
  235.6 2.1 collective-permute-start.31
  237.8 2.4 collective-permute-start.32
  240.2 1.6 close.1.refs_4_
  (74 shorter events, 23.3 us)
Async XLA Ops:
  4.4 5.5 %copy-start.1 = (bf16[4,8192,128]{2,1,0:T(8,128)(2,1)S(1)}, bf16[4,8192,128]{2,1,0:T(8,128)(2,1)}, u32[]{:S(2)}) copy-start(bf16[4,8192,128]{2,1,0:T(8,128)(2,1)} %param.3) | copy-start | bytes 25165828
  4.4 5.5 %copy-start.3 = (bf16[2,128,512]{2,1,0:T(8,128)(2,1)S(1)}, bf16[2,128,512]{2,1,0:T(8,128)(2,1)}, u32[]{:S(2)}) copy-start(bf16[2,128,512]{2,1,0:T(8,128)(2,1)} %act.5) | copy-start | bytes 786436
  6.3 18.4 %collective-permute-start = (bf16[7,2,192,128]{3,2,1,0:T(8,128)(2,1)S(1)}, bf16[7,2,192,128]{3,2,1,0:T(8,128)(2,1)S(1)}, u32[]{:S(2)}, u32[]{:S(2)}) collective-permute-start(bf16[7,2,192,128]{3,2,1,0:T(8,128)(2,1)S(1)} %get-tuple-element.78), channel_id=1, source_target_pairs={{0,2},{2,0},{4,6},{6,4},{1,3},{3,1},{5,7},{7,5},{8,10},{10,8},{12,... | collective-permute-start | bytes 2064392 | tf_op jit(solution)/shard_map/ppermute | solution.py:41
  6.8 32.7 %collective-permute-start.1 = (bf16[7,2,192,128]{3,2,1,0:T(8,128)(2,1)S(1)}, bf16[7,2,192,128]{3,2,1,0:T(8,128)(2,1)S(1)}, u32[]{:S(2)}, u32[]{:S(2)}) collective-permute-start(bf16[7,2,192,128]{3,2,1,0:T(8,128)(2,1)S(1)} %get-tuple-element.79), channel_id=1, source_target_pairs={{0,4},{2,6},{4,0},{6,2},{1,5},{3,7},{5,1},{7,3},{8,12},{10,14},{12... | collective-permute-start | bytes 2064392 | tf_op jit(solution)/shard_map/ppermute | solution.py:41
  9.5 31.4 %collective-permute-start.2 = (bf16[7,2,192,128]{3,2,1,0:T(8,128)(2,1)S(1)}, bf16[7,2,192,128]{3,2,1,0:T(8,128)(2,1)S(1)}, u32[]{:S(2)}, u32[]{:S(2)}) collective-permute-start(bf16[7,2,192,128]{3,2,1,0:T(8,128)(2,1)S(1)} %get-tuple-element.80), channel_id=1, source_target_pairs={{0,6},{2,4},{4,2},{6,0},{1,7},{3,5},{5,3},{7,1},{8,14},{10,12},{12... | collective-permute-start | bytes 2064392 | tf_op jit(solution)/shard_map/ppermute | solution.py:41
  11.8 33.6 %collective-permute-start.3 = (bf16[7,4,96,128]{3,2,1,0:T(8,128)(2,1)S(1)}, bf16[7,4,96,128]{3,2,1,0:T(8,128)(2,1)S(1)}, u32[]{:S(2)}, u32[]{:S(2)}) collective-permute-start(bf16[7,4,96,128]{3,2,1,0:T(8,128)(2,1)S(1)} %get-tuple-element.84), channel_id=1, source_target_pairs={{0,16},{8,24},{16,0},{24,8},{1,17},{9,25},{17,1},{25,9},{2,18},{10... | collective-permute-start | bytes 2064392 | tf_op jit(solution)/shard_map/ppermute | solution.py:41
  13.8 32.7 %collective-permute-start.4 = (bf16[7,4,96,128]{3,2,1,0:T(8,128)(2,1)S(1)}, bf16[7,4,96,128]{3,2,1,0:T(8,128)(2,1)S(1)}, u32[]{:S(2)}, u32[]{:S(2)}) collective-permute-start(bf16[7,4,96,128]{3,2,1,0:T(8,128)(2,1)S(1)} %get-tuple-element.85), channel_id=1, source_target_pairs={{0,8},{8,0},{16,24},{24,16},{1,9},{9,1},{17,25},{25,17},{2,10},{10... | collective-permute-start | bytes 2064392 | tf_op jit(solution)/shard_map/ppermute | solution.py:41
  24.7 32.2 %collective-permute-start.5 = (bf16[7,4,96,128]{3,2,1,0:T(8,128)(2,1)S(1)}, bf16[7,4,96,128]{3,2,1,0:T(8,128)(2,1)S(1)}, u32[]{:S(2)}, u32[]{:S(2)}) collective-permute-start(bf16[7,4,96,128]{3,2,1,0:T(8,128)(2,1)S(1)} %get-tuple-element.86), channel_id=1, source_target_pairs={{0,24},{8,16},{16,8},{24,0},{1,25},{9,17},{17,9},{25,1},{2,26},{10... | collective-permute-start | bytes 2064392 | tf_op jit(solution)/shard_map/ppermute | solution.py:41
  41.7 41.1 %collective-permute-start.10 = (bf16[4,3,2,192,128]{4,3,2,1,0:T(8,128)(2,1)S(1)}, bf16[4,3,2,192,128]{4,3,2,1,0:T(8,128)(2,1)S(1)}, u32[]{:S(2)}, u32[]{:S(2)}) collective-permute-start(bf16[4,3,2,192,128]{4,3,2,1,0:T(8,128)(2,1)S(1)} %get-tuple-element.93), channel_id=1, source_target_pairs={{0,1},{1,0},{2,3},{3,2},{4,5},{5,4},{6,7},{7,6},{8,9},{9,8},{10,11... | collective-permute-start | bytes 3538952 | tf_op jit(solution)/shard_map/ppermute | solution.py:41
  41.8 19.6 %collective-permute-start.6 = (bf16[4,2,192,128]{3,2,1,0:T(8,128)(2,1)S(1)}, bf16[4,2,192,128]{3,2,1,0:T(8,128)(2,1)S(1)}, u32[]{:S(2)}, u32[]{:S(2)}) collective-permute-start(bf16[4,2,192,128]{3,2,1,0:T(8,128)(2,1)S(1)} %get-tuple-element.89), channel_id=1, source_target_pairs={{0,1},{1,0},{2,3},{3,2},{4,5},{5,4},{6,7},{7,6},{8,9},{9,8},{10,11... | collective-permute-start | bytes 1179656 | tf_op jit(solution)/shard_map/ppermute | solution.py:41
  58.4 45.0 %collective-permute-start.15 = (bf16[4,3,4,96,128]{4,3,2,1,0:T(8,128)(2,1)S(1)}, bf16[4,3,4,96,128]{4,3,2,1,0:T(8,128)(2,1)S(1)}, u32[]{:S(2)}, u32[]{:S(2)}) collective-permute-start(bf16[4,3,4,96,128]{4,3,2,1,0:T(8,128)(2,1)S(1)} %get-tuple-element.100), channel_id=1, source_target_pairs={{0,1},{1,0},{2,3},{3,2},{4,5},{5,4},{6,7},{7,6},{8,9},{9,8},{10,11... | collective-permute-start | bytes 3538952 | tf_op jit(solution)/shard_map/ppermute | solution.py:41
  58.5 10.9 %collective-permute-start.7 = (bf16[4,2,192,128]{3,2,1,0:T(8,128)(2,1)S(1)}, bf16[4,2,192,128]{3,2,1,0:T(8,128)(2,1)S(1)}, u32[]{:S(2)}, u32[]{:S(2)}) collective-permute-start(bf16[4,2,192,128]{3,2,1,0:T(8,128)(2,1)S(1)} %get-tuple-element.90), channel_id=1, source_target_pairs={{0,3},{1,2},{2,1},{3,0},{4,7},{5,6},{6,5},{7,4},{8,11},{9,10},{10,... | collective-permute-start | bytes 1179656 | tf_op jit(solution)/shard_map/ppermute | solution.py:41
  59.1 19.9 %collective-permute-start.8 = (bf16[4,2,192,128]{3,2,1,0:T(8,128)(2,1)S(1)}, bf16[4,2,192,128]{3,2,1,0:T(8,128)(2,1)S(1)}, u32[]{:S(2)}, u32[]{:S(2)}) collective-permute-start(bf16[4,2,192,128]{3,2,1,0:T(8,128)(2,1)S(1)} %get-tuple-element.91), channel_id=1, source_target_pairs={{0,5},{1,4},{2,7},{3,6},{4,1},{5,0},{6,3},{7,2},{8,13},{9,12},{10,... | collective-permute-start | bytes 1179656 | tf_op jit(solution)/shard_map/ppermute | solution.py:41
  61.3 19.2 %collective-permute-start.9 = (bf16[4,2,192,128]{3,2,1,0:T(8,128)(2,1)S(1)}, bf16[4,2,192,128]{3,2,1,0:T(8,128)(2,1)S(1)}, u32[]{:S(2)}, u32[]{:S(2)}) collective-permute-start(bf16[4,2,192,128]{3,2,1,0:T(8,128)(2,1)S(1)} %get-tuple-element.92), channel_id=1, source_target_pairs={{0,7},{1,6},{2,5},{3,4},{4,3},{5,2},{6,1},{7,0},{8,15},{9,14},{10,... | collective-permute-start | bytes 1179656 | tf_op jit(solution)/shard_map/ppermute | solution.py:41
  69.4 20.4 %collective-permute-start.11 = (bf16[4,4,96,128]{3,2,1,0:T(8,128)(2,1)S(1)}, bf16[4,4,96,128]{3,2,1,0:T(8,128)(2,1)S(1)}, u32[]{:S(2)}, u32[]{:S(2)}) collective-permute-start(bf16[4,4,96,128]{3,2,1,0:T(8,128)(2,1)S(1)} %get-tuple-element.96), channel_id=1, source_target_pairs={{0,1},{1,0},{2,3},{3,2},{4,5},{5,4},{6,7},{7,6},{8,9},{9,8},{10,11... | collective-permute-start | bytes 1179656 | tf_op jit(solution)/shard_map/ppermute | solution.py:41
  78.9 12.4 %collective-permute-start.12 = (bf16[4,4,96,128]{3,2,1,0:T(8,128)(2,1)S(1)}, bf16[4,4,96,128]{3,2,1,0:T(8,128)(2,1)S(1)}, u32[]{:S(2)}, u32[]{:S(2)}) collective-permute-start(bf16[4,4,96,128]{3,2,1,0:T(8,128)(2,1)S(1)} %get-tuple-element.97), channel_id=1, source_target_pairs={{0,17},{1,16},{8,25},{9,24},{16,1},{17,0},{24,9},{25,8},{2,19},{3,... | collective-permute-start | bytes 1179656 | tf_op jit(solution)/shard_map/ppermute | solution.py:41
  80.6 19.9 %collective-permute-start.13 = (bf16[4,4,96,128]{3,2,1,0:T(8,128)(2,1)S(1)}, bf16[4,4,96,128]{3,2,1,0:T(8,128)(2,1)S(1)}, u32[]{:S(2)}, u32[]{:S(2)}) collective-permute-start(bf16[4,4,96,128]{3,2,1,0:T(8,128)(2,1)S(1)} %get-tuple-element.98), channel_id=1, source_target_pairs={{0,9},{1,8},{8,1},{9,0},{16,25},{17,24},{24,17},{25,16},{2,11},{3,... | collective-permute-start | bytes 1179656 | tf_op jit(solution)/shard_map/ppermute | solution.py:41
  82.8 20.6 %collective-permute-start.14 = (bf16[4,4,96,128]{3,2,1,0:T(8,128)(2,1)S(1)}, bf16[4,4,96,128]{3,2,1,0:T(8,128)(2,1)S(1)}, u32[]{:S(2)}, u32[]{:S(2)}) collective-permute-start(bf16[4,4,96,128]{3,2,1,0:T(8,128)(2,1)S(1)} %get-tuple-element.99), channel_id=1, source_target_pairs={{0,25},{1,24},{8,17},{9,16},{16,9},{17,8},{24,1},{25,0},{2,27},{3,... | collective-permute-start | bytes 1179656 | tf_op jit(solution)/shard_map/ppermute | solution.py:41
  89.8 20.0 %collective-permute-start.16 = (bf16[8,2,4,32,128]{4,3,2,1,0:T(8,128)(2,1)S(1)}, bf16[8,2,4,32,128]{4,3,2,1,0:T(8,128)(2,1)S(1)}, u32[]{:S(2)}, u32[]{:S(2)}) collective-permute-start(bf16[8,2,4,32,128]{4,3,2,1,0:T(8,128)(2,1)S(1)} %get-tuple-element.104), channel_id=1, source_target_pairs={{0,32},{32,0},{64,96},{96,64},{1,33},{33,1},{65,97},{97,65},{2,34}... | collective-permute-start | bytes 1572872 | tf_op jit(solution)/shard_map/ppermute | solution.py:41
  91.4 26.0 %collective-permute-start.17 = (bf16[8,2,4,32,128]{4,3,2,1,0:T(8,128)(2,1)S(1)}, bf16[8,2,4,32,128]{4,3,2,1,0:T(8,128)(2,1)S(1)}, u32[]{:S(2)}, u32[]{:S(2)}) collective-permute-start(bf16[8,2,4,32,128]{4,3,2,1,0:T(8,128)(2,1)S(1)} %get-tuple-element.105), channel_id=1, source_target_pairs={{0,64},{32,96},{64,0},{96,32},{1,65},{33,97},{65,1},{97,33},{2,66}... | collective-permute-start | bytes 1572872 | tf_op jit(solution)/shard_map/ppermute | solution.py:41
  100.5 26.6 %collective-permute-start.18 = (bf16[8,2,4,32,128]{4,3,2,1,0:T(8,128)(2,1)S(1)}, bf16[8,2,4,32,128]{4,3,2,1,0:T(8,128)(2,1)S(1)}, u32[]{:S(2)}, u32[]{:S(2)}) collective-permute-start(bf16[8,2,4,32,128]{4,3,2,1,0:T(8,128)(2,1)S(1)} %get-tuple-element.106), channel_id=1, source_target_pairs={{0,96},{32,64},{64,32},{96,0},{1,97},{33,65},{65,33},{97,1},{2,98}... | collective-permute-start | bytes 1572872 | tf_op jit(solution)/shard_map/ppermute | solution.py:41
  128.3 36.5 %collective-permute-start.23 = (bf16[4,4,2,4,32,128]{5,4,3,2,1,0:T(8,128)(2,1)S(1)}, bf16[4,4,2,4,32,128]{5,4,3,2,1,0:T(8,128)(2,1)S(1)}, u32[]{:S(2)}, u32[]{:S(2)}) collective-permute-start(bf16[4,4,2,4,32,128]{5,4,3,2,1,0:T(8,128)(2,1)S(1)} %get-tuple-element.112), channel_id=1, source_target_pairs={{0,1},{1,0},{2,3},{3,2},{4,5},{5,4},{6,7},{7,6},{8,9},{9,8},{10,11... | collective-permute-start | bytes 3145736 | tf_op jit(solution)/shard_map/ppermute | solution.py:41
  128.4 3.8 %collective-permute-start.19 = (bf16[4,2,4,32,128]{4,3,2,1,0:T(8,128)(2,1)S(1)}, bf16[4,2,4,32,128]{4,3,2,1,0:T(8,128)(2,1)S(1)}, u32[]{:S(2)}, u32[]{:S(2)}) collective-permute-start(bf16[4,2,4,32,128]{4,3,2,1,0:T(8,128)(2,1)S(1)} %get-tuple-element.108), channel_id=1, source_target_pairs={{0,1},{1,0},{2,3},{3,2},{4,5},{5,4},{6,7},{7,6},{8,9},{9,8},{10,11... | collective-permute-start | bytes 786440 | tf_op jit(solution)/shard_map/ppermute | solution.py:41
  128.9 35.4 %collective-permute-start.33 = (bf16[2,384,512]{2,1,0:T(8,128)(2,1)S(1)}, bf16[2,384,512]{2,1,0:T(8,128)(2,1)S(1)}, u32[]{:S(2)}, u32[]{:S(2)}) collective-permute-start(bf16[2,384,512]{2,1,0:T(8,128)(2,1)S(1)} %get-tuple-element.126), channel_id=1, source_target_pairs={{0,32},{32,0},{64,96},{96,64},{1,33},{33,1},{65,97},{97,65},{2,34}... | collective-permute-start | bytes 2359304 | tf_op jit(solution)/shard_map/ppermute | solution.py:41
  129.2 24.0 %collective-permute-start.20 = (bf16[4,2,4,32,128]{4,3,2,1,0:T(8,128)(2,1)S(1)}, bf16[4,2,4,32,128]{4,3,2,1,0:T(8,128)(2,1)S(1)}, u32[]{:S(2)}, u32[]{:S(2)}) collective-permute-start(bf16[4,2,4,32,128]{4,3,2,1,0:T(8,128)(2,1)S(1)} %get-tuple-element.109), channel_id=1, source_target_pairs={{0,33},{1,32},{32,1},{33,0},{64,97},{65,96},{96,65},{97,64},{2,35}... | collective-permute-start | bytes 786440 | tf_op jit(solution)/shard_map/ppermute | solution.py:41
  130.4 29.8 %collective-permute-start.21 = (bf16[4,2,4,32,128]{4,3,2,1,0:T(8,128)(2,1)S(1)}, bf16[4,2,4,32,128]{4,3,2,1,0:T(8,128)(2,1)S(1)}, u32[]{:S(2)}, u32[]{:S(2)}) collective-permute-start(bf16[4,2,4,32,128]{4,3,2,1,0:T(8,128)(2,1)S(1)} %get-tuple-element.110), channel_id=1, source_target_pairs={{0,65},{1,64},{32,97},{33,96},{64,1},{65,0},{96,33},{97,32},{2,67}... | collective-permute-start | bytes 786440 | tf_op jit(solution)/shard_map/ppermute | solution.py:41
  132.3 29.8 %collective-permute-start.22 = (bf16[4,2,4,32,128]{4,3,2,1,0:T(8,128)(2,1)S(1)}, bf16[4,2,4,32,128]{4,3,2,1,0:T(8,128)(2,1)S(1)}, u32[]{:S(2)}, u32[]{:S(2)}) collective-permute-start(bf16[4,2,4,32,128]{4,3,2,1,0:T(8,128)(2,1)S(1)} %get-tuple-element.111), channel_id=1, source_target_pairs={{0,97},{1,96},{32,65},{33,64},{64,33},{65,32},{96,1},{97,0},{2,99}... | collective-permute-start | bytes 786440 | tf_op jit(solution)/shard_map/ppermute | solution.py:41
  153.2 19.7 %collective-permute-start.39 = (bf16[8,96,512]{2,1,0:T(8,128)(2,1)S(1)}, bf16[8,96,512]{2,1,0:T(8,128)(2,1)S(1)}, u32[]{:S(2)}, u32[]{:S(2)}) collective-permute-start(bf16[8,96,512]{2,1,0:T(8,128)(2,1)S(1)} %get-tuple-element.134), channel_id=1, source_target_pairs={{0,2},{2,0},{4,6},{6,4},{1,3},{3,1},{5,7},{7,5},{8,10},{10,8},{12,... | collective-permute-start | bytes 2359304 | tf_op jit(solution)/shard_map/ppermute | solution.py:41
  160.1 29.5 %collective-permute-start.40 = (bf16[8,96,512]{2,1,0:T(8,128)(2,1)S(1)}, bf16[8,96,512]{2,1,0:T(8,128)(2,1)S(1)}, u32[]{:S(2)}, u32[]{:S(2)}) collective-permute-start(bf16[8,96,512]{2,1,0:T(8,128)(2,1)S(1)} %get-tuple-element.135), channel_id=1, source_target_pairs={{0,4},{2,6},{4,0},{6,2},{1,5},{3,7},{5,1},{7,3},{8,12},{10,14},{12... | collective-permute-start | bytes 2359304 | tf_op jit(solution)/shard_map/ppermute | solution.py:41
  162.1 37.3 %collective-permute-start.41 = (bf16[8,96,512]{2,1,0:T(8,128)(2,1)S(1)}, bf16[8,96,512]{2,1,0:T(8,128)(2,1)S(1)}, u32[]{:S(2)}, u32[]{:S(2)}) collective-permute-start(bf16[8,96,512]{2,1,0:T(8,128)(2,1)S(1)} %get-tuple-element.136), channel_id=1, source_target_pairs={{0,6},{2,4},{4,2},{6,0},{1,7},{3,5},{5,3},{7,1},{8,14},{10,12},{12... | collective-permute-start | bytes 2359304 | tf_op jit(solution)/shard_map/ppermute | solution.py:41
  164.4 55.8 %collective-permute-start.34 = (bf16[2,384,512]{2,1,0:T(8,128)(2,1)S(1)}, bf16[2,384,512]{2,1,0:T(8,128)(2,1)S(1)}, u32[]{:S(2)}, u32[]{:S(2)}) collective-permute-start(bf16[2,384,512]{2,1,0:T(8,128)(2,1)S(1)} %get-tuple-element.127), channel_id=1, source_target_pairs={{0,64},{32,96},{64,0},{96,32},{1,65},{33,97},{65,1},{97,33},{2,66}... | collective-permute-start | bytes 2359304 | tf_op jit(solution)/shard_map/ppermute | solution.py:41
  164.8 57.5 %collective-permute-start.35 = (bf16[2,384,512]{2,1,0:T(8,128)(2,1)S(1)}, bf16[2,384,512]{2,1,0:T(8,128)(2,1)S(1)}, u32[]{:S(2)}, u32[]{:S(2)}) collective-permute-start(bf16[2,384,512]{2,1,0:T(8,128)(2,1)S(1)} %get-tuple-element.128), channel_id=1, source_target_pairs={{0,96},{32,64},{64,32},{96,0},{1,97},{33,65},{65,33},{97,1},{2,98}... | collective-permute-start | bytes 2359304 | tf_op jit(solution)/shard_map/ppermute | solution.py:41
  172.9 28.0 %collective-permute-start.24 = (bf16[4,128,512]{2,1,0:T(8,128)(2,1)S(1)}, bf16[4,128,512]{2,1,0:T(8,128)(2,1)S(1)}, u32[]{:S(2)}, u32[]{:S(2)}) collective-permute-start(bf16[4,128,512]{2,1,0:T(8,128)(2,1)S(1)} %get-tuple-element.114), channel_id=1, source_target_pairs={{0,16},{8,24},{16,0},{24,8},{1,17},{9,25},{17,1},{25,9},{2,18},{10... | collective-permute-start | bytes 1572872 | tf_op jit(solution)/shard_map/ppermute | solution.py:41
  189.6 16.2 %collective-permute-start.25 = (bf16[4,128,512]{2,1,0:T(8,128)(2,1)S(1)}, bf16[4,128,512]{2,1,0:T(8,128)(2,1)S(1)}, u32[]{:S(2)}, u32[]{:S(2)}) collective-permute-start(bf16[4,128,512]{2,1,0:T(8,128)(2,1)S(1)} %get-tuple-element.115), channel_id=1, source_target_pairs={{0,8},{8,0},{16,24},{24,16},{1,9},{9,1},{17,25},{25,17},{2,10},{10... | collective-permute-start | bytes 1572872 | tf_op jit(solution)/shard_map/ppermute | solution.py:41
  199.3 17.6 %collective-permute-start.26 = (bf16[4,128,512]{2,1,0:T(8,128)(2,1)S(1)}, bf16[4,128,512]{2,1,0:T(8,128)(2,1)S(1)}, u32[]{:S(2)}, u32[]{:S(2)}) collective-permute-start(bf16[4,128,512]{2,1,0:T(8,128)(2,1)S(1)} %get-tuple-element.116), channel_id=1, source_target_pairs={{0,24},{8,16},{16,8},{24,0},{1,25},{9,17},{17,9},{25,1},{2,26},{10... | collective-permute-start | bytes 1572872 | tf_op jit(solution)/shard_map/ppermute | solution.py:41
  200.9 24.1 %collective-permute-start.42 = (bf16[2,96,512]{2,1,0:T(8,128)(2,1)S(1)}, bf16[2,96,512]{2,1,0:T(8,128)(2,1)S(1)}, u32[]{:S(2)}, u32[]{:S(2)}) collective-permute-start(bf16[2,96,512]{2,1,0:T(8,128)(2,1)S(1)} %get-tuple-element.138), channel_id=1, source_target_pairs={{0,32},{32,0},{64,96},{96,64},{1,33},{33,1},{65,97},{97,65},{2,34}... | collective-permute-start | bytes 589832 | tf_op jit(solution)/shard_map/ppermute | solution.py:41
  205.8 19.4 %collective-permute-start.43 = (bf16[2,96,512]{2,1,0:T(8,128)(2,1)S(1)}, bf16[2,96,512]{2,1,0:T(8,128)(2,1)S(1)}, u32[]{:S(2)}, u32[]{:S(2)}) collective-permute-start(bf16[2,96,512]{2,1,0:T(8,128)(2,1)S(1)} %get-tuple-element.139), channel_id=1, source_target_pairs={{0,64},{32,96},{64,0},{96,32},{1,65},{33,97},{65,1},{97,33},{2,66}... | collective-permute-start | bytes 589832 | tf_op jit(solution)/shard_map/ppermute | solution.py:41
  216.9 10.3 %collective-permute-start.44 = (bf16[2,96,512]{2,1,0:T(8,128)(2,1)S(1)}, bf16[2,96,512]{2,1,0:T(8,128)(2,1)S(1)}, u32[]{:S(2)}, u32[]{:S(2)}) collective-permute-start(bf16[2,96,512]{2,1,0:T(8,128)(2,1)S(1)} %get-tuple-element.140), channel_id=1, source_target_pairs={{0,96},{32,64},{64,32},{96,0},{1,97},{33,65},{65,33},{97,1},{2,98}... | collective-permute-start | bytes 589832 | tf_op jit(solution)/shard_map/ppermute | solution.py:41
  220.1 9.7 %collective-permute-start.27 = (bf16[4,32,512]{2,1,0:T(8,128)(2,1)S(1)}, bf16[4,32,512]{2,1,0:T(8,128)(2,1)S(1)}, u32[]{:S(2)}, u32[]{:S(2)}) collective-permute-start(bf16[4,32,512]{2,1,0:T(8,128)(2,1)S(1)} %get-tuple-element.118), channel_id=1, source_target_pairs={{0,2},{2,0},{4,6},{6,4},{1,3},{3,1},{5,7},{7,5},{8,10},{10,8},{12,... | collective-permute-start | bytes 393224 | tf_op jit(solution)/shard_map/ppermute | solution.py:41
  222.3 8.7 %collective-permute-start.28 = (bf16[4,32,512]{2,1,0:T(8,128)(2,1)S(1)}, bf16[4,32,512]{2,1,0:T(8,128)(2,1)S(1)}, u32[]{:S(2)}, u32[]{:S(2)}) collective-permute-start(bf16[4,32,512]{2,1,0:T(8,128)(2,1)S(1)} %get-tuple-element.119), channel_id=1, source_target_pairs={{0,4},{2,6},{4,0},{6,2},{1,5},{3,7},{5,1},{7,3},{8,12},{10,14},{12... | collective-permute-start | bytes 393224 | tf_op jit(solution)/shard_map/ppermute | solution.py:41
  225.0 10.6 %collective-permute-start.36 = (bf16[192,512]{1,0:T(8,128)(2,1)S(1)}, bf16[192,512]{1,0:T(8,128)(2,1)S(1)}, u32[]{:S(2)}, u32[]{:S(2)}) collective-permute-start(bf16[192,512]{1,0:T(8,128)(2,1)S(1)} %get-tuple-element.130), channel_id=1, source_target_pairs={{0,16},{8,24},{16,0},{24,8},{1,17},{9,25},{17,1},{25,9},{2,18},{10... | collective-permute-start | bytes 589832 | tf_op jit(solution)/shard_map/ppermute | solution.py:41
  225.1 12.6 %collective-permute-start.37 = (bf16[192,512]{1,0:T(8,128)(2,1)S(1)}, bf16[192,512]{1,0:T(8,128)(2,1)S(1)}, u32[]{:S(2)}, u32[]{:S(2)}) collective-permute-start(bf16[192,512]{1,0:T(8,128)(2,1)S(1)} %get-tuple-element.131), channel_id=1, source_target_pairs={{0,8},{8,0},{16,24},{24,16},{1,9},{9,1},{17,25},{25,17},{2,10},{10... | collective-permute-start | bytes 589832 | tf_op jit(solution)/shard_map/ppermute | solution.py:41
  227.2 13.0 %collective-permute-start.38 = (bf16[192,512]{1,0:T(8,128)(2,1)S(1)}, bf16[192,512]{1,0:T(8,128)(2,1)S(1)}, u32[]{:S(2)}, u32[]{:S(2)}) collective-permute-start(bf16[192,512]{1,0:T(8,128)(2,1)S(1)} %get-tuple-element.132), channel_id=1, source_target_pairs={{0,24},{8,16},{16,8},{24,0},{1,25},{9,17},{17,9},{25,1},{2,26},{10... | collective-permute-start | bytes 589832 | tf_op jit(solution)/shard_map/ppermute | solution.py:41
  229.8 5.0 %collective-permute-start.29 = (bf16[4,32,512]{2,1,0:T(8,128)(2,1)S(1)}, bf16[4,32,512]{2,1,0:T(8,128)(2,1)S(1)}, u32[]{:S(2)}, u32[]{:S(2)}) collective-permute-start(bf16[4,32,512]{2,1,0:T(8,128)(2,1)S(1)} %get-tuple-element.120), channel_id=1, source_target_pairs={{0,6},{2,4},{4,2},{6,0},{1,7},{3,5},{5,3},{7,1},{8,14},{10,12},{12... | collective-permute-start | bytes 393224 | tf_op jit(solution)/shard_map/ppermute | solution.py:41
  230.9 9.3 %collective-permute-start.45 = (bf16[96,512]{1,0:T(8,128)(2,1)S(1)}, bf16[96,512]{1,0:T(8,128)(2,1)S(1)}, u32[]{:S(2)}, u32[]{:S(2)}) collective-permute-start(bf16[96,512]{1,0:T(8,128)(2,1)S(1)} %get-tuple-element.142), channel_id=1, source_target_pairs={{0,16},{8,24},{16,0},{24,8},{1,17},{9,25},{17,1},{25,9},{2,18},{10... | collective-permute-start | bytes 294920 | tf_op jit(solution)/shard_map/ppermute | solution.py:41
  235.4 6.4 %collective-permute-start.30 = (bf16[32,512]{1,0:T(8,128)(2,1)S(1)}, bf16[32,512]{1,0:T(8,128)(2,1)S(1)}, u32[]{:S(2)}, u32[]{:S(2)}) collective-permute-start(bf16[32,512]{1,0:T(8,128)(2,1)S(1)} %get-tuple-element.122), channel_id=1, source_target_pairs={{0,32},{32,0},{64,96},{96,64},{1,33},{33,1},{65,97},{97,65},{2,34}... | collective-permute-start | bytes 98312 | tf_op jit(solution)/shard_map/ppermute | solution.py:41
  235.6 6.2 %collective-permute-start.31 = (bf16[32,512]{1,0:T(8,128)(2,1)S(1)}, bf16[32,512]{1,0:T(8,128)(2,1)S(1)}, u32[]{:S(2)}, u32[]{:S(2)}) collective-permute-start(bf16[32,512]{1,0:T(8,128)(2,1)S(1)} %get-tuple-element.123), channel_id=1, source_target_pairs={{0,64},{32,96},{64,0},{96,32},{1,65},{33,97},{65,1},{97,33},{2,66}... | collective-permute-start | bytes 98312 | tf_op jit(solution)/shard_map/ppermute | solution.py:41
  237.8 5.1 %collective-permute-start.32 = (bf16[32,512]{1,0:T(8,128)(2,1)S(1)}, bf16[32,512]{1,0:T(8,128)(2,1)S(1)}, u32[]{:S(2)}, u32[]{:S(2)}) collective-permute-start(bf16[32,512]{1,0:T(8,128)(2,1)S(1)} %get-tuple-element.124), channel_id=1, source_target_pairs={{0,96},{32,64},{64,32},{96,0},{1,97},{33,65},{65,33},{97,1},{2,98}... | collective-permute-start | bytes 98312 | tf_op jit(solution)/shard_map/ppermute | solution.py:41
  (3 other events, 9.2 us)

commit v4 on v3

--- a/solution.py
+++ b/solution.py
@@ -302,25 +302,29 @@
     return [arrived[d] for d in range(len(parts))]
 
 
-def close_kernel(where, *refs):
-    fy, fz, out = refs[:4], refs[4:6], refs[6]
-    zl, half = where[2], ROWS_Z // 2
+def close_kernel(*refs):
+    fy, out = refs[:4], refs[4]
     total = fy[0][...]
     for part in fy[1:]:
         total = total + part[...].astype(F32)
     out[0, AT_Y : AT_Y + ROWS_Y, :] = total
+
+
+def final_kernel(where, *refs):
+    fx, fz, out, rows_x, rows_z, sem = refs[:4], refs[4:6], *refs[7:]
+    x, zl, quarter, half = where[0], where[2], ROWS_X // 4, ROWS_Z // 2
     for d in range(2):
-        out[0, pl.ds(pl.multiple_of(AT_Z + (zl ^ d) * half, 16), half), :] = fz[d][...].astype(F32)
-
-
-def final_kernel(where, *refs):
-    fx, out, rows, sem = refs[:4], refs[5], refs[6], refs[7]
-    x, quarter = where[0], ROWS_X // 4
+        rows_z[pl.ds(pl.multiple_of((zl ^ d) * half, 16), half), :] = fz[d][...].astype(F32)
     for d in range(4):
-        rows[pl.ds(pl.multiple_of((x ^ d) * quarter, 16), quarter), :] = fx[d][...].astype(F32)
-    copy = pltpu.make_async_copy(rows, out.at[0, pl.ds(0, ROWS_X)], sem.at[0])
-    copy.start()
-    copy.wait()
+        rows_x[pl.ds(pl.multiple_of((x ^ d) * quarter, 16), quarter), :] = fx[d][...].astype(F32)
+    copies = [
+        pltpu.make_async_copy(rows_z, out.at[0, pl.ds(AT_Z, ROWS_Z)], sem.at[0]),
+        pltpu.make_async_copy(rows_x, out.at[0, pl.ds(0, ROWS_X)], sem.at[1]),
+    ]
+    for copy in copies:
+        copy.start()
+    for copy in copies:
+        copy.wait()
 
 
 def per_device(weight, activation, points):
@@ -334,7 +338,9 @@
     for family in FAMILIES:
         sent, order = pack(family, view, activation, order)
         same = exchange(sent[:4], family)
-        cross = {d: flip(sent[4 + d], family, d, 1) for d in (2, 1, 3, 0)}
+        cross = {}
+        for d in range(4):
+            cross[d] = flip(sent[4 + d], family, d, 1)
         pieces[family] = same + [cross[d] for d in range(4)]
     order, shared = order[:1], {}
 
@@ -380,23 +386,27 @@
     out = pl.pallas_call(
         close_kernel,
         out_shape=jax.ShapeDtypeStruct((1, 512, TOKENS), F32),
-        in_specs=[SMEM] + [VMEM] * 6,
+        in_specs=[VMEM] * 4,
         out_specs=VMEM,
         cost_estimate=pl.CostEstimate(flops=1 << 20, bytes_accessed=3 << 20, transcendentals=0),
         compiler_params=pltpu.CompilerParams(vmem_limit_bytes=8 << 20),
         name="close",
-    )(where, *py, *pz)
+    )(*py)
     return pl.pallas_call(
         final_kernel,
         out_shape=jax.ShapeDtypeStruct((1, 512, TOKENS), F32),
-        in_specs=[SMEM] + [VMEM] * 4 + [HBM],
+        in_specs=[SMEM] + [VMEM] * 6 + [HBM],
         out_specs=HBM,
-        input_output_aliases={5: 0},
-        scratch_shapes=[pltpu.VMEM((ROWS_X, TOKENS), F32), pltpu.SemaphoreType.DMA((1,))],
+        input_output_aliases={7: 0},
+        scratch_shapes=[
+            pltpu.VMEM((ROWS_X, TOKENS), F32),
+            pltpu.VMEM((ROWS_Z, TOKENS), F32),
+            pltpu.SemaphoreType.DMA((2,)),
+        ],
         cost_estimate=pl.CostEstimate(flops=1 << 16, bytes_accessed=1 << 19, transcendentals=0),
         compiler_params=pltpu.CompilerParams(vmem_limit_bytes=4 << 20),
         name="final",
-    )(where, *px, out)
+    )(where, *px, *pz, out)
 
 
 def solution(mesh):

time: 248 us -> 248 us (level)
  transfers between devices with their start and end apart: 46 -> 46, of which waited for: 21 -> 21; matrix products, arithmetic and copies ran while one was open for 0% -> 0% of each run, Pallas kernels for 15% -> 14%
where the time goes in v4:
time: 248 us; the launch traced here: 244 us
  waiting for transfers between devices  137 us (55%)
  starting transfers between devices  62.9 us (25%)
  Pallas kernels  40 us (16%)
  local copies, waits for them, and re-layouts  4.43 us (2%)
    ppermute x46, waiting for transfers between devices, flip(): return lax.ppermute(value, tuple(over), pairs)  137 us
    ppermute x46, starting transfers between devices, flip(): return lax.ppermute(value, tuple(over), pairs)  62.9 us
    pallas_call x3, Pallas kernels, product(): pl.pallas_call(functools.partial(product_kernel, family), out_shape=[jax....  18.5 us
    pallas_call x2, Pallas kernels, begin(): pl.pallas_call(functools.partial(begin_kernel, family), out_shape=[jax.Sh...  6.19 us
    pallas_call x3, Pallas kernels, pack(): pl.pallas_call(functools.partial(pack_kernel, family), out_shape=shapes +...  5.36 us
  transfers between devices with their start and end apart: 46, of which 21 were waited for; matrix products, arithmetic and copies ran while one was open for 0% of the time, Pallas kernels for 14%

profile of v4, /device:TPU:8, one launch (start us, length us, event | category | flops | bytes accessed | tf_op | source)
XLA Modules:
  0.0 244.4 jit_solution(16021198582677560182)
XLA Ops:
  0.1 3.4 %copy-done = bf16[4,8192,128]{2,1,0:T(8,128)(2,1)S(1)} copy-done((bf16[4,8192,128]{2,1,0:T(8,128)(2,1)S(1)}, bf16[4,8192,128]{2,1,0:T(8,128)(2,1)}, u32[]{:S(2)}) %copy-start) | copy-done | bytes 8388632
  4.4 1.9 shard_map.37
  6.8 2.7 %collective-permute-start.1 = (bf16[7,2,192,128]{3,2,1,0:T(8,128)(2,1)S(1)}, bf16[7,2,192,128]{3,2,1,0:T(8,128)(2,1)S(1)}, u32[]{:S(2)}, u32[]{:S(2)}) collective-permute-start(bf16[7,2,192,128]{3,2,1,0:T(8,128)(2,1)S(1)} %get-tuple-element.79), channel_id=1, source_target_pairs={{0,4},{2,6},{4,0},{6,2},{1,5},{3,7},{5,1},{7,3},{8,12},{10,14},{12... | collective-permute-start | bytes 2064392 | tf_op jit(solution)/shard_map/ppermute | solution.py:41
  9.9 1.9 shard_map.38
  11.8 2.0 collective-permute-start.3
  13.8 3.6 %collective-permute-start.4 = (bf16[7,4,96,128]{3,2,1,0:T(8,128)(2,1)S(1)}, bf16[7,4,96,128]{3,2,1,0:T(8,128)(2,1)S(1)}, u32[]{:S(2)}, u32[]{:S(2)}) collective-permute-start(bf16[7,4,96,128]{3,2,1,0:T(8,128)(2,1)S(1)} %get-tuple-element.85), channel_id=1, source_target_pairs={{0,8},{8,0},{16,24},{24,16},{1,9},{9,1},{17,25},{25,17},{2,10},{10... | collective-permute-start | bytes 2064392 | tf_op jit(solution)/shard_map/ppermute | solution.py:41
  17.4 7.3 %collective-permute-done.refs_1_ = bf16[7,2,192,128]{3,2,1,0:T(8,128)(2,1)S(1)} collective-permute-done((bf16[7,2,192,128]{3,2,1,0:T(8,128)(2,1)S(1)}, bf16[7,2,192,128]{3,2,1,0:T(8,128)(2,1)S(1)}, u32[]{:S(2)}, u32[]{:S(2)}) %collective-permute-start) | collective-permute-done | bytes 688160 | tf_op jit(solution)/shard_map/ppermute | solution.py:41
  24.7 4.0 %collective-permute-start.5 = (bf16[7,4,96,128]{3,2,1,0:T(8,128)(2,1)S(1)}, bf16[7,4,96,128]{3,2,1,0:T(8,128)(2,1)S(1)}, u32[]{:S(2)}, u32[]{:S(2)}) collective-permute-start(bf16[7,4,96,128]{3,2,1,0:T(8,128)(2,1)S(1)} %get-tuple-element.86), channel_id=1, source_target_pairs={{0,24},{8,16},{16,8},{24,0},{1,25},{9,17},{17,9},{25,1},{2,26},{10... | collective-permute-start | bytes 2064392 | tf_op jit(solution)/shard_map/ppermute | solution.py:41
  28.8 1.6 shard_map.39
  30.3 9.1 %collective-permute-done.1.refs_2_ = bf16[7,2,192,128]{3,2,1,0:T(8,128)(2,1)S(1)} collective-permute-done((bf16[7,2,192,128]{3,2,1,0:T(8,128)(2,1)S(1)}, bf16[7,2,192,128]{3,2,1,0:T(8,128)(2,1)S(1)}, u32[]{:S(2)}, u32[]{:S(2)}) %collective-permute-start.1) | collective-permute-done | bytes 688160 | tf_op jit(solution)/shard_map/ppermute | solution.py:41
  42.3 3.1 %shard_map.41 = (f32[4,384,1024]{2,1,0:T(8,128)S(1)}, s32[1]{0:T(128)}) custom-call(s32[5]{0:T(128)S(1)} %stack.23.where, s32[1]{0:T(128)} %get-tuple-element.81.order, bf16[7,384,128]{2,1,0:T(8,128)(2,1)S(1)} %bitcast.61, bf16[7,384,128]{2,1,0:T(8,128)(2,1)S(1)} %bitcast.62, bf16[7,384,128]{2,1,0:T(8,128)(2,1)S(1)} %bitcast.63, ...), custom_call_target="tpu_custom_call" | custom-call | flops 1610612736 | bytes 8388608 | tf_op jit(solution)/shard_map/pallas_call | solution.py:205
  46.5 10.4 %collective-permute-done.5.refs_3_ = bf16[7,4,96,128]{3,2,1,0:T(8,128)(2,1)S(1)} collective-permute-done((bf16[7,4,96,128]{3,2,1,0:T(8,128)(2,1)S(1)}, bf16[7,4,96,128]{3,2,1,0:T(8,128)(2,1)S(1)}, u32[]{:S(2)}, u32[]{:S(2)}) %collective-permute-start.5) | collective-permute-done | bytes 688160 | tf_op jit(solution)/shard_map/ppermute | solution.py:41
  59.1 2.3 collective-permute-start.8
  61.8 3.1 %shard_map.43 = (f32[4,384,1024]{2,1,0:T(8,128)S(1)}, s32[1]{0:T(128)}) custom-call(s32[5]{0:T(128)S(1)} %stack.23.where, s32[1]{0:T(128)} %get-tuple-element.87.order, bf16[7,384,128]{2,1,0:T(8,128)(2,1)S(1)} %bitcast.57, bf16[7,384,128]{2,1,0:T(8,128)(2,1)S(1)} %bitcast.58, bf16[7,384,128]{2,1,0:T(8,128)(2,1)S(1)} %bitcast.59, ...), custom_call_target="tpu_custom_call" | custom-call | flops 1610612736 | bytes 8388608 | tf_op jit(solution)/shard_map/pallas_call | solution.py:205
  64.9 4.5 %collective-permute-done.7 = bf16[4,2,192,128]{3,2,1,0:T(8,128)(2,1)S(1)} collective-permute-done((bf16[4,2,192,128]{3,2,1,0:T(8,128)(2,1)S(1)}, bf16[4,2,192,128]{3,2,1,0:T(8,128)(2,1)S(1)}, u32[]{:S(2)}, u32[]{:S(2)}) %collective-permute-start.7) | collective-permute-done | bytes 393248 | tf_op jit(solution)/shard_map/ppermute | solution.py:41
  70.7 8.2 %collective-permute-done.8 = bf16[4,2,192,128]{3,2,1,0:T(8,128)(2,1)S(1)} collective-permute-done((bf16[4,2,192,128]{3,2,1,0:T(8,128)(2,1)S(1)}, bf16[4,2,192,128]{3,2,1,0:T(8,128)(2,1)S(1)}, u32[]{:S(2)}, u32[]{:S(2)}) %collective-permute-start.8) | collective-permute-done | bytes 393248 | tf_op jit(solution)/shard_map/ppermute | solution.py:41
  78.9 1.6 collective-permute-done.9
  80.6 2.2 collective-permute-start.13
  83.4 6.4 %shard_map.44 = (bf16[2,384,512]{2,1,0:T(8,128)(2,1)S(1)}, bf16[2,384,512]{2,1,0:T(8,128)(2,1)S(1)}, bf16[2,384,512]{2,1,0:T(8,128)(2,1)S(1)}, bf16[2,384,512]{2,1,0:T(8,128)(2,1)S(1)}, s32[1]{0:T(128)}) custom-call(s32[5]{0:T(128)S(1)} %stack.23.where, f32[8]{0:T(128)S(1)} %convert_multiply_fusion.factors, s32[1]{0:T(128)} %get-tuple-element.88.order, ...), custom_call_target="tpu_custom_call" | custom-call | flops 6442450944 | bytes 8388608 | tf_op jit(solution)/shard_map/pallas_call | solution.py:261
  89.8 1.6 collective-permute-start.16
  91.4 2.7 %collective-permute-start.17 = (bf16[8,2,4,32,128]{4,3,2,1,0:T(8,128)(2,1)S(1)}, bf16[8,2,4,32,128]{4,3,2,1,0:T(8,128)(2,1)S(1)}, u32[]{:S(2)}, u32[]{:S(2)}) collective-permute-start(bf16[8,2,4,32,128]{4,3,2,1,0:T(8,128)(2,1)S(1)} %get-tuple-element.105), channel_id=1, source_target_pairs={{0,64},{32,96},{64,0},{96,32},{1,65},{33,97},{65,1},{97,33},{2,66}... | collective-permute-start | bytes 1572872 | tf_op jit(solution)/shard_map/ppermute | solution.py:41
  94.1 6.4 %collective-permute-done.13 = bf16[4,4,96,128]{3,2,1,0:T(8,128)(2,1)S(1)} collective-permute-done((bf16[4,4,96,128]{3,2,1,0:T(8,128)(2,1)S(1)}, bf16[4,4,96,128]{3,2,1,0:T(8,128)(2,1)S(1)}, u32[]{:S(2)}, u32[]{:S(2)}) %collective-permute-start.13) | collective-permute-done | bytes 393248 | tf_op jit(solution)/shard_map/ppermute | solution.py:41
  100.5 2.8 %collective-permute-start.18 = (bf16[8,2,4,32,128]{4,3,2,1,0:T(8,128)(2,1)S(1)}, bf16[8,2,4,32,128]{4,3,2,1,0:T(8,128)(2,1)S(1)}, u32[]{:S(2)}, u32[]{:S(2)}) collective-permute-start(bf16[8,2,4,32,128]{4,3,2,1,0:T(8,128)(2,1)S(1)} %get-tuple-element.106), channel_id=1, source_target_pairs={{0,96},{32,64},{64,32},{96,0},{1,97},{33,65},{65,33},{97,1},{2,98}... | collective-permute-start | bytes 1572872 | tf_op jit(solution)/shard_map/ppermute | solution.py:41
  103.4 6.4 %shard_map.45 = (bf16[8,96,512]{2,1,0:T(8,128)(2,1)S(1)}, bf16[8,96,512]{2,1,0:T(8,128)(2,1)S(1)}, bf16[8,96,512]{2,1,0:T(8,128)(2,1)S(1)}, bf16[8,96,512]{2,1,0:T(8,128)(2,1)S(1)}, s32[1]{0:T(128)}) custom-call(s32[5]{0:T(128)S(1)} %stack.23.where, f32[8]{0:T(128)S(1)} %convert_multiply_fusion.factors, s32[1]{0:T(128)} %get-tuple-element.95.order, ...), custom_call_target="tpu_custom_call" | custom-call | flops 6442450944 | bytes 8388608 | tf_op jit(solution)/shard_map/pallas_call | solution.py:261
  109.8 7.6 %collective-permute-done.17.refs_2_ = bf16[8,2,4,32,128]{4,3,2,1,0:T(8,128)(2,1)S(1)} collective-permute-done((bf16[8,2,4,32,128]{4,3,2,1,0:T(8,128)(2,1)S(1)}, bf16[8,2,4,32,128]{4,3,2,1,0:T(8,128)(2,1)S(1)}, u32[]{:S(2)}, u32[]{:S(2)}) %collective-permute-start.17) | collective-permute-done | bytes 524320 | tf_op jit(solution)/shard_map/ppermute | solution.py:41
  117.3 9.7 %collective-permute-done.18.refs_3_ = bf16[8,2,4,32,128]{4,3,2,1,0:T(8,128)(2,1)S(1)} collective-permute-done((bf16[8,2,4,32,128]{4,3,2,1,0:T(8,128)(2,1)S(1)}, bf16[8,2,4,32,128]{4,3,2,1,0:T(8,128)(2,1)S(1)}, u32[]{:S(2)}, u32[]{:S(2)}) %collective-permute-start.18) | collective-permute-done | bytes 524320 | tf_op jit(solution)/shard_map/ppermute | solution.py:41
  130.4 1.9 collective-permute-start.21
  133.4 19.9 %collective-permute-done.20 = bf16[4,2,4,32,128]{4,3,2,1,0:T(8,128)(2,1)S(1)} collective-permute-done((bf16[4,2,4,32,128]{4,3,2,1,0:T(8,128)(2,1)S(1)}, bf16[4,2,4,32,128]{4,3,2,1,0:T(8,128)(2,1)S(1)}, u32[]{:S(2)}, u32[]{:S(2)}) %collective-permute-start.20) | collective-permute-done | bytes 262176 | tf_op jit(solution)/shard_map/ppermute | solution.py:41
  153.2 2.2 collective-permute-start.33
  155.4 4.7 %collective-permute-done.21 = bf16[4,2,4,32,128]{4,3,2,1,0:T(8,128)(2,1)S(1)} collective-permute-done((bf16[4,2,4,32,128]{4,3,2,1,0:T(8,128)(2,1)S(1)}, bf16[4,2,4,32,128]{4,3,2,1,0:T(8,128)(2,1)S(1)}, u32[]{:S(2)}, u32[]{:S(2)}) %collective-permute-start.21) | collective-permute-done | bytes 262176 | tf_op jit(solution)/shard_map/ppermute | solution.py:41
  160.1 1.9 collective-permute-start.34
  162.1 2.3 collective-permute-start.35
  164.8 2.2 collective-permute-start.42
  167.0 5.7 %shard_map.47 = (bf16[4,128,512]{2,1,0:T(8,128)(2,1)S(1)}, bf16[4,128,512]{2,1,0:T(8,128)(2,1)S(1)}, bf16[4,128,512]{2,1,0:T(8,128)(2,1)S(1)}, bf16[4,128,512]{2,1,0:T(8,128)(2,1)S(1)}, s32[1]{0:T(128)}) custom-call(s32[5]{0:T(128)S(1)} %stack.23.where, f32[8]{0:T(128)S(1)} %convert_multiply_fusion.factors, s32[1]{0:T(128)} %get-tuple-element.107.order, ...), custom_call_target="tpu_custom_call" | custom-call | flops 4294967296 | bytes 8388608 | tf_op jit(solution)/shard_map/pallas_call | solution.py:261
  172.9 16.7 %collective-permute-done.34 = bf16[8,96,512]{2,1,0:T(8,128)(2,1)S(1)} collective-permute-done((bf16[8,96,512]{2,1,0:T(8,128)(2,1)S(1)}, bf16[8,96,512]{2,1,0:T(8,128)(2,1)S(1)}, u32[]{:S(2)}, u32[]{:S(2)}) %collective-permute-start.34) | collective-permute-done | bytes 786464 | tf_op jit(solution)/shard_map/ppermute | solution.py:41
  189.6 9.7 %collective-permute-done.35 = bf16[8,96,512]{2,1,0:T(8,128)(2,1)S(1)} collective-permute-done((bf16[8,96,512]{2,1,0:T(8,128)(2,1)S(1)}, bf16[8,96,512]{2,1,0:T(8,128)(2,1)S(1)}, u32[]{:S(2)}, u32[]{:S(2)}) %collective-permute-start.35) | collective-permute-done | bytes 786464 | tf_op jit(solution)/shard_map/ppermute | solution.py:41
  201.0 4.8 %collective-permute-done.25 = bf16[4,128,512]{2,1,0:T(8,128)(2,1)S(1)} collective-permute-done((bf16[4,128,512]{2,1,0:T(8,128)(2,1)S(1)}, bf16[4,128,512]{2,1,0:T(8,128)(2,1)S(1)}, u32[]{:S(2)}, u32[]{:S(2)}) %collective-permute-start.25) | collective-permute-done | bytes 524320 | tf_op jit(solution)/shard_map/ppermute | solution.py:41
  205.8 2.6 %collective-permute-start.37 = (bf16[2,96,512]{2,1,0:T(8,128)(2,1)S(1)}, bf16[2,96,512]{2,1,0:T(8,128)(2,1)S(1)}, u32[]{:S(2)}, u32[]{:S(2)}) collective-permute-start(bf16[2,96,512]{2,1,0:T(8,128)(2,1)S(1)} %get-tuple-element.131), channel_id=1, source_target_pairs={{0,64},{32,96},{64,0},{96,32},{1,65},{33,97},{65,1},{97,33},{2,66}... | collective-permute-start | bytes 589832 | tf_op jit(solution)/shard_map/ppermute | solution.py:41
  208.3 8.6 %collective-permute-done.26 = bf16[4,128,512]{2,1,0:T(8,128)(2,1)S(1)} collective-permute-done((bf16[4,128,512]{2,1,0:T(8,128)(2,1)S(1)}, bf16[4,128,512]{2,1,0:T(8,128)(2,1)S(1)}, u32[]{:S(2)}, u32[]{:S(2)}) %collective-permute-start.26) | collective-permute-done | bytes 524320 | tf_op jit(solution)/shard_map/ppermute | solution.py:41
  216.9 2.4 collective-permute-start.38
  220.1 2.1 collective-permute-start.27
  223.3 1.8 collective-permute-start.28
  225.1 2.0 collective-permute-start.44
  227.1 2.6 %collective-permute-start.45 = (bf16[192,512]{1,0:T(8,128)(2,1)S(1)}, bf16[192,512]{1,0:T(8,128)(2,1)S(1)}, u32[]{:S(2)}, u32[]{:S(2)}) collective-permute-start(bf16[192,512]{1,0:T(8,128)(2,1)S(1)} %get-tuple-element.142), channel_id=1, source_target_pairs={{0,24},{8,16},{16,8},{24,0},{1,25},{9,17},{17,9},{25,1},{2,26},{10... | collective-permute-start | bytes 589832 | tf_op jit(solution)/shard_map/ppermute | solution.py:41
  231.9 2.8 %collective-permute-done.29.refs_3_ = bf16[4,32,512]{2,1,0:T(8,128)(2,1)S(1)} collective-permute-done((bf16[4,32,512]{2,1,0:T(8,128)(2,1)S(1)}, bf16[4,32,512]{2,1,0:T(8,128)(2,1)S(1)}, u32[]{:S(2)}, u32[]{:S(2)}) %collective-permute-start.29) | collective-permute-done | bytes 131104 | tf_op jit(solution)/shard_map/ppermute | solution.py:41
  235.5 2.1 collective-permute-start.31
  237.7 2.4 collective-permute-start.32
  241.2 1.6 collective-permute-done.32.refs_3_
  (74 shorter events, 24.4 us)
Async XLA Ops:
  4.4 5.5 %copy-start.1 = (bf16[4,8192,128]{2,1,0:T(8,128)(2,1)S(1)}, bf16[4,8192,128]{2,1,0:T(8,128)(2,1)}, u32[]{:S(2)}) copy-start(bf16[4,8192,128]{2,1,0:T(8,128)(2,1)} %param.3) | copy-start | bytes 25165828
  4.4 5.5 %copy-start.3 = (bf16[2,128,512]{2,1,0:T(8,128)(2,1)S(1)}, bf16[2,128,512]{2,1,0:T(8,128)(2,1)}, u32[]{:S(2)}) copy-start(bf16[2,128,512]{2,1,0:T(8,128)(2,1)} %act.5) | copy-start | bytes 786436
  6.3 18.4 %collective-permute-start = (bf16[7,2,192,128]{3,2,1,0:T(8,128)(2,1)S(1)}, bf16[7,2,192,128]{3,2,1,0:T(8,128)(2,1)S(1)}, u32[]{:S(2)}, u32[]{:S(2)}) collective-permute-start(bf16[7,2,192,128]{3,2,1,0:T(8,128)(2,1)S(1)} %get-tuple-element.78), channel_id=1, source_target_pairs={{0,2},{2,0},{4,6},{6,4},{1,3},{3,1},{5,7},{7,5},{8,10},{10,8},{12,... | collective-permute-start | bytes 2064392 | tf_op jit(solution)/shard_map/ppermute | solution.py:41
  6.8 32.7 %collective-permute-start.1 = (bf16[7,2,192,128]{3,2,1,0:T(8,128)(2,1)S(1)}, bf16[7,2,192,128]{3,2,1,0:T(8,128)(2,1)S(1)}, u32[]{:S(2)}, u32[]{:S(2)}) collective-permute-start(bf16[7,2,192,128]{3,2,1,0:T(8,128)(2,1)S(1)} %get-tuple-element.79), channel_id=1, source_target_pairs={{0,4},{2,6},{4,0},{6,2},{1,5},{3,7},{5,1},{7,3},{8,12},{10,14},{12... | collective-permute-start | bytes 2064392 | tf_op jit(solution)/shard_map/ppermute | solution.py:41
  9.5 31.4 %collective-permute-start.2 = (bf16[7,2,192,128]{3,2,1,0:T(8,128)(2,1)S(1)}, bf16[7,2,192,128]{3,2,1,0:T(8,128)(2,1)S(1)}, u32[]{:S(2)}, u32[]{:S(2)}) collective-permute-start(bf16[7,2,192,128]{3,2,1,0:T(8,128)(2,1)S(1)} %get-tuple-element.80), channel_id=1, source_target_pairs={{0,6},{2,4},{4,2},{6,0},{1,7},{3,5},{5,3},{7,1},{8,14},{10,12},{12... | collective-permute-start | bytes 2064392 | tf_op jit(solution)/shard_map/ppermute | solution.py:41
  11.8 33.6 %collective-permute-start.3 = (bf16[7,4,96,128]{3,2,1,0:T(8,128)(2,1)S(1)}, bf16[7,4,96,128]{3,2,1,0:T(8,128)(2,1)S(1)}, u32[]{:S(2)}, u32[]{:S(2)}) collective-permute-start(bf16[7,4,96,128]{3,2,1,0:T(8,128)(2,1)S(1)} %get-tuple-element.84), channel_id=1, source_target_pairs={{0,16},{8,24},{16,0},{24,8},{1,17},{9,25},{17,1},{25,9},{2,18},{10... | collective-permute-start | bytes 2064392 | tf_op jit(solution)/shard_map/ppermute | solution.py:41
  13.8 32.7 %collective-permute-start.4 = (bf16[7,4,96,128]{3,2,1,0:T(8,128)(2,1)S(1)}, bf16[7,4,96,128]{3,2,1,0:T(8,128)(2,1)S(1)}, u32[]{:S(2)}, u32[]{:S(2)}) collective-permute-start(bf16[7,4,96,128]{3,2,1,0:T(8,128)(2,1)S(1)} %get-tuple-element.85), channel_id=1, source_target_pairs={{0,8},{8,0},{16,24},{24,16},{1,9},{9,1},{17,25},{25,17},{2,10},{10... | collective-permute-start | bytes 2064392 | tf_op jit(solution)/shard_map/ppermute | solution.py:41
  24.7 32.2 %collective-permute-start.5 = (bf16[7,4,96,128]{3,2,1,0:T(8,128)(2,1)S(1)}, bf16[7,4,96,128]{3,2,1,0:T(8,128)(2,1)S(1)}, u32[]{:S(2)}, u32[]{:S(2)}) collective-permute-start(bf16[7,4,96,128]{3,2,1,0:T(8,128)(2,1)S(1)} %get-tuple-element.86), channel_id=1, source_target_pairs={{0,24},{8,16},{16,8},{24,0},{1,25},{9,17},{17,9},{25,1},{2,26},{10... | collective-permute-start | bytes 2064392 | tf_op jit(solution)/shard_map/ppermute | solution.py:41
  41.7 41.1 %collective-permute-start.10 = (bf16[4,3,2,192,128]{4,3,2,1,0:T(8,128)(2,1)S(1)}, bf16[4,3,2,192,128]{4,3,2,1,0:T(8,128)(2,1)S(1)}, u32[]{:S(2)}, u32[]{:S(2)}) collective-permute-start(bf16[4,3,2,192,128]{4,3,2,1,0:T(8,128)(2,1)S(1)} %get-tuple-element.93), channel_id=1, source_target_pairs={{0,1},{1,0},{2,3},{3,2},{4,5},{5,4},{6,7},{7,6},{8,9},{9,8},{10,11... | collective-permute-start | bytes 3538952 | tf_op jit(solution)/shard_map/ppermute | solution.py:41
  41.8 19.6 %collective-permute-start.6 = (bf16[4,2,192,128]{3,2,1,0:T(8,128)(2,1)S(1)}, bf16[4,2,192,128]{3,2,1,0:T(8,128)(2,1)S(1)}, u32[]{:S(2)}, u32[]{:S(2)}) collective-permute-start(bf16[4,2,192,128]{3,2,1,0:T(8,128)(2,1)S(1)} %get-tuple-element.89), channel_id=1, source_target_pairs={{0,1},{1,0},{2,3},{3,2},{4,5},{5,4},{6,7},{7,6},{8,9},{9,8},{10,11... | collective-permute-start | bytes 1179656 | tf_op jit(solution)/shard_map/ppermute | solution.py:41
  58.4 45.0 %collective-permute-start.15 = (bf16[4,3,4,96,128]{4,3,2,1,0:T(8,128)(2,1)S(1)}, bf16[4,3,4,96,128]{4,3,2,1,0:T(8,128)(2,1)S(1)}, u32[]{:S(2)}, u32[]{:S(2)}) collective-permute-start(bf16[4,3,4,96,128]{4,3,2,1,0:T(8,128)(2,1)S(1)} %get-tuple-element.100), channel_id=1, source_target_pairs={{0,1},{1,0},{2,3},{3,2},{4,5},{5,4},{6,7},{7,6},{8,9},{9,8},{10,11... | collective-permute-start | bytes 3538952 | tf_op jit(solution)/shard_map/ppermute | solution.py:41
  58.5 10.9 %collective-permute-start.7 = (bf16[4,2,192,128]{3,2,1,0:T(8,128)(2,1)S(1)}, bf16[4,2,192,128]{3,2,1,0:T(8,128)(2,1)S(1)}, u32[]{:S(2)}, u32[]{:S(2)}) collective-permute-start(bf16[4,2,192,128]{3,2,1,0:T(8,128)(2,1)S(1)} %get-tuple-element.90), channel_id=1, source_target_pairs={{0,3},{1,2},{2,1},{3,0},{4,7},{5,6},{6,5},{7,4},{8,11},{9,10},{10,... | collective-permute-start | bytes 1179656 | tf_op jit(solution)/shard_map/ppermute | solution.py:41
  59.1 19.9 %collective-permute-start.8 = (bf16[4,2,192,128]{3,2,1,0:T(8,128)(2,1)S(1)}, bf16[4,2,192,128]{3,2,1,0:T(8,128)(2,1)S(1)}, u32[]{:S(2)}, u32[]{:S(2)}) collective-permute-start(bf16[4,2,192,128]{3,2,1,0:T(8,128)(2,1)S(1)} %get-tuple-element.91), channel_id=1, source_target_pairs={{0,5},{1,4},{2,7},{3,6},{4,1},{5,0},{6,3},{7,2},{8,13},{9,12},{10,... | collective-permute-start | bytes 1179656 | tf_op jit(solution)/shard_map/ppermute | solution.py:41
  61.3 19.2 %collective-permute-start.9 = (bf16[4,2,192,128]{3,2,1,0:T(8,128)(2,1)S(1)}, bf16[4,2,192,128]{3,2,1,0:T(8,128)(2,1)S(1)}, u32[]{:S(2)}, u32[]{:S(2)}) collective-permute-start(bf16[4,2,192,128]{3,2,1,0:T(8,128)(2,1)S(1)} %get-tuple-element.92), channel_id=1, source_target_pairs={{0,7},{1,6},{2,5},{3,4},{4,3},{5,2},{6,1},{7,0},{8,15},{9,14},{10,... | collective-permute-start | bytes 1179656 | tf_op jit(solution)/shard_map/ppermute | solution.py:41
  69.4 20.4 %collective-permute-start.11 = (bf16[4,4,96,128]{3,2,1,0:T(8,128)(2,1)S(1)}, bf16[4,4,96,128]{3,2,1,0:T(8,128)(2,1)S(1)}, u32[]{:S(2)}, u32[]{:S(2)}) collective-permute-start(bf16[4,4,96,128]{3,2,1,0:T(8,128)(2,1)S(1)} %get-tuple-element.96), channel_id=1, source_target_pairs={{0,1},{1,0},{2,3},{3,2},{4,5},{5,4},{6,7},{7,6},{8,9},{9,8},{10,11... | collective-permute-start | bytes 1179656 | tf_op jit(solution)/shard_map/ppermute | solution.py:41
  78.9 12.4 %collective-permute-start.12 = (bf16[4,4,96,128]{3,2,1,0:T(8,128)(2,1)S(1)}, bf16[4,4,96,128]{3,2,1,0:T(8,128)(2,1)S(1)}, u32[]{:S(2)}, u32[]{:S(2)}) collective-permute-start(bf16[4,4,96,128]{3,2,1,0:T(8,128)(2,1)S(1)} %get-tuple-element.97), channel_id=1, source_target_pairs={{0,17},{1,16},{8,25},{9,24},{16,1},{17,0},{24,9},{25,8},{2,19},{3,... | collective-permute-start | bytes 1179656 | tf_op jit(solution)/shard_map/ppermute | solution.py:41
  80.6 19.9 %collective-permute-start.13 = (bf16[4,4,96,128]{3,2,1,0:T(8,128)(2,1)S(1)}, bf16[4,4,96,128]{3,2,1,0:T(8,128)(2,1)S(1)}, u32[]{:S(2)}, u32[]{:S(2)}) collective-permute-start(bf16[4,4,96,128]{3,2,1,0:T(8,128)(2,1)S(1)} %get-tuple-element.98), channel_id=1, source_target_pairs={{0,9},{1,8},{8,1},{9,0},{16,25},{17,24},{24,17},{25,16},{2,11},{3,... | collective-permute-start | bytes 1179656 | tf_op jit(solution)/shard_map/ppermute | solution.py:41
  82.8 20.6 %collective-permute-start.14 = (bf16[4,4,96,128]{3,2,1,0:T(8,128)(2,1)S(1)}, bf16[4,4,96,128]{3,2,1,0:T(8,128)(2,1)S(1)}, u32[]{:S(2)}, u32[]{:S(2)}) collective-permute-start(bf16[4,4,96,128]{3,2,1,0:T(8,128)(2,1)S(1)} %get-tuple-element.99), channel_id=1, source_target_pairs={{0,25},{1,24},{8,17},{9,16},{16,9},{17,8},{24,1},{25,0},{2,27},{3,... | collective-permute-start | bytes 1179656 | tf_op jit(solution)/shard_map/ppermute | solution.py:41
  89.8 20.0 %collective-permute-start.16 = (bf16[8,2,4,32,128]{4,3,2,1,0:T(8,128)(2,1)S(1)}, bf16[8,2,4,32,128]{4,3,2,1,0:T(8,128)(2,1)S(1)}, u32[]{:S(2)}, u32[]{:S(2)}) collective-permute-start(bf16[8,2,4,32,128]{4,3,2,1,0:T(8,128)(2,1)S(1)} %get-tuple-element.104), channel_id=1, source_target_pairs={{0,32},{32,0},{64,96},{96,64},{1,33},{33,1},{65,97},{97,65},{2,34}... | collective-permute-start | bytes 1572872 | tf_op jit(solution)/shard_map/ppermute | solution.py:41
  91.4 26.0 %collective-permute-start.17 = (bf16[8,2,4,32,128]{4,3,2,1,0:T(8,128)(2,1)S(1)}, bf16[8,2,4,32,128]{4,3,2,1,0:T(8,128)(2,1)S(1)}, u32[]{:S(2)}, u32[]{:S(2)}) collective-permute-start(bf16[8,2,4,32,128]{4,3,2,1,0:T(8,128)(2,1)S(1)} %get-tuple-element.105), channel_id=1, source_target_pairs={{0,64},{32,96},{64,0},{96,32},{1,65},{33,97},{65,1},{97,33},{2,66}... | collective-permute-start | bytes 1572872 | tf_op jit(solution)/shard_map/ppermute | solution.py:41
  100.5 26.6 %collective-permute-start.18 = (bf16[8,2,4,32,128]{4,3,2,1,0:T(8,128)(2,1)S(1)}, bf16[8,2,4,32,128]{4,3,2,1,0:T(8,128)(2,1)S(1)}, u32[]{:S(2)}, u32[]{:S(2)}) collective-permute-start(bf16[8,2,4,32,128]{4,3,2,1,0:T(8,128)(2,1)S(1)} %get-tuple-element.106), channel_id=1, source_target_pairs={{0,96},{32,64},{64,32},{96,0},{1,97},{33,65},{65,33},{97,1},{2,98}... | collective-permute-start | bytes 1572872 | tf_op jit(solution)/shard_map/ppermute | solution.py:41
  128.3 36.5 %collective-permute-start.23 = (bf16[4,4,2,4,32,128]{5,4,3,2,1,0:T(8,128)(2,1)S(1)}, bf16[4,4,2,4,32,128]{5,4,3,2,1,0:T(8,128)(2,1)S(1)}, u32[]{:S(2)}, u32[]{:S(2)}) collective-permute-start(bf16[4,4,2,4,32,128]{5,4,3,2,1,0:T(8,128)(2,1)S(1)} %get-tuple-element.112), channel_id=1, source_target_pairs={{0,1},{1,0},{2,3},{3,2},{4,5},{5,4},{6,7},{7,6},{8,9},{9,8},{10,11... | collective-permute-start | bytes 3145736 | tf_op jit(solution)/shard_map/ppermute | solution.py:41
  128.4 3.8 %collective-permute-start.19 = (bf16[4,2,4,32,128]{4,3,2,1,0:T(8,128)(2,1)S(1)}, bf16[4,2,4,32,128]{4,3,2,1,0:T(8,128)(2,1)S(1)}, u32[]{:S(2)}, u32[]{:S(2)}) collective-permute-start(bf16[4,2,4,32,128]{4,3,2,1,0:T(8,128)(2,1)S(1)} %get-tuple-element.108), channel_id=1, source_target_pairs={{0,1},{1,0},{2,3},{3,2},{4,5},{5,4},{6,7},{7,6},{8,9},{9,8},{10,11... | collective-permute-start | bytes 786440 | tf_op jit(solution)/shard_map/ppermute | solution.py:41
  128.9 35.4 %collective-permute-start.40 = (bf16[2,384,512]{2,1,0:T(8,128)(2,1)S(1)}, bf16[2,384,512]{2,1,0:T(8,128)(2,1)S(1)}, u32[]{:S(2)}, u32[]{:S(2)}) collective-permute-start(bf16[2,384,512]{2,1,0:T(8,128)(2,1)S(1)} %get-tuple-element.136), channel_id=1, source_target_pairs={{0,32},{32,0},{64,96},{96,64},{1,33},{33,1},{65,97},{97,65},{2,34}... | collective-permute-start | bytes 2359304 | tf_op jit(solution)/shard_map/ppermute | solution.py:41
  129.2 24.0 %collective-permute-start.20 = (bf16[4,2,4,32,128]{4,3,2,1,0:T(8,128)(2,1)S(1)}, bf16[4,2,4,32,128]{4,3,2,1,0:T(8,128)(2,1)S(1)}, u32[]{:S(2)}, u32[]{:S(2)}) collective-permute-start(bf16[4,2,4,32,128]{4,3,2,1,0:T(8,128)(2,1)S(1)} %get-tuple-element.109), channel_id=1, source_target_pairs={{0,33},{1,32},{32,1},{33,0},{64,97},{65,96},{96,65},{97,64},{2,35}... | collective-permute-start | bytes 786440 | tf_op jit(solution)/shard_map/ppermute | solution.py:41
  130.4 29.8 %collective-permute-start.21 = (bf16[4,2,4,32,128]{4,3,2,1,0:T(8,128)(2,1)S(1)}, bf16[4,2,4,32,128]{4,3,2,1,0:T(8,128)(2,1)S(1)}, u32[]{:S(2)}, u32[]{:S(2)}) collective-permute-start(bf16[4,2,4,32,128]{4,3,2,1,0:T(8,128)(2,1)S(1)} %get-tuple-element.110), channel_id=1, source_target_pairs={{0,65},{1,64},{32,97},{33,96},{64,1},{65,0},{96,33},{97,32},{2,67}... | collective-permute-start | bytes 786440 | tf_op jit(solution)/shard_map/ppermute | solution.py:41
  132.3 29.8 %collective-permute-start.22 = (bf16[4,2,4,32,128]{4,3,2,1,0:T(8,128)(2,1)S(1)}, bf16[4,2,4,32,128]{4,3,2,1,0:T(8,128)(2,1)S(1)}, u32[]{:S(2)}, u32[]{:S(2)}) collective-permute-start(bf16[4,2,4,32,128]{4,3,2,1,0:T(8,128)(2,1)S(1)} %get-tuple-element.111), channel_id=1, source_target_pairs={{0,97},{1,96},{32,65},{33,64},{64,33},{65,32},{96,1},{97,0},{2,99}... | collective-permute-start | bytes 786440 | tf_op jit(solution)/shard_map/ppermute | solution.py:41
  153.2 19.7 %collective-permute-start.33 = (bf16[8,96,512]{2,1,0:T(8,128)(2,1)S(1)}, bf16[8,96,512]{2,1,0:T(8,128)(2,1)S(1)}, u32[]{:S(2)}, u32[]{:S(2)}) collective-permute-start(bf16[8,96,512]{2,1,0:T(8,128)(2,1)S(1)} %get-tuple-element.126), channel_id=1, source_target_pairs={{0,2},{2,0},{4,6},{6,4},{1,3},{3,1},{5,7},{7,5},{8,10},{10,8},{12,... | collective-permute-start | bytes 2359304 | tf_op jit(solution)/shard_map/ppermute | solution.py:41
  160.1 29.5 %collective-permute-start.34 = (bf16[8,96,512]{2,1,0:T(8,128)(2,1)S(1)}, bf16[8,96,512]{2,1,0:T(8,128)(2,1)S(1)}, u32[]{:S(2)}, u32[]{:S(2)}) collective-permute-start(bf16[8,96,512]{2,1,0:T(8,128)(2,1)S(1)} %get-tuple-element.127), channel_id=1, source_target_pairs={{0,4},{2,6},{4,0},{6,2},{1,5},{3,7},{5,1},{7,3},{8,12},{10,14},{12... | collective-permute-start | bytes 2359304 | tf_op jit(solution)/shard_map/ppermute | solution.py:41
  162.1 37.3 %collective-permute-start.35 = (bf16[8,96,512]{2,1,0:T(8,128)(2,1)S(1)}, bf16[8,96,512]{2,1,0:T(8,128)(2,1)S(1)}, u32[]{:S(2)}, u32[]{:S(2)}) collective-permute-start(bf16[8,96,512]{2,1,0:T(8,128)(2,1)S(1)} %get-tuple-element.128), channel_id=1, source_target_pairs={{0,6},{2,4},{4,2},{6,0},{1,7},{3,5},{5,3},{7,1},{8,14},{10,12},{12... | collective-permute-start | bytes 2359304 | tf_op jit(solution)/shard_map/ppermute | solution.py:41
  164.4 55.8 %collective-permute-start.41 = (bf16[2,384,512]{2,1,0:T(8,128)(2,1)S(1)}, bf16[2,384,512]{2,1,0:T(8,128)(2,1)S(1)}, u32[]{:S(2)}, u32[]{:S(2)}) collective-permute-start(bf16[2,384,512]{2,1,0:T(8,128)(2,1)S(1)} %get-tuple-element.137), channel_id=1, source_target_pairs={{0,64},{32,96},{64,0},{96,32},{1,65},{33,97},{65,1},{97,33},{2,66}... | collective-permute-start | bytes 2359304 | tf_op jit(solution)/shard_map/ppermute | solution.py:41
  164.8 57.5 %collective-permute-start.42 = (bf16[2,384,512]{2,1,0:T(8,128)(2,1)S(1)}, bf16[2,384,512]{2,1,0:T(8,128)(2,1)S(1)}, u32[]{:S(2)}, u32[]{:S(2)}) collective-permute-start(bf16[2,384,512]{2,1,0:T(8,128)(2,1)S(1)} %get-tuple-element.138), channel_id=1, source_target_pairs={{0,96},{32,64},{64,32},{96,0},{1,97},{33,65},{65,33},{97,1},{2,98}... | collective-permute-start | bytes 2359304 | tf_op jit(solution)/shard_map/ppermute | solution.py:41
  172.9 28.0 %collective-permute-start.24 = (bf16[4,128,512]{2,1,0:T(8,128)(2,1)S(1)}, bf16[4,128,512]{2,1,0:T(8,128)(2,1)S(1)}, u32[]{:S(2)}, u32[]{:S(2)}) collective-permute-start(bf16[4,128,512]{2,1,0:T(8,128)(2,1)S(1)} %get-tuple-element.114), channel_id=1, source_target_pairs={{0,16},{8,24},{16,0},{24,8},{1,17},{9,25},{17,1},{25,9},{2,18},{10... | collective-permute-start | bytes 1572872 | tf_op jit(solution)/shard_map/ppermute | solution.py:41
  189.6 16.2 %collective-permute-start.25 = (bf16[4,128,512]{2,1,0:T(8,128)(2,1)S(1)}, bf16[4,128,512]{2,1,0:T(8,128)(2,1)S(1)}, u32[]{:S(2)}, u32[]{:S(2)}) collective-permute-start(bf16[4,128,512]{2,1,0:T(8,128)(2,1)S(1)} %get-tuple-element.115), channel_id=1, source_target_pairs={{0,8},{8,0},{16,24},{24,16},{1,9},{9,1},{17,25},{25,17},{2,10},{10... | collective-permute-start | bytes 1572872 | tf_op jit(solution)/shard_map/ppermute | solution.py:41
  199.3 17.6 %collective-permute-start.26 = (bf16[4,128,512]{2,1,0:T(8,128)(2,1)S(1)}, bf16[4,128,512]{2,1,0:T(8,128)(2,1)S(1)}, u32[]{:S(2)}, u32[]{:S(2)}) collective-permute-start(bf16[4,128,512]{2,1,0:T(8,128)(2,1)S(1)} %get-tuple-element.116), channel_id=1, source_target_pairs={{0,24},{8,16},{16,8},{24,0},{1,25},{9,17},{17,9},{25,1},{2,26},{10... | collective-permute-start | bytes 1572872 | tf_op jit(solution)/shard_map/ppermute | solution.py:41
  200.9 22.4 %collective-permute-start.36 = (bf16[2,96,512]{2,1,0:T(8,128)(2,1)S(1)}, bf16[2,96,512]{2,1,0:T(8,128)(2,1)S(1)}, u32[]{:S(2)}, u32[]{:S(2)}) collective-permute-start(bf16[2,96,512]{2,1,0:T(8,128)(2,1)S(1)} %get-tuple-element.130), channel_id=1, source_target_pairs={{0,32},{32,0},{64,96},{96,64},{1,33},{33,1},{65,97},{97,65},{2,34}... | collective-permute-start | bytes 589832 | tf_op jit(solution)/shard_map/ppermute | solution.py:41
  205.8 19.3 %collective-permute-start.37 = (bf16[2,96,512]{2,1,0:T(8,128)(2,1)S(1)}, bf16[2,96,512]{2,1,0:T(8,128)(2,1)S(1)}, u32[]{:S(2)}, u32[]{:S(2)}) collective-permute-start(bf16[2,96,512]{2,1,0:T(8,128)(2,1)S(1)} %get-tuple-element.131), channel_id=1, source_target_pairs={{0,64},{32,96},{64,0},{96,32},{1,65},{33,97},{65,1},{97,33},{2,66}... | collective-permute-start | bytes 589832 | tf_op jit(solution)/shard_map/ppermute | solution.py:41
  216.9 10.2 %collective-permute-start.38 = (bf16[2,96,512]{2,1,0:T(8,128)(2,1)S(1)}, bf16[2,96,512]{2,1,0:T(8,128)(2,1)S(1)}, u32[]{:S(2)}, u32[]{:S(2)}) collective-permute-start(bf16[2,96,512]{2,1,0:T(8,128)(2,1)S(1)} %get-tuple-element.132), channel_id=1, source_target_pairs={{0,96},{32,64},{64,32},{96,0},{1,97},{33,65},{65,33},{97,1},{2,98}... | collective-permute-start | bytes 589832 | tf_op jit(solution)/shard_map/ppermute | solution.py:41
  220.1 9.6 %collective-permute-start.27 = (bf16[4,32,512]{2,1,0:T(8,128)(2,1)S(1)}, bf16[4,32,512]{2,1,0:T(8,128)(2,1)S(1)}, u32[]{:S(2)}, u32[]{:S(2)}) collective-permute-start(bf16[4,32,512]{2,1,0:T(8,128)(2,1)S(1)} %get-tuple-element.118), channel_id=1, source_target_pairs={{0,2},{2,0},{4,6},{6,4},{1,3},{3,1},{5,7},{7,5},{8,10},{10,8},{12,... | collective-permute-start | bytes 393224 | tf_op jit(solution)/shard_map/ppermute | solution.py:41
  223.2 12.3 %collective-permute-start.43 = (bf16[192,512]{1,0:T(8,128)(2,1)S(1)}, bf16[192,512]{1,0:T(8,128)(2,1)S(1)}, u32[]{:S(2)}, u32[]{:S(2)}) collective-permute-start(bf16[192,512]{1,0:T(8,128)(2,1)S(1)} %get-tuple-element.140), channel_id=1, source_target_pairs={{0,16},{8,24},{16,0},{24,8},{1,17},{9,25},{17,1},{25,9},{2,18},{10... | collective-permute-start | bytes 589832 | tf_op jit(solution)/shard_map/ppermute | solution.py:41
  223.3 7.7 %collective-permute-start.28 = (bf16[4,32,512]{2,1,0:T(8,128)(2,1)S(1)}, bf16[4,32,512]{2,1,0:T(8,128)(2,1)S(1)}, u32[]{:S(2)}, u32[]{:S(2)}) collective-permute-start(bf16[4,32,512]{2,1,0:T(8,128)(2,1)S(1)} %get-tuple-element.119), channel_id=1, source_target_pairs={{0,4},{2,6},{4,0},{6,2},{1,5},{3,7},{5,1},{7,3},{8,12},{10,14},{12... | collective-permute-start | bytes 393224 | tf_op jit(solution)/shard_map/ppermute | solution.py:41
  225.1 12.5 %collective-permute-start.44 = (bf16[192,512]{1,0:T(8,128)(2,1)S(1)}, bf16[192,512]{1,0:T(8,128)(2,1)S(1)}, u32[]{:S(2)}, u32[]{:S(2)}) collective-permute-start(bf16[192,512]{1,0:T(8,128)(2,1)S(1)} %get-tuple-element.141), channel_id=1, source_target_pairs={{0,8},{8,0},{16,24},{24,16},{1,9},{9,1},{17,25},{25,17},{2,10},{10... | collective-permute-start | bytes 589832 | tf_op jit(solution)/shard_map/ppermute | solution.py:41
  227.1 13.0 %collective-permute-start.45 = (bf16[192,512]{1,0:T(8,128)(2,1)S(1)}, bf16[192,512]{1,0:T(8,128)(2,1)S(1)}, u32[]{:S(2)}, u32[]{:S(2)}) collective-permute-start(bf16[192,512]{1,0:T(8,128)(2,1)S(1)} %get-tuple-element.142), channel_id=1, source_target_pairs={{0,24},{8,16},{16,8},{24,0},{1,25},{9,17},{17,9},{25,1},{2,26},{10... | collective-permute-start | bytes 589832 | tf_op jit(solution)/shard_map/ppermute | solution.py:41
  229.7 5.0 %collective-permute-start.29 = (bf16[4,32,512]{2,1,0:T(8,128)(2,1)S(1)}, bf16[4,32,512]{2,1,0:T(8,128)(2,1)S(1)}, u32[]{:S(2)}, u32[]{:S(2)}) collective-permute-start(bf16[4,32,512]{2,1,0:T(8,128)(2,1)S(1)} %get-tuple-element.120), channel_id=1, source_target_pairs={{0,6},{2,4},{4,2},{6,0},{1,7},{3,5},{5,3},{7,1},{8,14},{10,12},{12... | collective-permute-start | bytes 393224 | tf_op jit(solution)/shard_map/ppermute | solution.py:41
  231.0 10.1 %collective-permute-start.39 = (bf16[96,512]{1,0:T(8,128)(2,1)S(1)}, bf16[96,512]{1,0:T(8,128)(2,1)S(1)}, u32[]{:S(2)}, u32[]{:S(2)}) collective-permute-start(bf16[96,512]{1,0:T(8,128)(2,1)S(1)} %get-tuple-element.134), channel_id=1, source_target_pairs={{0,16},{8,24},{16,0},{24,8},{1,17},{9,25},{17,1},{25,9},{2,18},{10... | collective-permute-start | bytes 294920 | tf_op jit(solution)/shard_map/ppermute | solution.py:41
  235.3 5.8 %collective-permute-start.30 = (bf16[32,512]{1,0:T(8,128)(2,1)S(1)}, bf16[32,512]{1,0:T(8,128)(2,1)S(1)}, u32[]{:S(2)}, u32[]{:S(2)}) collective-permute-start(bf16[32,512]{1,0:T(8,128)(2,1)S(1)} %get-tuple-element.122), channel_id=1, source_target_pairs={{0,32},{32,0},{64,96},{96,64},{1,33},{33,1},{65,97},{97,65},{2,34}... | collective-permute-start | bytes 98312 | tf_op jit(solution)/shard_map/ppermute | solution.py:41
  235.5 5.6 %collective-permute-start.31 = (bf16[32,512]{1,0:T(8,128)(2,1)S(1)}, bf16[32,512]{1,0:T(8,128)(2,1)S(1)}, u32[]{:S(2)}, u32[]{:S(2)}) collective-permute-start(bf16[32,512]{1,0:T(8,128)(2,1)S(1)} %get-tuple-element.123), channel_id=1, source_target_pairs={{0,64},{32,96},{64,0},{96,32},{1,65},{33,97},{65,1},{97,33},{2,66}... | collective-permute-start | bytes 98312 | tf_op jit(solution)/shard_map/ppermute | solution.py:41
  237.7 5.1 %collective-permute-start.32 = (bf16[32,512]{1,0:T(8,128)(2,1)S(1)}, bf16[32,512]{1,0:T(8,128)(2,1)S(1)}, u32[]{:S(2)}, u32[]{:S(2)}) collective-permute-start(bf16[32,512]{1,0:T(8,128)(2,1)S(1)} %get-tuple-element.124), channel_id=1, source_target_pairs={{0,96},{32,64},{64,32},{96,0},{1,97},{33,65},{65,33},{97,1},{2,98}... | collective-permute-start | bytes 98312 | tf_op jit(solution)/shard_map/ppermute | solution.py:41
  (3 other events, 9.2 us)
